TPU v7x, 512 devices: a whole 4x4x16 slice. The times are simulated.
512 devices in a mesh: gx: 16 (over z_hi, y, core), gy: 32 (over z_lo, x).
Axes of the slice: x: 4, y: 4, z: 16 (z_hi: 2, z_lo: 8; z = z_hi * 8 + z_lo), core: 2. Of those that a mesh axis runs over, the one named last changes fastest.
Arguments:
- features: bfloat16 [16, 32, 128, 256], P('gx', 'gy'), may hold values from -6 to 6
- occupancy: int32 [16, 32, 128], P('gx', 'gy'), may hold values from 0 to 1, as said below
- coords: int32 [16, 32, 3, 128], P('gx', 'gy'), may hold values from 0 to 7, as said below
- norm_gains: float32 [2, 2, 256], replicated, may hold values from 0.1 to 1.9
- bias_tables: float32 [2, 3, 8, 15], replicated, may hold values from -4 to 4
- w_qkv: bfloat16 [2, 256, 768], replicated, may hold values from -0.375 to 0.375
- w_out: bfloat16 [2, 256, 256], replicated, may hold values from -0.375 to 0.375
- w_up: bfloat16 [2, 256, 1024], replicated, may hold values from -0.375 to 0.375
- w_down: bfloat16 [2, 1024, 256], replicated, may hold values from -0.1875 to 0.1875
- grad_out: bfloat16 [16, 32, 128, 256], P('gx', 'gy'), may hold values from -6 to 6
Outputs:
- out_points: bfloat16 [16, 32, 128, 256], P('gx', 'gy')
- grad_points: bfloat16 [16, 32, 128, 256], P('gx', 'gy')
- grad_tables: float32 [2, 3, 8, 15], replicated
Inputs may be any that keep to these rules, and one draw needn't show every extreme that they name: `occupancy`: 1 marks an occupied slot. In each quarter of 32 slots of a window the occupied slots come first, and every quarter holds at least one. `coords`: the x coordinate of a slot of quarter (a, b) lies in [a * 4, (a + 1) * 4) and its y coordinate in [b * 4, (b + 1) * 4); z lies in [0, 8).
All inputs are finite; a program needn't handle non-finite values.
Results may differ from a plain program's by a relative error of at most 0.02.
Values may be sent and summed in bfloat16 or wider, within the bound.
No kernel may reach another device: no remote copies, remote signals or barrier semaphores. Data moves between devices by JAX's collectives and lax.ppermute only.
A program may use at most 64 MiB of HBM per device.

v0:
```python
from functools import partial

import jax
import jax.numpy as jnp
from jax import lax
from jax.sharding import PartitionSpec as P

highest_precision = lax.Precision.HIGHEST
epsilon = 1e-05


def from_behind(value, axis, steps):
    count = lax.axis_size(axis)
    pairs = [(source, (source + steps) % count) for source in range(count)]
    return lax.ppermute(value, axis, pairs)


def layer_norm(values, gain):
    mean_value = jnp.mean(values, axis=-1, keepdims=True)
    centred = values - mean_value
    variance = jnp.mean(centred * centred, axis=-1, keepdims=True)
    return centred * lax.rsqrt(variance + epsilon) * gain


def relative_bias(coords, bias_table):
    table_span = bias_table.shape[-1]
    window_span = (table_span + 1) // 2
    cell_index = jnp.arange(window_span, dtype=jnp.int32)
    offsets = cell_index[:, None] - cell_index[None, :] + window_span - 1
    selection_matrix = (
        offsets[:, :, None] == jnp.arange(table_span, dtype=jnp.int32)[None, None, :]
    ).astype(jnp.float32)
    total = None
    for axis_index in range(3):
        indicator_matrix = (coords[axis_index][:, None] == cell_index[None, :]).astype(jnp.float32)
        banded_offset_matrix = jnp.einsum(
            "hr,abr->hab", bias_table[axis_index], selection_matrix, precision=highest_precision
        )
        left_factor = jnp.einsum(
            "dx,cxq->cdq", indicator_matrix, banded_offset_matrix, precision=highest_precision
        )
        axis_contribution_part = jnp.einsum(
            "klu,tu->klt", left_factor, indicator_matrix, precision=highest_precision
        )
        total = axis_contribution_part if total is None else total + axis_contribution_part
    return total


def attend(queries, keys_part, values_part, bias_table, occupied, coords):
    head_size = queries.shape[-1]
    scores = jnp.einsum("qhd,khd->hqk", queries, keys_part, preferred_element_type=jnp.float32)
    scores = scores * head_size ** (-0.5) + relative_bias(coords, bias_table)
    scores = jnp.where(occupied[None, None, :] > 0, scores, -1e30)
    weights_soft = jax.nn.softmax(scores, axis=-1).astype(jnp.bfloat16)
    mixed = jnp.einsum(
        "hqk,khd->qhd", weights_soft, values_part, preferred_element_type=jnp.float32
    )
    return mixed.reshape(mixed.shape[0], -1).astype(jnp.bfloat16)


def swin_block(
    hidden,
    bias_table,
    occupied,
    coords,
    gains,
    weight_qkv,
    weight_out,
    up_weight_matrix,
    weight_down,
):
    slots, width = hidden.shape
    heads = bias_table.shape[1]
    core = jax.checkpoint(partial(attend, occupied=occupied, coords=coords))
    normed = layer_norm(hidden.astype(jnp.float32), gains[0]).astype(jnp.bfloat16)
    projected = jnp.dot(normed, weight_qkv, preferred_element_type=jnp.float32).astype(jnp.bfloat16)
    qkv_parts = projected.reshape(slots, 3, heads, width // heads)
    mixed = core(qkv_parts[:, 0], qkv_parts[:, 1], qkv_parts[:, 2], bias_table)
    middle = hidden.astype(jnp.float32) + jnp.dot(
        mixed, weight_out, preferred_element_type=jnp.float32
    )
    normed_two = layer_norm(middle, gains[1]).astype(jnp.bfloat16)
    expanded = jax.nn.gelu(
        jnp.dot(normed_two, up_weight_matrix, preferred_element_type=jnp.float32)
    ).astype(jnp.bfloat16)
    return (middle + jnp.dot(expanded, weight_down, preferred_element_type=jnp.float32)).astype(
        jnp.bfloat16
    )


def run_block(
    occupied,
    coords,
    gains,
    weight_qkv,
    weight_out,
    up_weight_matrix,
    weight_down,
    hidden,
    bias_table,
):
    return swin_block(
        hidden,
        bias_table,
        occupied,
        coords,
        gains,
        weight_qkv,
        weight_out,
        up_weight_matrix,
        weight_down,
    )


def roll_half(array, position, step_sign, sender):
    lower_half = lax.index_in_dim(array, 0, position, keepdims=False)
    upper_half = lax.index_in_dim(array, 1, position, keepdims=False)
    if step_sign < 0:
        return jnp.stack([upper_half, sender(lower_half, step_sign)], axis=position)
    return jnp.stack([sender(upper_half, step_sign), lower_half], axis=position)


def send_values_y_first(piece, step_sign):
    return from_behind(piece, "gy", step_sign)


def send_values_x_second(piece, step_sign):
    return from_behind(piece, "gx", step_sign)


def send_meta_x(piece, step_sign):
    return from_behind(piece, "gx", step_sign)


def send_meta_y(piece, step_sign):
    return from_behind(piece, "gy", step_sign)


def roll_values(points, step_sign):
    slots, width = points.shape
    tiles = points.reshape(2, 2, slots // 4, width)
    tiles = roll_half(tiles, 1, step_sign, send_values_y_first)
    tiles = roll_half(tiles, 0, step_sign, send_values_x_second)
    return tiles.reshape(slots, width)


def on_device(
    features, occupancy, coords, norm_gains, bias_tables, w_qkv, w_out, w_up, w_down, grad_out
):
    points = features[0, 0]
    slots, width = points.shape
    quarter = slots // 4
    window_span = (bias_tables.shape[-1] + 1) // 2
    half_span = window_span // 2
    local_coords = coords[0, 0]
    slot_meta = jnp.concatenate([occupancy[0, 0][None], local_coords], axis=0).reshape(
        4, 2, 2, quarter
    )
    slot_meta = roll_half(slot_meta, 1, -1, send_meta_x)
    slot_meta = roll_half(slot_meta, 2, -1, send_meta_y)
    slot_meta = slot_meta.reshape(4, slots)
    shifted_coords = jnp.stack(
        [
            (slot_meta[1] + half_span) % window_span,
            (slot_meta[2] + half_span) % window_span,
            slot_meta[3],
        ],
        axis=0,
    )
    occupied = occupancy[0, 0].astype(jnp.float32)
    shifted_occupied = slot_meta[0].astype(jnp.float32)
    occupied_mask = occupancy[0, 0].astype(jnp.bfloat16)[:, None]
    first_out, pullback_first_block = jax.vjp(
        partial(
            run_block, occupied, local_coords, norm_gains[0], w_qkv[0], w_out[0], w_up[0], w_down[0]
        ),
        points,
        bias_tables[0],
    )
    rolled = roll_values(first_out, -1)
    second, pull_second = jax.vjp(
        partial(
            run_block,
            shifted_occupied,
            shifted_coords,
            norm_gains[1],
            w_qkv[1],
            w_out[1],
            w_up[1],
            w_down[1],
        ),
        rolled,
        bias_tables[1],
    )
    out_points = roll_values(second, 1) * occupied_mask
    grad_masked = grad_out[0, 0] * occupied_mask
    grad_second = roll_values(grad_masked, -1)
    grad_rolled, table_second = pull_second(grad_second)
    grad_first = roll_values(grad_rolled, 1)
    grad_points, table_first = pullback_first_block(grad_first)
    grad_tables = lax.psum(jnp.stack([table_first, table_second]), ("gx", "gy"))
    return (out_points[None, None], grad_points[None, None], grad_tables)


def solution(mesh):
    return jax.shard_map(
        on_device,
        mesh=mesh,
        in_specs=(
            P("gx", "gy", None, None),
            P("gx", "gy", None),
            P("gx", "gy", None, None),
            P(),
            P(),
            P(),
            P(),
            P(),
            P(),
            P("gx", "gy", None, None),
        ),
        out_specs=(P("gx", "gy", None, None), P("gx", "gy", None, None), P()),
        check_vma=False,
    )
```

profile of v0, /device:TPU:1, one launch (start us, length us, event | category | flops | bytes accessed | tf_op | source)
XLA Modules:
  0.0 234.5 jit_solution(2990567563567968579)
XLA Ops:
  0.6 0.5 broadcast.665
  1.2 2.0 convert_bitcast_fusion.2
  3.2 0.7 reduce.4
  4.0 8.7 %collective-permute-start.2 = (s32[4,2,32]{2,0,1:T(4,128)S(1)}, s32[4,2,32]{2,0,1:T(4,128)S(1)}, u32[]{:S(2)}, u32[]{:S(2)}) collective-permute-start(s32[4,2,32]{2,0,1:T(4,128)S(1)} %get-tuple-element.56), channel_id=1, source_target_pairs={{0,480},{32,0},{64,32},{96,64},{128,96},{160,128},{192,160},{224,1... | collective-permute-start | bytes 3080 | tf_op jit(solution)/shard_map/ppermute | solution.py:15
  12.8 0.7 convert_reduce_fusion.2
  13.7 9.7 %collective-permute-start.6 = (bf16[2,32,256]{2,1,0:T(8,128)(2,1)S(1)}, bf16[2,32,256]{2,1,0:T(8,128)(2,1)S(1)}, u32[]{:S(2)}, u32[]{:S(2)}) collective-permute-start(bf16[2,32,256]{2,1,0:T(8,128)(2,1)S(1)} %get-tuple-element.46), channel_id=1, source_target_pairs={{0,31},{1,0},{2,1},{3,2},{4,3},{5,4},{6,5},{7,6},{8,7},{9,8},{10,9... | collective-permute-start | bytes 98312 | tf_op jit(solution)/shard_map/ppermute | solution.py:15
  24.9 0.6 copy-done.42
  26.1 1.2 convolution_convert_fusion.5
  29.9 0.7 copy-done.2
  31.6 0.6 copy-done.32
  33.3 2.4 %collective-permute-start = (bf16[2,32,256]{2,1,0:T(8,128)(2,1)S(1)}, bf16[2,32,256]{2,1,0:T(8,128)(2,1)S(1)}, u32[]{:S(2)}, u32[]{:S(2)}) collective-permute-start(bf16[2,32,256]{2,1,0:T(8,128)(2,1)S(1)} %get-tuple-element.52), channel_id=1, source_target_pairs={{0,31},{1,0},{2,1},{3,2},{4,3},{5,4},{6,5},{7,6},{8,7},{9,8},{10,9... | collective-permute-start | bytes 98312 | tf_op jit(solution)/shard_map/ppermute | solution.py:15
  36.1 0.6 slice_bitcast_fusion.5
  37.0 2.2 collective-permute-start.3
  39.2 0.6 slice_bitcast_fusion.12
  39.8 0.6 copy.107
  40.6 0.7 collective-permute-done.3
  43.4 11.8 %collective-permute-start.1 = (bf16[2,32,256]{2,1,0:T(8,128)(2,1)S(1)}, bf16[2,32,256]{2,1,0:T(8,128)(2,1)S(1)}, u32[]{:S(2)}, u32[]{:S(2)}) collective-permute-start(bf16[2,32,256]{2,1,0:T(8,128)(2,1)S(1)} %get-tuple-element.50), channel_id=1, source_target_pairs={{0,480},{32,0},{64,32},{96,64},{128,96},{160,128},{192,160},{224,1... | collective-permute-start | bytes 98312 | tf_op jit(solution)/shard_map/ppermute | solution.py:15
  55.2 1.9 collective-permute-start.7
  60.4 0.9 fusion.25
  61.3 0.6 div.153
  62.0 1.8 multiply_reduce_fusion.4
  64.0 0.5 copy-done.38
  68.8 0.9 fusion.34
  70.2 0.8 fusion.37
  71.0 0.9 fusion.36
  71.8 0.6 convolution_bitcast_fusion
  72.4 0.6 convolution_bitcast_fusion.1
  73.0 0.6 convolution_bitcast_fusion.2
  73.6 0.7 add.251
  74.3 1.4 slice_bitcast_fusion.9
  75.7 3.0 %collective-permute-start.4 = (bf16[2,32,256]{2,1,0:T(8,128)(2,1)}, bf16[2,32,256]{2,1,0:T(8,128)(2,1)S(1)}, u32[]{:S(2)}, u32[]{:S(2)}) collective-permute-start(bf16[2,32,256]{2,1,0:T(8,128)(2,1)} %get-tuple-element.47), channel_id=1, source_target_pairs={{0,1},{1,2},{2,3},{3,4},{4,5},{5,6},{6,7},{7,8},{8,9},{9,10},{10,1... | collective-permute-start | bytes 98312 | tf_op jit(solution)/shard_map/ppermute | solution.py:15
  78.7 0.9 pad_add_fusion.1
  79.6 0.6 copy-done.24
  80.2 1.4 multiply_reduce_fusion.3
  81.6 0.7 copy-done.35
  82.5 0.6 copy-done.39
  83.3 1.9 collective-permute-start.8
  85.2 0.6 fusion.273
  85.8 0.6 copy-done.31
  86.6 0.6 fusion.280
  87.5 0.6 fusion.286
  88.5 8.2 %collective-permute-done.8 = bf16[2,32,256]{2,1,0:T(8,128)(2,1)S(1)} collective-permute-done((bf16[2,32,256]{2,1,0:T(8,128)(2,1)S(1)}, bf16[2,32,256]{2,1,0:T(8,128)(2,1)S(1)}, u32[]{:S(2)}, u32[]{:S(2)}) %collective-permute-start.8) | collective-permute-done | bytes 32800 | tf_op jit(solution)/shard_map/ppermute | solution.py:15
  96.7 5.1 %collective-permute-start.9 = (bf16[2,32,256]{2,1,0:T(8,128)(2,1)S(1)}, bf16[2,32,256]{2,1,0:T(8,128)(2,1)S(1)}, u32[]{:S(2)}, u32[]{:S(2)}) collective-permute-start(bf16[2,32,256]{2,1,0:T(8,128)(2,1)S(1)} %fusion.180), channel_id=1, source_target_pairs={{0,32},{32,64},{64,96},{96,128},{128,160},{160,192},{192,224},{224... | collective-permute-start | bytes 98312 | tf_op jit(solution)/shard_map/ppermute | solution.py:15
  101.8 1.9 collective-permute-start.5
  103.8 0.6 copy-done.21
  104.4 1.8 multiply_reduce_fusion.2
  106.2 0.6 copy-done.45
  106.8 0.7 copy-done.33
  113.7 0.7 copy-done.4
  114.9 0.6 convolution_bitcast_fusion.3
  115.5 0.6 convolution_bitcast_fusion.4
  116.1 0.6 convolution_bitcast_fusion.5
  117.5 0.6 copy-done.23
  118.2 1.4 fusion.147
  119.5 0.7 copy-done.43
  120.2 0.6 copy-done.37
  121.1 0.6 copy-done.6
  121.7 0.8 fusion.162
  122.5 0.6 fusion.292
  123.3 0.6 fusion.299
  124.2 0.6 fusion.305
  125.2 107.9 %psum.7 = f32[2,3,8,15]{3,2,1,0:T(8,128)} all-reduce(f32[2,3,8,15]{3,2,1,0:T(8,128)S(1)} %pad_maximum_fusion.6), channel_id=1, replica_groups=mesh['gx'=16,'gy'=32] {'gx','gy'}, use_global_device_ids=true, to_apply=%region_26.27 | all-reduce | flops 720 | bytes 5760 | tf_op jit(solution)/shard_map/psum | solution.py:201
  233.1 0.7 copy-done.34
  233.8 0.7 broadcast_multiply_fusion
  (251 shorter events, 27.4 us)
Async XLA Ops:
  0.6 12.9 %copy-start.15 = (bf16[1,1,128,256]{3,2,1,0:T(8,128)(2,1)S(1)}, bf16[1,1,128,256]{3,2,1,0:T(8,128)(2,1)}, u32[]{:S(2)}) copy-start(bf16[1,1,128,256]{3,2,1,0:T(8,128)(2,1)} %param.19) | copy-start | bytes 196612
  4.0 32.9 %collective-permute-start.2 = (s32[4,2,32]{2,0,1:T(4,128)S(1)}, s32[4,2,32]{2,0,1:T(4,128)S(1)}, u32[]{:S(2)}, u32[]{:S(2)}) collective-permute-start(s32[4,2,32]{2,0,1:T(4,128)S(1)} %get-tuple-element.56), channel_id=1, source_target_pairs={{0,480},{32,0},{64,32},{96,64},{128,96},{160,128},{192,160},{224,1... | collective-permute-start | bytes 3080 | tf_op jit(solution)/shard_map/ppermute | solution.py:15
  13.7 9.8 %copy-start.46 = (s32[1,1,128]{2,1,0:T(1,128)S(1)}, s32[1,1,128]{2,1,0:T(1,128)}, u32[]{:S(2)}) copy-start(s32[1,1,128]{2,1,0:T(1,128)} %param.11) | copy-start | bytes 1540
  13.7 9.8 %copy-start.16 = (f32[2,3,8,15]{3,2,1,0:T(8,128)S(1)}, f32[2,3,8,15]{3,2,1,0:T(8,128)}, u32[]{:S(2)}) copy-start(f32[2,3,8,15]{3,2,1,0:T(8,128)} %param.14) | copy-start | bytes 8644
  13.7 9.8 %copy-start.17 = (s32[1,1,3,128]{3,1,2,0:T(1,128)S(1)}, s32[1,1,3,128]{3,1,2,0:T(1,128)}, u32[]{:S(2)}) copy-start(s32[1,1,3,128]{3,1,2,0:T(1,128)} %param.12) | copy-start | bytes 4612
  13.7 41.5 %collective-permute-start.6 = (bf16[2,32,256]{2,1,0:T(8,128)(2,1)S(1)}, bf16[2,32,256]{2,1,0:T(8,128)(2,1)S(1)}, u32[]{:S(2)}, u32[]{:S(2)}) collective-permute-start(bf16[2,32,256]{2,1,0:T(8,128)(2,1)S(1)} %get-tuple-element.46), channel_id=1, source_target_pairs={{0,31},{1,0},{2,1},{3,2},{4,3},{5,4},{6,5},{7,6},{8,7},{9,8},{10,9... | collective-permute-start | bytes 98312 | tf_op jit(solution)/shard_map/ppermute | solution.py:15
  23.5 42.0 %copy-start.30 = (s32[8,8]{1,0:T(8,128)}, s32[8,8]{1,0:T(8,128)S(1)}, u32[]{:S(2)}) copy-start(s32[8,8]{1,0:T(8,128)S(1)} %subtract_add_fusion) | copy-start | bytes 772
  23.7 0.8 copy-start
  24.7 1.1 copy-start.22
  24.7 0.8 copy-start.29
  24.9 0.6 copy-start.42
  25.5 0.5 copy-start.36
  25.5 0.6 copy-start.40
  25.5 6.1 %copy-start.25 = (f32[1,1,256]{2,1,0:T(1,128)}, f32[1,1,256]{2,1,0:T(1,128)S(1)}, u32[]{:S(2)}) copy-start(f32[1,1,256]{2,1,0:T(1,128)S(1)} %get-tuple-element.64) | copy-start | bytes 3076
  25.5 32.0 %copy-start.27 = (f32[1,1,256]{2,1,0:T(1,128)}, f32[1,1,256]{2,1,0:T(1,128)S(1)}, u32[]{:S(2)}) copy-start(f32[1,1,256]{2,1,0:T(1,128)S(1)} %get-tuple-element.66) | copy-start | bytes 3076
  29.6 1.0 copy-start.2
  29.6 2.5 %copy-start.1 = (bf16[2,256,1024]{2,1,0:T(8,128)(2,1)S(1)}, bf16[2,256,1024]{2,1,0:T(8,128)(2,1)}, u32[]{:S(2)}) copy-start(bf16[2,256,1024]{2,1,0:T(8,128)(2,1)} %param.17) | copy-start | bytes 3145732
  29.9 2.6 %copy-start.48 = (bf16[2,1024,256]{2,1,0:T(8,128)(2,1)S(1)}, bf16[2,1024,256]{2,1,0:T(8,128)(2,1)}, u32[]{:S(2)}) copy-start(bf16[2,1024,256]{2,1,0:T(8,128)(2,1)} %param.18) | copy-start | bytes 3145732
  30.9 0.7 copy-start.20
  31.1 0.5 copy-start.44
  31.6 0.6 copy-start.32
  32.5 0.8 copy-start.7
  33.3 10.1 %collective-permute-start = (bf16[2,32,256]{2,1,0:T(8,128)(2,1)S(1)}, bf16[2,32,256]{2,1,0:T(8,128)(2,1)S(1)}, u32[]{:S(2)}, u32[]{:S(2)}) collective-permute-start(bf16[2,32,256]{2,1,0:T(8,128)(2,1)S(1)} %get-tuple-element.52), channel_id=1, source_target_pairs={{0,31},{1,0},{2,1},{3,2},{4,3},{5,4},{6,5},{7,6},{8,7},{9,8},{10,9... | collective-permute-start | bytes 98312 | tf_op jit(solution)/shard_map/ppermute | solution.py:15
  36.8 75.0 %copy-start.3 = (bf16[128,8,32]{0,2,1:T(8,128)(2,1)}, bf16[128,8,32]{0,2,1:T(8,128)(2,1)S(1)}, u32[]{:S(2)}) copy-start(bf16[128,8,32]{0,2,1:T(8,128)(2,1)S(1)} %get-tuple-element.27) | copy-start | bytes 196612
  37.0 4.4 %collective-permute-start.3 = (s32[4,2,32]{2,1,0:T(2,128)S(1)}, s32[4,2,32]{2,1,0:T(2,128)S(1)}, u32[]{:S(2)}, u32[]{:S(2)}) collective-permute-start(s32[4,2,32]{2,1,0:T(2,128)S(1)} %get-tuple-element.62), channel_id=1, source_target_pairs={{0,31},{1,0},{2,1},{3,2},{4,3},{5,4},{6,5},{7,6},{8,7},{9,8},{10,9... | collective-permute-start | bytes 3080 | tf_op jit(solution)/shard_map/ppermute | solution.py:15
  42.9 14.7 %copy-start.14 = (bf16[2,256,768]{2,1,0:T(8,128)(2,1)S(1)}, bf16[2,256,768]{2,1,0:T(8,128)(2,1)}, u32[]{:S(2)}) copy-start(bf16[2,256,768]{2,1,0:T(8,128)(2,1)} %param.15) | copy-start | bytes 2359300
  43.4 13.8 %collective-permute-start.1 = (bf16[2,32,256]{2,1,0:T(8,128)(2,1)S(1)}, bf16[2,32,256]{2,1,0:T(8,128)(2,1)S(1)}, u32[]{:S(2)}, u32[]{:S(2)}) collective-permute-start(bf16[2,32,256]{2,1,0:T(8,128)(2,1)S(1)} %get-tuple-element.50), channel_id=1, source_target_pairs={{0,480},{32,0},{64,32},{96,64},{128,96},{160,128},{192,160},{224,1... | collective-permute-start | bytes 98312 | tf_op jit(solution)/shard_map/ppermute | solution.py:15
  55.2 6.7 %collective-permute-start.7 = (bf16[2,32,256]{2,1,0:T(8,128)(2,1)S(1)}, bf16[2,32,256]{2,1,0:T(8,128)(2,1)S(1)}, u32[]{:S(2)}, u32[]{:S(2)}) collective-permute-start(bf16[2,32,256]{2,1,0:T(8,128)(2,1)S(1)} %get-tuple-element.44), channel_id=1, source_target_pairs={{0,480},{32,0},{64,32},{96,64},{128,96},{160,128},{192,160},{224,1... | collective-permute-start | bytes 98312 | tf_op jit(solution)/shard_map/ppermute | solution.py:15
  59.1 1.2 copy-start.49
  64.0 0.5 copy-start.38
  74.3 4.4 %copy-start.12 = (bf16[128,1,8,32]{0,3,2,1:T(8,128)(2,1)S(1)}, bf16[128,1,8,32]{0,3,2,1:T(8,128)(2,1)}, u32[]{:S(2)}) copy-start(bf16[128,1,8,32]{0,3,2,1:T(8,128)(2,1)} %fusion.37) | copy-start | bytes 196612
  74.3 4.4 %copy-start.13 = (bf16[128,1,8,32]{0,3,2,1:T(8,128)(2,1)S(1)}, bf16[128,1,8,32]{0,3,2,1:T(8,128)(2,1)}, u32[]{:S(2)}) copy-start(bf16[128,1,8,32]{0,3,2,1:T(8,128)(2,1)} %fusion.36) | copy-start | bytes 196612
  75.7 26.0 %copy-start.9 = (bf16[2,1,32,256]{3,2,1,0:T(8,128)(2,1)}, bf16[2,1,32,256]{3,2,1,0:T(8,128)(2,1)S(1)}, u32[]{:S(2)}) copy-start(bf16[2,1,32,256]{3,2,1,0:T(8,128)(2,1)S(1)} %get-tuple-element.48) | copy-start | bytes 98308
  75.7 26.0 %collective-permute-start.4 = (bf16[2,32,256]{2,1,0:T(8,128)(2,1)}, bf16[2,32,256]{2,1,0:T(8,128)(2,1)S(1)}, u32[]{:S(2)}, u32[]{:S(2)}) collective-permute-start(bf16[2,32,256]{2,1,0:T(8,128)(2,1)} %get-tuple-element.47), channel_id=1, source_target_pairs={{0,1},{1,2},{2,3},{3,4},{4,5},{5,6},{6,7},{7,8},{8,9},{9,10},{10,1... | collective-permute-start | bytes 98312 | tf_op jit(solution)/shard_map/ppermute | solution.py:15
  79.6 0.6 copy-start.24
  79.6 0.6 copy-start.28
  81.6 0.7 copy-start.35
  82.5 0.6 copy-start.39
  83.3 13.4 %collective-permute-start.8 = (bf16[2,32,256]{2,1,0:T(8,128)(2,1)S(1)}, bf16[2,32,256]{2,1,0:T(8,128)(2,1)S(1)}, u32[]{:S(2)}, u32[]{:S(2)}) collective-permute-start(bf16[2,32,256]{2,1,0:T(8,128)(2,1)S(1)} %get-tuple-element.41), channel_id=1, source_target_pairs={{0,1},{1,2},{2,3},{3,4},{4,5},{5,6},{6,7},{7,8},{8,9},{9,10},{10,1... | collective-permute-start | bytes 98312 | tf_op jit(solution)/shard_map/ppermute | solution.py:15
  85.8 0.7 copy-start.31
  87.5 16.2 %copy-start.8 = (f32[128,1024]{1,0:T(8,128)S(1)}, f32[128,1024]{1,0:T(8,128)}, u32[]{:S(2)}) copy-start(f32[128,1024]{1,0:T(8,128)} %copy-done.7) | copy-start | bytes 1572868
  96.7 7.0 %collective-permute-start.9 = (bf16[2,32,256]{2,1,0:T(8,128)(2,1)S(1)}, bf16[2,32,256]{2,1,0:T(8,128)(2,1)S(1)}, u32[]{:S(2)}, u32[]{:S(2)}) collective-permute-start(bf16[2,32,256]{2,1,0:T(8,128)(2,1)S(1)} %fusion.180), channel_id=1, source_target_pairs={{0,32},{32,64},{64,96},{96,128},{128,160},{160,192},{192,224},{224... | collective-permute-start | bytes 98312 | tf_op jit(solution)/shard_map/ppermute | solution.py:15
  101.8 15.2 %collective-permute-start.5 = (bf16[2,32,256]{2,1,0:T(8,128)(2,1)S(1)}, bf16[2,32,256]{2,1,0:T(8,128)(2,1)S(1)}, u32[]{:S(2)}, u32[]{:S(2)}) collective-permute-start(bf16[2,32,256]{2,1,0:T(8,128)(2,1)S(1)} %fusion.183), channel_id=1, source_target_pairs={{0,32},{32,64},{64,96},{96,128},{128,160},{160,192},{192,224},{224... | collective-permute-start | bytes 98312 | tf_op jit(solution)/shard_map/ppermute | solution.py:15
  103.7 4.0 %copy-start.5 = (bf16[2,2,32,256]{3,2,1,0:T(8,128)(2,1)}, bf16[2,2,32,256]{3,2,1,0:T(8,128)(2,1)S(1)}, u32[]{:S(2)}) copy-start(bf16[2,2,32,256]{3,2,1,0:T(8,128)(2,1)S(1)} %fusion.166) | copy-start | bytes 196612
  103.7 0.7 copy-start.21
  103.7 0.7 copy-start.26
  106.2 0.6 copy-start.45
  106.8 0.7 copy-start.33
  107.7 0.7 copy-start.18
  107.7 2.5 %copy-start.19 = (s32[1,1,3,128]{3,2,1,0:T(4,128)S(1)}, s32[1,1,3,128]{3,2,1,0:T(4,128)}, u32[]{:S(2)}) copy-start(s32[1,1,3,128]{3,2,1,0:T(4,128)} %copy.107) | copy-start | bytes 4612
  109.6 0.6 copy-start.47
  112.5 0.8 copy-start.11
  113.6 0.8 copy-start.4
  116.7 0.8 copy-start.10
  117.5 0.7 copy-start.23
  117.5 0.7 copy-start.41
  119.5 0.7 copy-start.43
  120.2 0.6 copy-start.37
  120.9 0.8 copy-start.6
  233.1 0.7 copy-start.34
where the time goes:
time: 236 us; the launch traced here: 234 us
  blocking collectives  108 us (46%)
  starting transfers between devices  48.7 us (21%)
  matrix products  35.1 us (15%)
  local copies, waits for them, and re-layouts  22.2 us (9%)
  other arithmetic  9.55 us (4%)
  waiting for transfers between devices  8.97 us (4%)
    psum x1, blocking collectives, on_device(): grad_tables = lax.psum(jnp.stack([table_first, table_second]), ('gx', 'gy'))  108 us
    ppermute x10, starting transfers between devices, from_behind(): return lax.ppermute(value, axis, pairs)  48.7 us
    unnamed x103, local copies, waits for them, and re-layouts  15.8 us
    ppermute x10, waiting for transfers between devices, from_behind(): return lax.ppermute(value, axis, pairs)  8.97 us
    dot_general x18, matrix products, relative_bias(): jnp.einsum('klu,tu->klt', left_factor, indicator_matrix, precision=highes...  8.74 us
    dot_general x18, matrix products, relative_bias(): jnp.einsum('dx,cxq->cdq', indicator_matrix, banded_offset_matrix, precisi...  5.59 us
    dot_general x18, matrix products, relative_bias(): jnp.einsum('hr,abr->hab', bias_table[axis_index], selection_matrix, preci...  4.86 us
  transfers between devices with their start and end apart: 10, of which 2 were waited for; matrix products, arithmetic and copies ran while one was open for 13% of the time, Pallas kernels for 0%

commit v1 on v0

v1 whole, which is shorter than its diff:
```python
from functools import partial

import jax
import jax.numpy as jnp
from jax import lax
from jax.experimental import pallas as pl
from jax.experimental.pallas import tpu as pltpu
from jax.sharding import Mesh
from jax.sharding import PartitionSpec as P

INTERPRET = False
EPS = 1e-05
BF = jnp.bfloat16
F32 = jnp.float32
SLOTS, WIDTH, HEADS, HD, QUAD = 128, 256, 8, 32, 32
SPAN, PITCH = 8, 16
SCALE = HD ** (-0.5)
MASKED = -1e30
VMEM_LIMIT = 24 * 1024 * 1024


def mm(a, b):
    return lax.dot_general(a, b, (((1,), (0,)), ((), ())), preferred_element_type=F32)


def mm_t(a, b):
    return lax.dot_general(a, b, (((1,), (1,)), ((), ())), preferred_element_type=F32)


def iota(shape, axis):
    return lax.broadcasted_iota(jnp.int32, shape, axis)


def normalise(values):
    centred = values - jnp.mean(values, axis=-1, keepdims=True)
    inv = lax.rsqrt(jnp.mean(centred * centred, axis=-1, keepdims=True) + EPS)
    return centred * inv, inv


def normalise_back(cot, unit, inv):
    return inv * (
        cot
        - jnp.mean(cot, axis=-1, keepdims=True)
        - unit * jnp.mean(cot * unit, axis=-1, keepdims=True)
    )


def cells(coords, mirrored):
    row = iota((PITCH, SLOTS), 0)
    if mirrored:
        row = SPAN - 1 - row
    return jnp.concatenate(
        [(coords[e : e + 1] == row).astype(F32) for e in range(3)], axis=0
    )


def slot_matrices(coords, occupied):
    mirrored = cells(coords, True)
    first_row = iota((PITCH, SLOTS), 0) == 0
    ones = jnp.where(first_row, 1.0, 0.0)
    mask = jnp.where(first_row & (occupied <= 0), MASKED, 0.0)
    blank = jnp.zeros((PITCH, SLOTS), F32)
    query = jnp.concatenate([mirrored, ones, blank, blank, blank, blank], axis=0)
    key = jnp.concatenate([mirrored, mirrored, mask, blank], axis=0)
    return jnp.transpose(query).astype(BF), jnp.transpose(key).astype(BF)


def table_matrix(table):
    lane = iota((SPAN, 128), 1)
    wide = []
    for e in range(3):
        row = jnp.concatenate(
            [table[e] * (1.0 / SCALE), jnp.zeros((HEADS, 128 - table.shape[-1]), F32)], axis=1
        )
        start = e * PITCH - (SPAN - 1)
        wide.append(
            pltpu.roll(row, start % 128, 1) + pltpu.roll(row, (start + 3 * PITCH) % 128, 1)
        )
    columns = []
    for h in range(HEADS):
        rows = []
        for e in range(3):
            value = pltpu.roll(
                jnp.broadcast_to(wide[e][h : h + 1], (SPAN, 128)), 0, 1, stride=1, stride_axis=0
            )
            high = value.astype(BF).astype(F32)
            value = jnp.where(lane < 3 * PITCH, high, value - high)
            base = lane % (3 * PITCH) - e * PITCH
            keep = (base >= 0) & (base < SPAN) & (lane < 6 * PITCH)
            rows += [jnp.where(keep, value, 0.0), jnp.zeros((SPAN, 128), F32)]
        one = (iota((PITCH, 128), 0) == 0) & (iota((PITCH, 128), 1) == 6 * PITCH)
        rows += [jnp.where(one, 1.0, 0.0), jnp.zeros((128 - 4 * PITCH, 128), F32)]
        columns.append(jnp.concatenate(rows, axis=0))
    return jnp.concatenate(columns, axis=1).astype(BF)


def spread(group):
    head = iota(group.shape, 1) // HD
    return jnp.concatenate(
        [jnp.where(head == j, group, jnp.zeros_like(group)) for j in range(4)], axis=0
    )


def side_by_side(stack):
    return jnp.concatenate([stack[j * SLOTS : (j + 1) * SLOTS] for j in range(4)], axis=1)


def gelu_parts(v):
    c = 0.7978845608028654
    t = jnp.tanh(c * (v + 0.044715 * (v * v * v)))
    return 0.5 * v * (1.0 + t), t


def gelu_slope(v):
    c = 0.7978845608028654
    t = jnp.tanh(c * (v + 0.044715 * (v * v * v)))
    return 0.5 * (1.0 + t) + 0.5 * v * (1.0 - t * t) * c * (1.0 + 3 * 0.044715 * (v * v))


def block_forward(hidden, gains, coords, occupied, table, w_qkv, w_out, w_up, w_down):
    unit, _ = normalise(hidden)
    projected = mm((unit * gains[0:1]).astype(BF), w_qkv[...]).astype(BF)
    query_side, key_side = slot_matrices(coords, occupied)
    bias_left = mm(query_side, table_matrix(table)).astype(BF)
    probs, mixed = [], []
    for g in range(2):
        q = projected[:, 128 * g : 128 * g + 128]
        k = projected[:, 256 + 128 * g : 256 + 128 * g + 128]
        v = projected[:, 512 + 128 * g : 512 + 128 * g + 128]
        lefts = jnp.concatenate(
            [bias_left[:, 128 * h : 128 * h + 128] for h in range(4 * g, 4 * g + 4)], axis=0
        )
        scores = mm_t(
            jnp.concatenate([spread(q), lefts], axis=1), jnp.concatenate([k, key_side], axis=1)
        )
        top = jnp.max(scores, axis=-1, keepdims=True)
        weights = jnp.exp((scores - top) * SCALE)
        soft = (weights * (1.0 / jnp.sum(weights, axis=-1, keepdims=True))).astype(BF)
        probs.append(soft)
        mixed.append(mm(side_by_side(soft), spread(v)))
    middle = hidden + mm(jnp.concatenate(mixed, axis=1).astype(BF), w_out[...])
    unit_two, _ = normalise(middle)
    up = mm((unit_two * gains[1:2]).astype(BF), w_up[...])
    expanded, _ = gelu_parts(up)
    out = middle + mm(expanded.astype(BF), w_down[...])
    return out.astype(BF), (projected, probs, middle, up)


def block_backward(cot, hidden, gains, coords, saved, w_qkv, w_out, w_up, w_down):
    projected, probs, middle, up = saved
    unit_two, inv_two = normalise(middle)
    cot_up = mm_t(cot, w_down[...]) * gelu_slope(up)
    cot_two = mm_t(cot_up.astype(BF), w_up[...]) * gains[1:2]
    cot_middle = cot.astype(F32) + normalise_back(cot_two, unit_two, inv_two)
    cot_mixed = mm_t(cot_middle.astype(BF), w_out[...]).astype(BF)
    cells_t = cells(coords, False).astype(BF)
    blank = jnp.zeros((SLOTS - 3 * PITCH, SLOTS), F32)
    cells_key = jnp.transpose(jnp.concatenate([cells(coords, True), blank], axis=0)).astype(BF)
    cot_q, cot_k, cot_v, pair_sums = [], [], [], []
    for g in range(2):
        q = projected[:, 128 * g : 128 * g + 128]
        k = projected[:, 256 + 128 * g : 256 + 128 * g + 128]
        v = projected[:, 512 + 128 * g : 512 + 128 * g + 128]
        dm = cot_mixed[:, 128 * g : 128 * g + 128]
        q_t = jnp.transpose(q.astype(F32)).astype(BF)
        dm_t = jnp.transpose(dm.astype(F32)).astype(BF)
        soft = probs[g]
        cot_soft = mm_t(spread(dm), v)
        weighted = soft.astype(F32) * cot_soft
        total = jnp.sum(weighted, axis=-1, keepdims=True)
        cot_scores = (weighted - soft.astype(F32) * total).astype(BF)
        cot_q.append(mm(side_by_side(cot_scores), spread(k)) * SCALE)
        k_rows, v_rows = [], []
        for j in range(4):
            rows = slice(j * SLOTS, (j + 1) * SLOTS)
            lanes = slice(j * HD, (j + 1) * HD)
            both = mm(jnp.concatenate([q_t[lanes], cells_t], axis=0), cot_scores[rows])
            k_rows.append(both[:HD])
            pair_sums.append(both[HD:])
            v_rows.append(mm(dm_t[lanes], soft[rows]))
        cot_k.append(jnp.transpose(jnp.concatenate(k_rows, axis=0)) * SCALE)
        cot_v.append(jnp.transpose(jnp.concatenate(v_rows, axis=0)))
    cot_projected = jnp.concatenate(cot_q + cot_k + cot_v, axis=1).astype(BF)
    cot_normed = mm_t(cot_projected, w_qkv[...]) * gains[0:1]
    unit, inv = normalise(hidden)
    cot_hidden = cot_middle + normalise_back(cot_normed, unit, inv)
    pairs = mm(jnp.concatenate(pair_sums, axis=0).astype(BF), cells_key)
    lane = iota((SPAN, 128), 1)
    tables = []
    for h in range(HEADS):
        per_axis = [
            pairs[(3 * h + e) * PITCH : (3 * h + e) * PITCH + SPAN] for e in range(3)
        ]
        value = jnp.where(lane < PITCH, per_axis[0], jnp.where(lane < 2 * PITCH, per_axis[1], per_axis[2]))
        value = jnp.where(lane < 3 * PITCH, value, 0.0)
        value = pltpu.roll(value, 0, 1, stride=1, stride_axis=0)
        tables.append(jnp.sum(value, axis=0, keepdims=True))
    return cot_hidden.astype(BF), jnp.concatenate(tables, axis=0)


def first_kernel(
    features, occupancy, coords, gains, tables, w_qkv, w_out, w_up, w_down, grad_out,
    own, to_y, to_x, to_xy, projected, probs, middle, up,
):
    occupied = occupancy[...]
    place = coords[...]
    out, saved = block_forward(
        features[...].astype(F32), gains[0], place, occupied, tables[0],
        w_qkv.at[0], w_out.at[0], w_up.at[0], w_down.at[0],
    )
    projected[...] = saved[0]
    probs[0] = saved[1][0]
    probs[1] = saved[1][1]
    middle[...] = saved[2]
    up[...] = saved[3]
    column = jnp.transpose(jnp.broadcast_to(occupied.astype(F32), (SLOTS, SLOTS)))
    grad = grad_out[...] * jnp.concatenate([column, column], axis=1).astype(BF)
    meta = jnp.concatenate([occupied, place, jnp.zeros((4, SLOTS), jnp.int32)], axis=0).astype(F32)
    meta = jnp.concatenate([meta, jnp.zeros((8, SLOTS), F32)], axis=0)
    meta = jnp.concatenate([meta, jnp.zeros((16, SLOTS), F32)], axis=1).astype(BF)
    for quarter, target in ((3, own), (2, to_y), (1, to_x), (0, to_xy)):
        rows = slice(quarter * QUAD, (quarter + 1) * QUAD)
        target[0:QUAD] = out[rows]
        target[QUAD : 2 * QUAD] = grad[rows]
        target[2 * QUAD : 2 * QUAD + 16] = meta


def second_kernel(
    own, from_y, from_x, from_xy, gains, tables, w_qkv, w_out, w_up, w_down,
    back_own, back_y, back_x, back_xy, table_cot,
):
    parts = (own, from_y, from_x, from_xy)
    hidden = jnp.concatenate([part[0:QUAD] for part in parts], axis=0).astype(F32)
    grad = jnp.concatenate([part[QUAD : 2 * QUAD] for part in parts], axis=0)
    quarter = iota((8, SLOTS), 1) // QUAD
    meta = jnp.zeros((8, SLOTS), F32)
    for position, part in enumerate(parts):
        rows = part[2 * QUAD : 2 * QUAD + 16].astype(F32)[0:8, 0:SLOTS]
        rows = pltpu.roll(rows, (2 * position - 3) * QUAD % SLOTS, 1)
        meta = jnp.where(quarter == position, rows, meta)
    meta = meta.astype(jnp.int32)
    half = SPAN // 2
    occupied = meta[0:1]
    place = jnp.concatenate(
        [(meta[1:2] + half) % SPAN, (meta[2:3] + half) % SPAN, meta[3:4]], axis=0
    )
    weights = (w_qkv.at[1], w_out.at[1], w_up.at[1], w_down.at[1])
    out, saved = block_forward(hidden, gains[1], place, occupied, tables[1], *weights)
    cot, table_cot[...] = block_backward(grad, hidden, gains[1], place, saved, *weights)
    for position, target in enumerate((back_own, back_y, back_x, back_xy)):
        rows = slice(position * QUAD, (position + 1) * QUAD)
        target[0:QUAD] = out[rows]
        target[QUAD : 2 * QUAD] = cot[rows]


def third_kernel(
    from_xy, from_x, from_y, own, features, occupancy, coords, gains, w_qkv, w_out, w_up, w_down,
    projected, probs, middle, up, table_cot,
    out_points, grad_points, tables_out,
):
    occupied = occupancy[...]
    parts = (from_xy, from_x, from_y, own)
    second = jnp.concatenate([part[0:QUAD] for part in parts], axis=0)
    cot = jnp.concatenate([part[QUAD : 2 * QUAD] for part in parts], axis=0)
    column = jnp.transpose(jnp.broadcast_to(occupied.astype(F32), (SLOTS, SLOTS)))
    out_points[...] = second * jnp.concatenate([column, column], axis=1).astype(BF)
    saved = (projected[...], (probs[0], probs[1]), middle[...], up[...])
    grad_points[...], table = block_backward(
        cot, features[...].astype(F32), gains[0], coords[...], saved,
        w_qkv.at[0], w_out.at[0], w_up.at[0], w_down.at[0],
    )
    both = table + pltpu.roll(table_cot[...], 3 * PITCH, 1)
    for i in range(tables_out.shape[0]):
        tables_out[i] = both


def unpack_kernel(parts, out):
    total = parts[0]
    for i in range(1, parts.shape[0]):
        total = total + parts[i]
    for k in range(2):
        for e in range(3):
            start = (3 * k + e) * PITCH
            moved = total if start == 0 else pltpu.roll(total, 128 - start, 1)
            out[k, e] = moved[:, : out.shape[-1]]


def call(kernel, shapes, *args):
    return pl.pallas_call(
        kernel,
        out_shape=[jax.ShapeDtypeStruct(s, d) for s, d in shapes],
        compiler_params=pltpu.CompilerParams(vmem_limit_bytes=VMEM_LIMIT),
        interpret=INTERPRET,
    )(*args)


def shift(value, axes, steps):
    sizes = [lax.axis_size(a) for a in axes]
    count = 1
    for n in sizes:
        count *= n
    pairs = []
    for source in range(count):
        rest, target, stride = source, 0, 1
        for n, t in zip(reversed(sizes), reversed(steps)):
            target += (rest % n + t) % n * stride
            rest //= n
            stride *= n
        pairs.append((source, target))
    return lax.ppermute(value, axes, pairs)


def on_device(
    gx, gy, phases,
    features, occupancy, coords, norm_gains, bias_tables, w_qkv, w_out, w_up, w_down, grad_out,
):
    size_x = lax.axis_size(gx)
    size_y = lax.axis_size(gy)

    def move(value, step_x, step_y):
        pairs = []
        for i in range(size_x):
            for j in range(size_y):
                target = (i + step_x) % size_x * size_y + (j + step_y) % size_y
                pairs.append((i * size_y + j, target))
        return lax.ppermute(value, gx + gy, pairs)

    points, occupied, place = features[0, 0], occupancy[0], coords[0, 0]
    weights = (w_qkv, w_out, w_up, w_down)
    width_ff = w_up.shape[-1]
    packet = ((2 * QUAD + 16, WIDTH), BF)
    reply = ((2 * QUAD, WIDTH), BF)
    own, to_y, to_x, to_xy, *saved = call(
        first_kernel,
        [packet] * 4
        + [((SLOTS, 3 * WIDTH), BF), ((2, 4 * SLOTS, SLOTS), BF), ((SLOTS, WIDTH), F32), ((SLOTS, width_ff), F32)],
        points, occupied, place, norm_gains, bias_tables, *weights, grad_out[0, 0],
    )
    from_y, from_x, from_xy = move(to_y, 0, -1), move(to_x, -1, 0), move(to_xy, -1, -1)
    back_own, back_y, back_x, back_xy, table_cot = call(
        second_kernel,
        [reply] * 4 + [((HEADS, 128), F32)],
        own, from_y, from_x, from_xy, norm_gains, bias_tables, *weights,
    )
    home_y, home_x, home_xy = move(back_y, 0, 1), move(back_x, 1, 0), move(back_xy, 1, 1)
    first = lax.axis_size(phases[0])
    out_points, grad_points, tables = call(
        third_kernel,
        [((SLOTS, WIDTH), BF), ((SLOTS, WIDTH), BF), ((first, HEADS, 128), F32)],
        home_xy, home_x, home_y, back_own, points, occupied, place, norm_gains, *weights,
        *saved, table_cot,
    )
    for phase, after in zip(phases, phases[1:] + (None,)):
        tables = lax.all_to_all(tables, phase, 0, 0)
        if after is not None:
            tables = jnp.broadcast_to(
                jnp.sum(tables, axis=0)[None], (lax.axis_size(after), HEADS, 128)
            )
    (grad_tables,) = call(unpack_kernel, [(bias_tables.shape, F32)], tables)
    return out_points[None, None], grad_points[None, None], grad_tables


def solution(mesh):
    shape = tuple(mesh.shape[a] for a in ("gx", "gy"))
    if shape == (16, 32):
        fine = Mesh(mesh.devices.reshape(2, 4, 2, 8, 4), ("zh", "y", "c", "zl", "x"))
        gx, gy = ("zh", "y", "c"), ("zl", "x")
        phases = (("y", "c", "x"), ("zh", "zl"))
    else:
        fine = Mesh(mesh.devices, ("gx", "gy"))
        gx, gy, phases = ("gx",), ("gy",), (("gx",), ("gy",))
    grid = P(gx, gy, None, None)
    return jax.shard_map(
        partial(on_device, gx, gy, phases),
        mesh=fine,
        in_specs=(grid, P(gx, gy, None), grid, P(), P(), P(), P(), P(), P(), grid),
        out_specs=(grid, grid, P()),
        check_vma=False,
    )
```

time: 236 us -> 104 us (0.44)
  blocking collectives: 108 us -> 38 us
  matrix products: 35.1 us -> 0 us
  local copies, waits for them, and re-layouts: 22.2 us -> 8.34 us
  starting transfers between devices: 48.7 us -> 35.7 us
  other arithmetic: 9.55 us -> 0.04 us
  Pallas kernels: 0 us -> 9.42 us
  waiting for transfers between devices: 8.97 us -> 11.6 us
    psum x1 -> x0, blocking collectives: 108 us -> none  [on_device(): grad_tables = lax.psum(jnp.stack([table_first, table_second]), ('gx', 'gy'))]
    all_to_all x0 -> x2, blocking collectives: none -> 38 us  [on_device(): tables = lax.all_to_all(tables, phase, 0, 0)]
    dot_general x82 -> x0, matrix products: 35.1 us -> none  [the longest x18 8.74 us: relative_bias(): jnp.einsum('klu,tu->klt', left_factor, indicator_matrix, precision=highes...]
    ppermute x10 -> x6, starting transfers between devices: 48.7 us -> 35.7 us  [move(): return lax.ppermute(value, gx + gy, pairs)]
    pallas_call x0 -> x4, Pallas kernels: none -> 9.42 us  [call(): pl.pallas_call(kernel, out_shape=[jax.ShapeDtypeStruct(s, d) for s, d in...]
    unnamed x103 -> x27, local copies, waits for them, and re-layouts: 15.8 us -> 8.33 us
    convert_element_type x5 -> x0, other arithmetic: 2.8 us -> none  [the longest x1 1.99 us: on_device(): occupied = occupancy[0, 0].astype(jnp.float32)]
    squeeze x5 -> x0, local copies, waits for them, and re-layouts: 2.67 us -> none  [the longest x2 1.42 us: roll_half(): upper_half = lax.index_in_dim(array, 1, position, keepdims=False)]
  transfers between devices with their start and end apart: 10 -> 6, of which waited for: 2 -> 3; matrix products, arithmetic and copies ran while one was open for 13% -> 0% of each run, Pallas kernels for 0% -> 0%
where the time goes in v1:
time: 104 us
  blocking collectives  38 us (37%)
  starting transfers between devices  35.7 us (34%)
  waiting for transfers between devices  11.6 us (11%)
  Pallas kernels  9.42 us (9%)
  local copies, waits for them, and re-layouts  8.34 us (8%)
    all_to_all x2, blocking collectives, on_device(): tables = lax.all_to_all(tables, phase, 0, 0)  38 us
    ppermute x6, starting transfers between devices, move(): return lax.ppermute(value, gx + gy, pairs)  35.7 us
    ppermute x6, waiting for transfers between devices, move(): return lax.ppermute(value, gx + gy, pairs)  11.6 us
    pallas_call x4, Pallas kernels, call(): pl.pallas_call(kernel, out_shape=[jax.ShapeDtypeStruct(s, d) for s, d in...  9.42 us
    unnamed x27, local copies, waits for them, and re-layouts  8.33 us
  transfers between devices with their start and end apart: 6, of which 3 were waited for; matrix products, arithmetic and copies ran while one was open for 0% of the time, Pallas kernels for 0%

profile of v1, /device:TPU:1, one launch (start us, length us, event | category | flops | bytes accessed | tf_op | source)
XLA Modules:
  0.0 103.8 jit_solution(12219192104613300715)
XLA Ops:
  0.6 0.7 copy.15
  1.3 0.0 copy-start.11
  1.3 0.0 copy-start.12
  1.3 0.7 copy-done.11
  2.0 0.0 copy-done.12
  2.0 0.0 copy-start
  2.0 1.2 %copy-done = bf16[2,256,1024]{2,1,0:T(8,128)(2,1)S(1)} copy-done((bf16[2,256,1024]{2,1,0:T(8,128)(2,1)S(1)}, bf16[2,256,1024]{2,1,0:T(8,128)(2,1)}, u32[]{:S(2)}) %copy-start) | copy-done | bytes 1048600
  3.2 0.0 copy-start.2
  3.2 1.2 %copy-done.2 = bf16[2,1024,256]{2,1,0:T(8,128)(2,1)S(1)} copy-done((bf16[2,1024,256]{2,1,0:T(8,128)(2,1)S(1)}, bf16[2,1024,256]{2,1,0:T(8,128)(2,1)}, u32[]{:S(2)}) %copy-start.2) | copy-done | bytes 1048600
  4.5 0.0 copy-start.4
  4.5 1.1 %copy-done.4 = bf16[2,256,768]{2,1,0:T(8,128)(2,1)S(1)} copy-done((bf16[2,256,768]{2,1,0:T(8,128)(2,1)S(1)}, bf16[2,256,768]{2,1,0:T(8,128)(2,1)}, u32[]{:S(2)}) %copy-start.4) | copy-done | bytes 786456
  5.6 0.0 copy-start.6
  5.6 0.9 copy-done.6
  6.5 0.0 copy-start.7
  6.5 0.8 copy-done.7
  7.4 0.0 copy-start.9
  7.4 0.7 copy-done.9
  8.1 0.0 copy-start.10
  8.1 0.8 copy-done.10
  9.0 0.0 copy-start.1
  9.0 0.0 copy-start.3
  9.0 0.0 copy-start.5
  9.0 2.0 %shard_map.121 = (bf16[80,256]{1,0:T(8,128)(2,1)S(1)}, bf16[80,256]{1,0:T(8,128)(2,1)S(1)}, bf16[80,256]{1,0:T(8,128)(2,1)S(1)}, bf16[80,256]{1,0:T(8,128)(2,1)S...) custom-call(bf16[128,256]{1,0:T(8,128)(2,1)S(1)} %bitcast.8, ...), custom_call_target="tpu_custom_call" | custom-call | tf_op jit(solution)/shard_map/pallas_call | solution.py:289
  11.0 15.9 %collective-permute-start = (bf16[80,256]{1,0:T(8,128)(2,1)S(1)}, bf16[80,256]{1,0:T(8,128)(2,1)S(1)}, u32[]{:S(2)}, u32[]{:S(2)}) collective-permute-start(bf16[80,256]{1,0:T(8,128)(2,1)S(1)} %get-tuple-element.20), channel_id=1, source_target_pairs={{0,31},{1,0},{2,1},{3,2},{4,3},{5,4},{6,5},{7,6},{8,7},{9,8},{10,9... | collective-permute-start | bytes 122888 | tf_op jit(solution)/shard_map/ppermute | solution.py:326
  26.9 2.9 %collective-permute-start.1 = (bf16[80,256]{1,0:T(8,128)(2,1)S(1)}, bf16[80,256]{1,0:T(8,128)(2,1)S(1)}, u32[]{:S(2)}, u32[]{:S(2)}) collective-permute-start(bf16[80,256]{1,0:T(8,128)(2,1)S(1)} %get-tuple-element.21), channel_id=1, source_target_pairs={{0,480},{1,481},{2,482},{3,483},{4,484},{5,485},{6,486},{7,487},{8... | collective-permute-start | bytes 122888 | tf_op jit(solution)/shard_map/ppermute | solution.py:326
  29.8 10.3 %collective-permute-start.2 = (bf16[80,256]{1,0:T(8,128)(2,1)S(1)}, bf16[80,256]{1,0:T(8,128)(2,1)S(1)}, u32[]{:S(2)}, u32[]{:S(2)}) collective-permute-start(bf16[80,256]{1,0:T(8,128)(2,1)S(1)} %get-tuple-element.22), channel_id=1, source_target_pairs={{0,511},{1,480},{2,481},{3,482},{4,483},{5,484},{6,485},{7,486},{8... | collective-permute-start | bytes 122888 | tf_op jit(solution)/shard_map/ppermute | solution.py:326
  40.1 0.0 collective-permute-done.from_y
  40.1 0.0 collective-permute-done.1.from_x
  40.1 1.1 %collective-permute-done.2.from_xy = bf16[80,256]{1,0:T(8,128)(2,1)S(1)} collective-permute-done((bf16[80,256]{1,0:T(8,128)(2,1)S(1)}, bf16[80,256]{1,0:T(8,128)(2,1)S(1)}, u32[]{:S(2)}, u32[]{:S(2)}) %collective-permute-start.2) | collective-permute-done | bytes 40992 | tf_op jit(solution)/shard_map/ppermute | solution.py:326
  41.1 0.0 copy-done.1
  41.1 0.0 copy-done.3
  41.1 0.0 copy-done.5
  41.1 0.0 copy-start.8
  41.2 3.9 %shard_map.122 = (bf16[64,256]{1,0:T(8,128)(2,1)S(1)}, bf16[64,256]{1,0:T(8,128)(2,1)S(1)}, bf16[64,256]{1,0:T(8,128)(2,1)S(1)}, bf16[64,256]{1,0:T(8,128)(2,1)S(1)}, f32[8,128]{1,0:T(8,128)S(1)}) custom-call(bf16[80,256]{1,0:T(8,128)(2,1)S(1)} %get-tuple-element.19.own, bf16[80,256]{1,0:T(8,128)(2,1)S(1)} %collective-permute-done.from_y, ...), custom_call_target="tpu_custom_call" | custom-call | tf_op jit(solution)/shard_map/pallas_call | solution.py:289
  45.1 1.9 %collective-permute-start.3 = (bf16[64,256]{1,0:T(8,128)(2,1)S(1)}, bf16[64,256]{1,0:T(8,128)(2,1)S(1)}, u32[]{:S(2)}, u32[]{:S(2)}) collective-permute-start(bf16[64,256]{1,0:T(8,128)(2,1)S(1)} %get-tuple-element.23), channel_id=1, source_target_pairs={{0,33},{1,34},{2,35},{3,36},{4,37},{5,38},{6,39},{7,40},{8,41},{9,... | collective-permute-start | bytes 98312 | tf_op jit(solution)/shard_map/ppermute | solution.py:326
  47.0 1.9 %collective-permute-start.4 = (bf16[64,256]{1,0:T(8,128)(2,1)S(1)}, bf16[64,256]{1,0:T(8,128)(2,1)S(1)}, u32[]{:S(2)}, u32[]{:S(2)}) collective-permute-start(bf16[64,256]{1,0:T(8,128)(2,1)S(1)} %get-tuple-element.24), channel_id=1, source_target_pairs={{0,32},{1,33},{2,34},{3,35},{4,36},{5,37},{6,38},{7,39},{8,40},{9,... | collective-permute-start | bytes 98312 | tf_op jit(solution)/shard_map/ppermute | solution.py:326
  48.9 2.8 %collective-permute-start.5 = (bf16[64,256]{1,0:T(8,128)(2,1)S(1)}, bf16[64,256]{1,0:T(8,128)(2,1)S(1)}, u32[]{:S(2)}, u32[]{:S(2)}) collective-permute-start(bf16[64,256]{1,0:T(8,128)(2,1)S(1)} %get-tuple-element.25), channel_id=1, source_target_pairs={{0,1},{1,2},{2,3},{3,4},{4,5},{5,6},{6,7},{7,8},{8,9},{9,10},{10,1... | collective-permute-start | bytes 98312 | tf_op jit(solution)/shard_map/ppermute | solution.py:326
  51.8 7.9 %collective-permute-done.3.from_xy = bf16[64,256]{1,0:T(8,128)(2,1)S(1)} collective-permute-done((bf16[64,256]{1,0:T(8,128)(2,1)S(1)}, bf16[64,256]{1,0:T(8,128)(2,1)S(1)}, u32[]{:S(2)}, u32[]{:S(2)}) %collective-permute-start.3) | collective-permute-done | bytes 32800 | tf_op jit(solution)/shard_map/ppermute | solution.py:326
  59.6 0.0 collective-permute-done.4.from_x
  59.6 2.7 %collective-permute-done.5.from_y = bf16[64,256]{1,0:T(8,128)(2,1)S(1)} collective-permute-done((bf16[64,256]{1,0:T(8,128)(2,1)S(1)}, bf16[64,256]{1,0:T(8,128)(2,1)S(1)}, u32[]{:S(2)}, u32[]{:S(2)}) %collective-permute-start.5) | collective-permute-done | bytes 32800 | tf_op jit(solution)/shard_map/ppermute | solution.py:326
  62.3 0.0 copy-done.8
  62.3 2.8 %shard_map.123 = (bf16[128,256]{1,0:T(8,128)(2,1)}, bf16[128,256]{1,0:T(8,128)(2,1)}, f32[32,8,128]{2,1,0:T(8,128)S(1)}) custom-call(bf16[64,256]{1,0:T(8,128)(2,1)S(1)} %collective-permute-done.3.from_xy, bf16[64,256]{1,0:T(8,128)(2,1)S(1)} %collective-permute-done.4.from_x, bf16[64,256]{1,0:T(8,128)(2,1)S(1)} %collective-permute-done.5.from_y, ...), custom_call_target="tpu_custom_call" | custom-call | tf_op jit(solution)/shard_map/pallas_call | solution.py:289
  65.1 19.2 %all_to_all.10 = f32[32,8,128]{2,1,0:T(8,128)S(1)} all-to-all(f32[32,8,128]{2,1,0:T(8,128)S(1)} %get-tuple-element.34), channel_id=1, replica_groups=mesh['zh'=2,'y'=4,'c'=2,'zl'=8,'x'=4] {'y','c','x'}, dimensions={0} | all-to-all | bytes 262144 | tf_op jit(solution)/shard_map/all_to_all | solution.py:354
  84.3 18.8 %all_to_all.11.parts = f32[16,8,128]{2,1,0:T(8,128)S(1)} all-to-all(f32[16,8,128]{2,1,0:T(8,128)S(1)} %broadcast_in_dim.14), channel_id=1, replica_groups=mesh['zh'=2,'y'=4,'c'=2,'zl'=8,'x'=4] {'zh','zl'}, dimensions={0} | all-to-all | bytes 131072 | tf_op jit(solution)/shard_map/all_to_all | solution.py:354
  103.1 0.7 shard_map.124
  (2 shorter events, 0.0 us)
Async XLA Ops:
  1.3 0.7 copy-start.11
  1.3 0.7 copy-start.12
  2.0 1.2 %copy-start = (bf16[2,256,1024]{2,1,0:T(8,128)(2,1)S(1)}, bf16[2,256,1024]{2,1,0:T(8,128)(2,1)}, u32[]{:S(2)}) copy-start(bf16[2,256,1024]{2,1,0:T(8,128)(2,1)} %w_up.5) | copy-start | bytes 3145732
  3.2 1.2 %copy-start.2 = (bf16[2,1024,256]{2,1,0:T(8,128)(2,1)S(1)}, bf16[2,1024,256]{2,1,0:T(8,128)(2,1)}, u32[]{:S(2)}) copy-start(bf16[2,1024,256]{2,1,0:T(8,128)(2,1)} %w_down.5) | copy-start | bytes 3145732
  4.5 1.1 %copy-start.4 = (bf16[2,256,768]{2,1,0:T(8,128)(2,1)S(1)}, bf16[2,256,768]{2,1,0:T(8,128)(2,1)}, u32[]{:S(2)}) copy-start(bf16[2,256,768]{2,1,0:T(8,128)(2,1)} %w_qkv.5) | copy-start | bytes 2359300
  5.6 0.9 copy-start.6
  6.5 0.8 copy-start.7
  7.4 0.7 copy-start.9
  8.1 0.8 copy-start.10
  9.0 32.2 %copy-start.1 = (bf16[2,256,1024]{2,1,0:T(8,128)(2,1)S(1)}, bf16[2,256,1024]{2,1,0:T(8,128)(2,1)}, u32[]{:S(2)}) copy-start(bf16[2,256,1024]{2,1,0:T(8,128)(2,1)} %w_up.5) | copy-start | bytes 3145732
  9.0 32.2 %copy-start.3 = (bf16[2,1024,256]{2,1,0:T(8,128)(2,1)S(1)}, bf16[2,1024,256]{2,1,0:T(8,128)(2,1)}, u32[]{:S(2)}) copy-start(bf16[2,1024,256]{2,1,0:T(8,128)(2,1)} %w_down.5) | copy-start | bytes 3145732
  9.0 32.2 %copy-start.5 = (bf16[2,256,768]{2,1,0:T(8,128)(2,1)S(1)}, bf16[2,256,768]{2,1,0:T(8,128)(2,1)}, u32[]{:S(2)}) copy-start(bf16[2,256,768]{2,1,0:T(8,128)(2,1)} %w_qkv.5) | copy-start | bytes 2359300
  11.0 29.0 %collective-permute-start = (bf16[80,256]{1,0:T(8,128)(2,1)S(1)}, bf16[80,256]{1,0:T(8,128)(2,1)S(1)}, u32[]{:S(2)}, u32[]{:S(2)}) collective-permute-start(bf16[80,256]{1,0:T(8,128)(2,1)S(1)} %get-tuple-element.20), channel_id=1, source_target_pairs={{0,31},{1,0},{2,1},{3,2},{4,3},{5,4},{6,5},{7,6},{8,7},{9,8},{10,9... | collective-permute-start | bytes 122888 | tf_op jit(solution)/shard_map/ppermute | solution.py:326
  26.9 13.2 %collective-permute-start.1 = (bf16[80,256]{1,0:T(8,128)(2,1)S(1)}, bf16[80,256]{1,0:T(8,128)(2,1)S(1)}, u32[]{:S(2)}, u32[]{:S(2)}) collective-permute-start(bf16[80,256]{1,0:T(8,128)(2,1)S(1)} %get-tuple-element.21), channel_id=1, source_target_pairs={{0,480},{1,481},{2,482},{3,483},{4,484},{5,485},{6,486},{7,487},{8... | collective-permute-start | bytes 122888 | tf_op jit(solution)/shard_map/ppermute | solution.py:326
  29.8 11.3 %collective-permute-start.2 = (bf16[80,256]{1,0:T(8,128)(2,1)S(1)}, bf16[80,256]{1,0:T(8,128)(2,1)S(1)}, u32[]{:S(2)}, u32[]{:S(2)}) collective-permute-start(bf16[80,256]{1,0:T(8,128)(2,1)S(1)} %get-tuple-element.22), channel_id=1, source_target_pairs={{0,511},{1,480},{2,481},{3,482},{4,483},{5,484},{6,485},{7,486},{8... | collective-permute-start | bytes 122888 | tf_op jit(solution)/shard_map/ppermute | solution.py:326
  41.1 21.2 %copy-start.8 = (bf16[1,1,128,256]{3,2,1,0:T(8,128)(2,1)S(1)}, bf16[1,1,128,256]{3,2,1,0:T(8,128)(2,1)}, u32[]{:S(2)}) copy-start(bf16[1,1,128,256]{3,2,1,0:T(8,128)(2,1)} %param.10) | copy-start | bytes 196612
  45.1 14.6 %collective-permute-start.3 = (bf16[64,256]{1,0:T(8,128)(2,1)S(1)}, bf16[64,256]{1,0:T(8,128)(2,1)S(1)}, u32[]{:S(2)}, u32[]{:S(2)}) collective-permute-start(bf16[64,256]{1,0:T(8,128)(2,1)S(1)} %get-tuple-element.23), channel_id=1, source_target_pairs={{0,33},{1,34},{2,35},{3,36},{4,37},{5,38},{6,39},{7,40},{8,41},{9,... | collective-permute-start | bytes 98312 | tf_op jit(solution)/shard_map/ppermute | solution.py:326
  47.0 12.6 %collective-permute-start.4 = (bf16[64,256]{1,0:T(8,128)(2,1)S(1)}, bf16[64,256]{1,0:T(8,128)(2,1)S(1)}, u32[]{:S(2)}, u32[]{:S(2)}) collective-permute-start(bf16[64,256]{1,0:T(8,128)(2,1)S(1)} %get-tuple-element.24), channel_id=1, source_target_pairs={{0,32},{1,33},{2,34},{3,35},{4,36},{5,37},{6,38},{7,39},{8,40},{9,... | collective-permute-start | bytes 98312 | tf_op jit(solution)/shard_map/ppermute | solution.py:326
  48.9 13.4 %collective-permute-start.5 = (bf16[64,256]{1,0:T(8,128)(2,1)S(1)}, bf16[64,256]{1,0:T(8,128)(2,1)S(1)}, u32[]{:S(2)}, u32[]{:S(2)}) collective-permute-start(bf16[64,256]{1,0:T(8,128)(2,1)S(1)} %get-tuple-element.25), channel_id=1, source_target_pairs={{0,1},{1,2},{2,3},{3,4},{4,5},{5,6},{6,7},{7,8},{8,9},{9,10},{10,1... | collective-permute-start | bytes 98312 | tf_op jit(solution)/shard_map/ppermute | solution.py:326

commit v2 on v1

v2 whole, which is shorter than its diff:
```python
from functools import partial

import jax
import jax.numpy as jnp
from jax import lax
from jax.experimental import pallas as pl
from jax.experimental.pallas import tpu as pltpu
from jax.sharding import Mesh
from jax.sharding import PartitionSpec as P

INTERPRET = False
EPS = 1e-05
BF = jnp.bfloat16
F32 = jnp.float32
SLOTS, WIDTH, HEADS, HD, QUAD = 128, 256, 8, 32, 32
SPAN, PITCH = 8, 16
SCALE = HD ** (-0.5)
MASKED = -1e30
VMEM_LIMIT = 24 * 1024 * 1024


def mm(a, b):
    return lax.dot_general(a, b, (((1,), (0,)), ((), ())), preferred_element_type=F32)


def mm_t(a, b):
    return lax.dot_general(a, b, (((1,), (1,)), ((), ())), preferred_element_type=F32)


def mm_left(a, b):
    return lax.dot_general(a, b, (((0,), (0,)), ((), ())), preferred_element_type=F32)


def iota(shape, axis):
    return lax.broadcasted_iota(jnp.int32, shape, axis)


def normalise(values):
    centred = values - jnp.mean(values, axis=-1, keepdims=True)
    inv = lax.rsqrt(jnp.mean(centred * centred, axis=-1, keepdims=True) + EPS)
    return centred * inv, inv


def normalise_back(cot, unit, inv):
    return inv * (
        cot
        - jnp.mean(cot, axis=-1, keepdims=True)
        - unit * jnp.mean(cot * unit, axis=-1, keepdims=True)
    )


def cells(coords, mirrored):
    row = iota((PITCH, SLOTS), 0)
    if mirrored:
        row = SPAN - 1 - row
    return jnp.concatenate(
        [(coords[e : e + 1] == row).astype(F32) for e in range(3)], axis=0
    )


def query_cells(coords):
    ones = jnp.where(iota((PITCH, SLOTS), 0) == 0, 1.0, 0.0)
    return jnp.concatenate(
        [cells(coords, True), ones, jnp.zeros((SLOTS - 4 * PITCH, SLOTS), F32)], axis=0
    )


def key_cells(coords, occupied):
    mirrored = cells(coords, True)
    mask = jnp.where((iota((PITCH, SLOTS), 0) == 0) & (occupied <= 0), MASKED, 0.0)
    return jnp.concatenate([mirrored, mirrored, mask, jnp.zeros((PITCH, SLOTS), F32)], axis=0)


def table_matrix(table):
    lane = iota((SPAN, 128), 1)
    wide = []
    for e in range(3):
        row = jnp.concatenate(
            [table[e] * (1.0 / SCALE), jnp.zeros((HEADS, 128 - table.shape[-1]), F32)], axis=1
        )
        start = e * PITCH - (SPAN - 1)
        wide.append(
            pltpu.roll(row, start % 128, 1) + pltpu.roll(row, (start + 3 * PITCH) % 128, 1)
        )
    columns = []
    for h in range(HEADS):
        rows = []
        for e in range(3):
            value = pltpu.roll(
                jnp.broadcast_to(wide[e][h : h + 1], (SPAN, 128)), 0, 1, stride=1, stride_axis=0
            )
            high = value.astype(BF).astype(F32)
            value = jnp.where(lane < 3 * PITCH, high, value - high)
            base = lane % (3 * PITCH) - e * PITCH
            keep = (base >= 0) & (base < SPAN) & (lane < 6 * PITCH)
            rows += [jnp.where(keep, value, 0.0), jnp.zeros((SPAN, 128), F32)]
        one = (iota((PITCH, 128), 0) == 0) & (iota((PITCH, 128), 1) == 6 * PITCH)
        rows += [jnp.where(one, 1.0, 0.0), jnp.zeros((128 - 4 * PITCH, 128), F32)]
        columns.append(jnp.concatenate(rows, axis=0))
    return jnp.concatenate(columns, axis=1).astype(BF)


def spread(group):
    head = iota(group.shape, 1) // HD
    return jnp.concatenate(
        [jnp.where(head == j, group, jnp.zeros_like(group)) for j in range(4)], axis=0
    )


def side_by_side(stack):
    return jnp.concatenate([stack[j * SLOTS : (j + 1) * SLOTS] for j in range(4)], axis=1)


def softmax(scores):
    weights = jnp.exp((scores - jnp.max(scores, axis=-1, keepdims=True)) * SCALE)
    return (weights * (1.0 / jnp.sum(weights, axis=-1, keepdims=True))).astype(BF)


def gelu_parts(v):
    c = 0.7978845608028654
    t = jnp.tanh(c * (v + 0.044715 * (v * v * v)))
    return 0.5 * v * (1.0 + t), t


def gelu_slope(v):
    c = 0.7978845608028654
    t = jnp.tanh(c * (v + 0.044715 * (v * v * v)))
    return 0.5 * (1.0 + t) + 0.5 * v * (1.0 - t * t) * c * (1.0 + 3 * 0.044715 * (v * v))


def block_forward(hidden, gains, coords, occupied, table, w_qkv, w_out, w_up, w_down):
    unit, _ = normalise(hidden)
    projected = mm((unit * gains[0:1]).astype(BF), w_qkv[...]).astype(BF)
    query_side = jnp.transpose(query_cells(coords)).astype(BF)
    key_side = jnp.transpose(key_cells(coords, occupied)).astype(BF)
    bias_left = mm(query_side, table_matrix(table)).astype(BF)
    probs, mixed = [], []
    for g in range(2):
        q = projected[:, 128 * g : 128 * g + 128]
        k = projected[:, 256 + 128 * g : 256 + 128 * g + 128]
        v = projected[:, 512 + 128 * g : 512 + 128 * g + 128]
        lefts = jnp.concatenate(
            [bias_left[:, 128 * h : 128 * h + 128] for h in range(4 * g, 4 * g + 4)], axis=0
        )
        scores = mm_t(
            jnp.concatenate([spread(q), lefts], axis=1), jnp.concatenate([k, key_side], axis=1)
        )
        soft = softmax(scores)
        probs.append(soft)
        mixed.append(mm(side_by_side(soft), spread(v)))
    middle = hidden + mm(jnp.concatenate(mixed, axis=1).astype(BF), w_out[...])
    unit_two, _ = normalise(middle)
    up = mm((unit_two * gains[1:2]).astype(BF), w_up[...])
    expanded, _ = gelu_parts(up)
    out = middle + mm(expanded.astype(BF), w_down[...])
    return out.astype(BF), (projected, probs, middle, up)


def feed_forward_back(cot, gains, middle, up, w_out, w_up, w_down):
    unit, inv = normalise(middle)
    cot_up = mm_t(cot, w_down[...]) * gelu_slope(up)
    cot_two = mm_t(cot_up.astype(BF), w_up[...]) * gains[1:2]
    cot_middle = cot.astype(F32) + normalise_back(cot_two, unit, inv)
    return cot_middle, mm_t(cot_middle.astype(BF), w_out[...]).astype(BF)


def table_sums(per_head):
    lane = iota((SPAN, 128), 1)
    tables = []
    for blocks in per_head:
        value = jnp.where(lane < PITCH, blocks[0], jnp.where(lane < 2 * PITCH, blocks[1], blocks[2]))
        value = jnp.where(lane < 3 * PITCH, value, 0.0)
        value = pltpu.roll(value, 0, 1, stride=1, stride_axis=0)
        tables.append(jnp.sum(value, axis=0, keepdims=True))
    return jnp.concatenate(tables, axis=0)


def block_backward(cot, hidden, gains, coords, saved, w_qkv, w_out, w_up, w_down):
    projected, probs, middle, up = saved
    cot_middle, cot_mixed = feed_forward_back(cot, gains, middle, up, w_out, w_up, w_down)
    cells_t = cells(coords, False).astype(BF)
    blank = jnp.zeros((SLOTS - 3 * PITCH, SLOTS), F32)
    cells_key = jnp.transpose(jnp.concatenate([cells(coords, True), blank], axis=0)).astype(BF)
    cot_q, cot_k, cot_v, pair_sums = [], [], [], []
    for g in range(2):
        q = projected[:, 128 * g : 128 * g + 128]
        k = projected[:, 256 + 128 * g : 256 + 128 * g + 128]
        v = projected[:, 512 + 128 * g : 512 + 128 * g + 128]
        dm = cot_mixed[:, 128 * g : 128 * g + 128]
        q_t = jnp.transpose(q.astype(F32)).astype(BF)
        dm_t = jnp.transpose(dm.astype(F32)).astype(BF)
        soft = probs[g]
        cot_soft = mm_t(spread(dm), v)
        weighted = soft.astype(F32) * cot_soft
        total = jnp.sum(weighted, axis=-1, keepdims=True)
        cot_scores = (weighted - soft.astype(F32) * total).astype(BF)
        cot_q.append(mm(side_by_side(cot_scores), spread(k)) * SCALE)
        k_rows, v_rows = [], []
        for j in range(4):
            rows = slice(j * SLOTS, (j + 1) * SLOTS)
            lanes = slice(j * HD, (j + 1) * HD)
            both = mm(jnp.concatenate([q_t[lanes], cells_t], axis=0), cot_scores[rows])
            k_rows.append(both[:HD])
            pair_sums.append(both[HD:])
            v_rows.append(mm(dm_t[lanes], soft[rows]))
        cot_k.append(jnp.transpose(jnp.concatenate(k_rows, axis=0)) * SCALE)
        cot_v.append(jnp.transpose(jnp.concatenate(v_rows, axis=0)))
    cot_projected = jnp.concatenate(cot_q + cot_k + cot_v, axis=1).astype(BF)
    cot_normed = mm_t(cot_projected, w_qkv[...]) * gains[0:1]
    unit, inv = normalise(hidden)
    cot_hidden = cot_middle + normalise_back(cot_normed, unit, inv)
    pairs = mm(jnp.concatenate(pair_sums, axis=0).astype(BF), cells_key)
    per_head = [
        [pairs[(3 * h + e) * PITCH : (3 * h + e) * PITCH + SPAN] for e in range(3)]
        for h in range(HEADS)
    ]
    return cot_hidden.astype(BF), table_sums(per_head)


def head_lanes(stack):
    rows = stack.shape[0] // 4
    head = iota((rows, 128), 1) // HD
    out = jnp.zeros((rows, 128), stack.dtype)
    for j in range(4):
        out = jnp.where(head == j, stack[j * rows : (j + 1) * rows], out)
    return out


def halo_forward(points, places, occupieds, place, gains, table, w_qkv, w_out, w_up, w_down):
    unit, inv = normalise(points)
    normed = (unit * gains[0:1]).astype(BF)
    key_value = mm(normed, w_qkv[:, WIDTH:]).astype(BF)
    quarters = [slice(p * SLOTS + (3 - p) * QUAD, p * SLOTS + (4 - p) * QUAD) for p in range(4)]
    query = mm(jnp.concatenate([normed[r] for r in quarters], axis=0), w_qkv[:, :WIDTH]).astype(BF)
    hidden = jnp.concatenate([points[r] for r in quarters], axis=0)
    query_side = jnp.transpose(query_cells(place)).astype(BF)
    bias_left = mm(query_side, table_matrix(table)).astype(BF)
    probs, mixed, key_sides = {}, [], []
    for p in range(4):
        key_side = jnp.transpose(key_cells(places[p], occupieds[p])).astype(BF)
        key_sides.append(key_side)
        rows, window = slice(p * QUAD, (p + 1) * QUAD), slice(p * SLOTS, (p + 1) * SLOTS)
        groups = []
        for g in range(2):
            lanes = slice(128 * g, 128 * g + 128)
            k = key_value[window, 128 * g : 128 * g + 128]
            v = key_value[window, WIDTH + 128 * g : WIDTH + 128 * g + 128]
            lefts = jnp.concatenate(
                [bias_left[rows, 128 * h : 128 * h + 128] for h in range(4 * g, 4 * g + 4)], axis=0
            )
            scores = mm_t(
                jnp.concatenate([spread(query[rows, lanes]), lefts], axis=1),
                jnp.concatenate([k, key_side], axis=1),
            )
            probs[p, g] = softmax(scores)
            groups.append(head_lanes(mm(probs[p, g], v)))
        mixed.append(jnp.concatenate(groups, axis=1))
    middle = hidden + mm(jnp.concatenate(mixed, axis=0).astype(BF), w_out[...])
    unit_two, _ = normalise(middle)
    up = mm((unit_two * gains[1:2]).astype(BF), w_up[...])
    expanded, _ = gelu_parts(up)
    out = middle + mm(expanded.astype(BF), w_down[...])
    return out.astype(BF), (unit, inv, query, key_value, probs, key_sides, middle, up)


def halo_backward(cot, place, gains, saved, w_qkv, w_out, w_up, w_down):
    unit, inv, query, key_value, probs, key_sides, middle, up = saved
    cot_middle, cot_mixed = feed_forward_back(cot, gains, middle, up, w_out, w_up, w_down)
    cot_query, cot_windows, pair_rows = [], [], []
    for p in range(4):
        rows, window = slice(p * QUAD, (p + 1) * QUAD), slice(p * SLOTS, (p + 1) * SLOTS)
        cot_q, cot_k, cot_v, pairs = [], [], [], []
        for g in range(2):
            lanes = slice(128 * g, 128 * g + 128)
            k = key_value[window, 128 * g : 128 * g + 128]
            v = key_value[window, WIDTH + 128 * g : WIDTH + 128 * g + 128]
            spread_dm = spread(cot_mixed[rows, lanes])
            soft = probs[p, g]
            weighted = soft.astype(F32) * mm_t(spread_dm, v)
            total = jnp.sum(weighted, axis=-1, keepdims=True)
            cot_scores = (weighted - soft.astype(F32) * total).astype(BF)
            both = mm(cot_scores, jnp.concatenate([k, key_sides[p]], axis=1))
            cot_q.append(head_lanes(both[:, :128]))
            pairs += [both[j * QUAD : (j + 1) * QUAD, 128:] for j in range(4)]
            cot_k.append(mm_left(cot_scores, spread(query[rows, lanes])))
            cot_v.append(mm_left(soft, spread_dm))
        cot_query.append(jnp.concatenate(cot_q, axis=1))
        cot_windows.append(
            jnp.concatenate([x * SCALE for x in cot_k] + cot_v, axis=1)
        )
        pair_rows.append(jnp.concatenate(pairs, axis=1))
    from_query = mm_t((jnp.concatenate(cot_query, axis=0) * SCALE).astype(BF), w_qkv[:, :WIDTH])
    cot_normed = mm_t(jnp.concatenate(cot_windows, axis=0).astype(BF), w_qkv[:, WIDTH:])
    spread_query, spread_middle = [], []
    for p in range(4):
        for source, target in ((from_query, spread_query), (cot_middle, spread_middle)):
            part = source[p * QUAD : (p + 1) * QUAD]
            target += [part if q == 3 - p else jnp.zeros_like(part) for q in range(4)]
    cot_normed = (cot_normed + jnp.concatenate(spread_query, axis=0)) * gains[0:1]
    cot_points = normalise_back(cot_normed, unit, inv) + jnp.concatenate(spread_middle, axis=0)
    pairs = mm(cells(place, False).astype(BF), jnp.concatenate(pair_rows, axis=0).astype(BF))
    per_head = [
        [pairs[e * PITCH : e * PITCH + SPAN, 128 * h : 128 * h + 128] for e in range(3)]
        for h in range(HEADS)
    ]
    return cot_points, table_sums(per_head)


def pack_kernel(
    features, occupancy, coords, grad_out, to_y, to_x, to_xy, occupied, place, arrived
):
    pairs = [(occupancy, occupied), (coords, place)]
    for quarter, target in ((2, to_y), (1, to_x), (0, to_xy)):
        pairs.append((features, target.at[0:SLOTS]))
        rows = slice(quarter * QUAD, (quarter + 1) * QUAD)
        pairs.append((grad_out.at[rows], target.at[SLOTS : SLOTS + QUAD]))
    copies = [
        pltpu.make_async_copy(source, target, arrived.at[i])
        for i, (source, target) in enumerate(pairs)
    ]
    for copy in copies:
        copy.start()
    copies[0].wait()
    copies[1].wait()
    meta = jnp.concatenate(
        [occupied[...]] + [place[e] for e in range(3)] + [jnp.zeros((4, SLOTS), jnp.int32)], axis=0
    ).astype(F32)
    meta = jnp.concatenate([meta, jnp.zeros((8, SLOTS), F32)], axis=0)
    meta = jnp.concatenate([meta, jnp.zeros((16, SLOTS), F32)], axis=1).astype(BF)
    for target in (to_y, to_x, to_xy):
        target[SLOTS + QUAD :] = meta
    for copy in copies[2:]:
        copy.wait()


def stage_kernel(*refs):
    count = (len(refs) - 2) // 2
    sources, targets, arrived = refs[1 : 1 + count], refs[1 + count : -1], refs[-1]
    copies = [
        pltpu.make_async_copy(source, target, arrived.at[i])
        for i, (source, target) in enumerate(zip(sources, targets))
    ]
    for copy in copies:
        copy.start()
    for copy in copies:
        copy.wait()


def main_kernel(
    features, occupancy, coords, grad_out, from_y, from_x, from_xy,
    gains, tables, w_qkv, w_out, w_up, w_down,
    own_cot, own_second, back_y, back_x, back_xy, tables_out,
):
    received = (from_y, from_x, from_xy)
    points = jnp.concatenate(
        [features[...]] + [part[0:SLOTS] for part in received], axis=0
    ).astype(F32)
    grad = jnp.concatenate(
        [grad_out[3 * QUAD :]] + [part[SLOTS : SLOTS + QUAD] for part in received], axis=0
    )
    metas = [
        jnp.concatenate(
            [occupancy[...]] + [coords[e] for e in range(3)] + [jnp.zeros((4, SLOTS), jnp.int32)],
            axis=0,
        )
    ] + [
        part[SLOTS + QUAD :].astype(F32)[0:8, 0:SLOTS].astype(jnp.int32) for part in received
    ]
    quarter = iota((8, SLOTS), 1) // QUAD
    meta = jnp.zeros((8, SLOTS), jnp.int32)
    for position, part in enumerate(metas):
        moved = pltpu.roll(part, (2 * position - 3) * QUAD % SLOTS, 1)
        meta = jnp.where(quarter == position, moved, meta)
    occupied, place = meta[0:1], meta[1:4]
    half = SPAN // 2
    shifted = jnp.concatenate(
        [(place[0:1] + half) % SPAN, (place[1:2] + half) % SPAN, place[2:3]], axis=0
    )
    column = jnp.transpose(jnp.broadcast_to(occupied.astype(F32), (SLOTS, SLOTS)))
    grad = grad * jnp.concatenate([column, column], axis=1).astype(BF)
    first_weights = (w_qkv.at[0], w_out.at[0], w_up.at[0], w_down.at[0])
    second_weights = (w_qkv.at[1], w_out.at[1], w_up.at[1], w_down.at[1])
    first_out, first_saved = halo_forward(
        points, [m[1:4] for m in metas], [m[0:1] for m in metas], place, gains[0], tables[0],
        *first_weights,
    )
    hidden = first_out.astype(F32)
    second, second_saved = block_forward(
        hidden, gains[1], shifted, occupied, tables[1], *second_weights
    )
    cot, second_table = block_backward(
        grad, hidden, gains[1], shifted, second_saved, *second_weights
    )
    cot_points, first_table = halo_backward(cot, place, gains[0], first_saved, *first_weights)
    own_cot[...] = cot_points[:SLOTS]
    own_second[...] = second[:QUAD]
    for position, target in enumerate((back_y, back_x, back_xy), 1):
        target[0:SLOTS] = cot_points[position * SLOTS : (position + 1) * SLOTS].astype(BF)
        target[SLOTS:] = second[position * QUAD : (position + 1) * QUAD]
    both = first_table + pltpu.roll(second_table, 3 * PITCH, 1)
    for i in range(tables_out.shape[0]):
        tables_out[i] = both


def gather_kernel(own_cot, own_second, home_y, home_x, home_xy, occupancy, out_points, grad_points):
    total = own_cot[...]
    for part in (home_y, home_x, home_xy):
        total = total + part[0:SLOTS].astype(F32)
    grad_points[...] = total.astype(BF)
    second = jnp.concatenate([part[SLOTS:] for part in (home_xy, home_x, home_y)] + [own_second[...]], axis=0)
    column = jnp.transpose(jnp.broadcast_to(occupancy[...].astype(F32), (SLOTS, SLOTS)))
    out_points[...] = second * jnp.concatenate([column, column], axis=1).astype(BF)


def unpack_kernel(parts, out):
    total = parts[0]
    for i in range(1, parts.shape[0]):
        total = total + parts[i]
    for k in range(2):
        for e in range(3):
            start = (3 * k + e) * PITCH
            moved = total if start == 0 else pltpu.roll(total, 128 - start, 1)
            out[k, e] = moved[:, : out.shape[-1]]


def call(kernel, shapes, *args, far=None, scratch=()):
    options = {}
    if far is not None:
        args = args[:far] + tuple(in_hbm(a) for a in args[far:])
        options["in_specs"] = [pl.BlockSpec(memory_space=pl.ANY)] * far + [
            pl.BlockSpec(memory_space=pltpu.HBM)
        ] * (len(args) - far)
    return pl.pallas_call(
        kernel,
        out_shape=[jax.ShapeDtypeStruct(s, d) for s, d in shapes],
        scratch_shapes=scratch,
        compiler_params=pltpu.CompilerParams(vmem_limit_bytes=VMEM_LIMIT),
        interpret=INTERPRET,
        **options,
    )(*args)


def in_hbm(value):
    return value if INTERPRET else pltpu.with_memory_space_constraint(value, pltpu.HBM)


def on_device(
    gx, gy, phases,
    features, occupancy, coords, norm_gains, bias_tables, w_qkv, w_out, w_up, w_down, grad_out,
):
    size_x = lax.axis_size(gx)
    size_y = lax.axis_size(gy)

    def move(value, step_x, step_y):
        pairs = []
        for i in range(size_x):
            for j in range(size_y):
                target = (i + step_x) % size_x * size_y + (j + step_y) % size_y
                pairs.append((i * size_y + j, target))
        return lax.ppermute(value, gx + gy, pairs)

    points, occupied, grad = features[0, 0], occupancy[0], grad_out[0, 0]
    place = jnp.swapaxes(coords[0], 0, 1)
    packet, reply = ((SLOTS + QUAD + 16, WIDTH), BF), ((SLOTS + QUAD, WIDTH), BF)
    to_y, to_x, to_xy = call(
        pack_kernel, [packet] * 3, points, occupied, place, grad, far=0,
        scratch=[pltpu.VMEM(occupied.shape, jnp.int32), pltpu.VMEM(place.shape, jnp.int32), pltpu.SemaphoreType.DMA((8,))],
    )
    sources = (points, occupied, place, grad, norm_gains, bias_tables, w_qkv, w_out, w_up, w_down)
    staged = call(
        stage_kernel, [(a.shape, a.dtype) for a in sources], to_y, *sources, far=1,
        scratch=[pltpu.SemaphoreType.DMA((len(sources),))],
    )
    first = lax.axis_size(phases[0])
    own_cot, own_second, back_y, back_x, back_xy, tables = call(
        main_kernel,
        [((SLOTS, WIDTH), F32), ((QUAD, WIDTH), BF)] + [reply] * 3 + [((first, HEADS, 128), F32)],
        *staged[:4], move(to_y, 0, -1), move(to_x, -1, 0), move(to_xy, -1, -1), *staged[4:],
    )
    home = move(back_y, 0, 1), move(back_x, 1, 0), move(back_xy, 1, 1)
    for phase, after in zip(phases, phases[1:] + (None,)):
        tables = lax.all_to_all(tables, phase, 0, 0)
        if after is not None:
            tables = jnp.broadcast_to(
                jnp.sum(tables, axis=0)[None], (lax.axis_size(after), HEADS, 128)
            )
    (grad_tables,) = call(unpack_kernel, [(bias_tables.shape, F32)], tables)
    out_points, grad_points = call(
        gather_kernel, [((SLOTS, WIDTH), BF)] * 2, own_cot, own_second, *home, staged[1]
    )
    return out_points[None, None], grad_points[None, None], grad_tables


def solution(mesh):
    shape = tuple(mesh.shape[a] for a in ("gx", "gy"))
    if shape == (16, 32):
        fine = Mesh(mesh.devices.reshape(2, 4, 2, 8, 4), ("zh", "y", "c", "zl", "x"))
        gx, gy = ("zh", "y", "c"), ("zl", "x")
        phases = (("y", "c", "x"), ("zh", "zl"))
    else:
        fine = Mesh(mesh.devices, ("gx", "gy"))
        gx, gy, phases = ("gx",), ("gy",), (("gx",), ("gy",))
    grid = P(gx, gy, None, None)
    return jax.shard_map(
        partial(on_device, gx, gy, phases),
        mesh=fine,
        in_specs=(grid, P(gx, gy, None), grid, P(), P(), P(), P(), P(), P(), grid),
        out_specs=(grid, grid, P()),
        check_vma=False,
    )
```

time: 104 us -> 103 us (level)
  the two profiles are of different devices: /device:TPU:1 before, /device:TPU:25 now
where the time goes in v2:
time: 103 us
  starting transfers between devices  55 us (53%)
  blocking collectives  16.6 us (16%)
  Pallas kernels  15 us (15%)
  waiting for transfers between devices  14.6 us (14%)
    ppermute x6, starting transfers between devices, move(): return lax.ppermute(value, gx + gy, pairs)  39.1 us
    all_to_all x1, blocking collectives, on_device(): tables = lax.all_to_all(tables, phase, 0, 0)  16.6 us
    all_to_all x1, starting transfers between devices, on_device(): tables = lax.all_to_all(tables, phase, 0, 0)  15.9 us
    pallas_call x5, Pallas kernels, call(): pl.pallas_call(kernel, out_shape=[jax.ShapeDtypeStruct(s, d) for s, d in...  15 us
    ppermute x6, waiting for transfers between devices, move(): return lax.ppermute(value, gx + gy, pairs)  14.6 us
  transfers between devices with their start and end apart: 7, of which 3 were waited for; matrix products, arithmetic and copies ran while one was open for 0% of the time, Pallas kernels for 3%

profile of v2, /device:TPU:25, one launch (start us, length us, event | category | flops | bytes accessed | tf_op | source)
XLA Modules:
  0.0 102.6 jit_solution(512301745238838744)
XLA Ops:
  0.6 1.1 %shard_map.121 = (bf16[176,256]{1,0:T(8,128)(2,1)S(1)}, bf16[176,256]{1,0:T(8,128)(2,1)S(1)}, bf16[176,256]{1,0:T(8,128)(2,1)S(1)}) custom-call(bf16[128,256]{1,0:T(8,128)(2,1)} %bitcast.6, s32[1,128]{1,0:T(1,128)} %bitcast.12, s32[3,1,128]{2,1,0:T(1,128)} %bitcast.10, bf16[128,256]{1,0:T(8,128)(2,1)} %bitcast.8), custom_call_target="tpu_custom_call" | custom-call | tf_op jit(solution)/shard_map/pallas_call | solution.py:433
  1.7 2.6 %collective-permute-start.1 = (bf16[176,256]{1,0:T(8,128)(2,1)S(1)}, bf16[176,256]{1,0:T(8,128)(2,1)S(1)}, u32[]{:S(2)}, u32[]{:S(2)}) collective-permute-start(bf16[176,256]{1,0:T(8,128)(2,1)S(1)} %get-tuple-element.29), channel_id=1, source_target_pairs={{0,480},{1,481},{2,482},{3,483},{4,484},{5,485},{6,486},{7,487},{8... | collective-permute-start | bytes 270344 | tf_op jit(solution)/shard_map/ppermute | solution.py:460
  4.3 15.1 %collective-permute-start.2 = (bf16[176,256]{1,0:T(8,128)(2,1)S(1)}, bf16[176,256]{1,0:T(8,128)(2,1)S(1)}, u32[]{:S(2)}, u32[]{:S(2)}) collective-permute-start(bf16[176,256]{1,0:T(8,128)(2,1)S(1)} %get-tuple-element.30), channel_id=1, source_target_pairs={{0,511},{1,480},{2,481},{3,482},{4,483},{5,484},{6,485},{7,486},{8... | collective-permute-start | bytes 270344 | tf_op jit(solution)/shard_map/ppermute | solution.py:460
  19.4 2.5 %collective-permute-start = (bf16[176,256]{1,0:T(8,128)(2,1)S(1)}, bf16[176,256]{1,0:T(8,128)(2,1)S(1)}, u32[]{:S(2)}, u32[]{:S(2)}) collective-permute-start(bf16[176,256]{1,0:T(8,128)(2,1)S(1)} %get-tuple-element.24.refs_0_), channel_id=1, source_target_pairs={{0,31},{1,0},{2,1},{3,2},{4,3},{5,4},{6,5},{7,6},{8,7},{9,8},{10,9... | collective-permute-start | bytes 270344 | tf_op jit(solution)/shard_map/ppermute | solution.py:460
  21.9 2.1 %shard_map.122 = (bf16[128,256]{1,0:T(8,128)(2,1)S(1)}, s32[1,128]{1,0:T(1,128)S(1)}, s32[3,1,128]{2,1,0:T(1,128)S(1)}, bf16[128,256]{1,0:T(8,128)(2,1)S(1)}, f3...) custom-call(bf16[176,256]{1,0:T(8,128)(2,1)S(1)} %get-tuple-element., ...), custom_call_target="tpu_custom_call" | custom-call | tf_op jit(solution)/shard_map/pallas_call | solution.py:433
  24.0 0.0 collective-permute-done.1.from_x
  24.0 0.0 collective-permute-done.2.from_xy
  24.0 0.7 collective-permute-done.from_y
  24.7 10.4 %shard_map.123 = (f32[128,256]{1,0:T(8,128)S(1)}, bf16[32,256]{1,0:T(8,128)(2,1)S(1)}, bf16[160,256]{1,0:T(8,128)(2,1)S(1)}, bf16[160,256]{1,0:T(8,128)(2,1)S(1)...) custom-call(bf16[128,256]{1,0:T(8,128)(2,1)S(1)} %get-tuple-element.25.features, ...), custom_call_target="tpu_custom_call" | custom-call | tf_op jit(solution)/shard_map/pallas_call | solution.py:433
  35.1 16.6 %all_to_all.10 = f32[32,8,128]{2,1,0:T(8,128)S(1)} all-to-all(f32[32,8,128]{2,1,0:T(8,128)S(1)} %get-tuple-element.44), channel_id=1, replica_groups=mesh['zh'=2,'y'=4,'c'=2,'zl'=8,'x'=4] {'y','c','x'}, dimensions={0} | all-to-all | bytes 262144 | tf_op jit(solution)/shard_map/all_to_all | solution.py:482
  51.7 0.6 broadcast_in_dim.14
  52.4 15.9 %all-to-all-start.1 = ((f32[16,8,128]{2,1,0:T(8,128)}), f32[16,8,128]{2,1,0:T(8,128)S(1)}, u32[]{:S(2)}, u32[]{:S(2)}) async-start(f32[16,8,128]{2,1,0:T(8,128)} %broadcast_in_dim.14), calls=%async_computation.1 | async-start | bytes 131072 | tf_op jit(solution)/shard_map/all_to_all | solution.py:482
  68.3 2.2 %collective-permute-start.3 = (bf16[160,256]{1,0:T(8,128)(2,1)S(1)}, bf16[160,256]{1,0:T(8,128)(2,1)S(1)}, u32[]{:S(2)}, u32[]{:S(2)}) collective-permute-start(bf16[160,256]{1,0:T(8,128)(2,1)S(1)} %get-tuple-element.39), channel_id=1, source_target_pairs={{0,1},{1,2},{2,3},{3,4},{4,5},{5,6},{6,7},{7,8},{8,9},{9,10},{10,1... | collective-permute-start | bytes 245768 | tf_op jit(solution)/shard_map/ppermute | solution.py:460
  70.5 14.5 %collective-permute-start.4 = (bf16[160,256]{1,0:T(8,128)(2,1)S(1)}, bf16[160,256]{1,0:T(8,128)(2,1)S(1)}, u32[]{:S(2)}, u32[]{:S(2)}) collective-permute-start(bf16[160,256]{1,0:T(8,128)(2,1)S(1)} %get-tuple-element.40), channel_id=1, source_target_pairs={{0,32},{1,33},{2,34},{3,35},{4,36},{5,37},{6,38},{7,39},{8,40},{9,... | collective-permute-start | bytes 245768 | tf_op jit(solution)/shard_map/ppermute | solution.py:460
  85.1 2.2 %collective-permute-start.5 = (bf16[160,256]{1,0:T(8,128)(2,1)S(1)}, bf16[160,256]{1,0:T(8,128)(2,1)S(1)}, u32[]{:S(2)}, u32[]{:S(2)}) collective-permute-start(bf16[160,256]{1,0:T(8,128)(2,1)S(1)} %get-tuple-element.41), channel_id=1, source_target_pairs={{0,33},{1,34},{2,35},{3,36},{4,37},{5,38},{6,39},{7,40},{8,41},{9,... | collective-permute-start | bytes 245768 | tf_op jit(solution)/shard_map/ppermute | solution.py:460
  87.2 0.0 collective-permute-done.3.home_y
  87.3 0.6 collective-permute-done.4.home_x
  87.8 13.3 %collective-permute-done.5.home_xy = bf16[160,256]{1,0:T(8,128)(2,1)S(1)} collective-permute-done((bf16[160,256]{1,0:T(8,128)(2,1)S(1)}, bf16[160,256]{1,0:T(8,128)(2,1)S(1)}, u32[]{:S(2)}, u32[]{:S(2)}) %collective-permute-start.5) | collective-permute-done | bytes 81952 | tf_op jit(solution)/shard_map/ppermute | solution.py:460
  101.2 0.7 shard_map.124
  101.9 0.0 all-to-all-done.1.parts
  101.9 0.7 shard_map.125
  (1 shorter events, 0.0 us)
Async XLA Ops:
  1.7 22.3 %collective-permute-start.1 = (bf16[176,256]{1,0:T(8,128)(2,1)S(1)}, bf16[176,256]{1,0:T(8,128)(2,1)S(1)}, u32[]{:S(2)}, u32[]{:S(2)}) collective-permute-start(bf16[176,256]{1,0:T(8,128)(2,1)S(1)} %get-tuple-element.29), channel_id=1, source_target_pairs={{0,480},{1,481},{2,482},{3,483},{4,484},{5,485},{6,486},{7,487},{8... | collective-permute-start | bytes 270344 | tf_op jit(solution)/shard_map/ppermute | solution.py:460
  4.3 19.7 %collective-permute-start.2 = (bf16[176,256]{1,0:T(8,128)(2,1)S(1)}, bf16[176,256]{1,0:T(8,128)(2,1)S(1)}, u32[]{:S(2)}, u32[]{:S(2)}) collective-permute-start(bf16[176,256]{1,0:T(8,128)(2,1)S(1)} %get-tuple-element.30), channel_id=1, source_target_pairs={{0,511},{1,480},{2,481},{3,482},{4,483},{5,484},{6,485},{7,486},{8... | collective-permute-start | bytes 270344 | tf_op jit(solution)/shard_map/ppermute | solution.py:460
  19.4 5.3 %collective-permute-start = (bf16[176,256]{1,0:T(8,128)(2,1)S(1)}, bf16[176,256]{1,0:T(8,128)(2,1)S(1)}, u32[]{:S(2)}, u32[]{:S(2)}) collective-permute-start(bf16[176,256]{1,0:T(8,128)(2,1)S(1)} %get-tuple-element.24.refs_0_), channel_id=1, source_target_pairs={{0,31},{1,0},{2,1},{3,2},{4,3},{5,4},{6,5},{7,6},{8,7},{9,8},{10,9... | collective-permute-start | bytes 270344 | tf_op jit(solution)/shard_map/ppermute | solution.py:460
  52.4 49.6 %all-to-all-start.1 = ((f32[16,8,128]{2,1,0:T(8,128)}), f32[16,8,128]{2,1,0:T(8,128)S(1)}, u32[]{:S(2)}, u32[]{:S(2)}) async-start(f32[16,8,128]{2,1,0:T(8,128)} %broadcast_in_dim.14), calls=%async_computation.1 | async-start | bytes 131072 | tf_op jit(solution)/shard_map/all_to_all | solution.py:482
  68.3 18.9 %collective-permute-start.3 = (bf16[160,256]{1,0:T(8,128)(2,1)S(1)}, bf16[160,256]{1,0:T(8,128)(2,1)S(1)}, u32[]{:S(2)}, u32[]{:S(2)}) collective-permute-start(bf16[160,256]{1,0:T(8,128)(2,1)S(1)} %get-tuple-element.39), channel_id=1, source_target_pairs={{0,1},{1,2},{2,3},{3,4},{4,5},{5,6},{6,7},{7,8},{8,9},{9,10},{10,1... | collective-permute-start | bytes 245768 | tf_op jit(solution)/shard_map/ppermute | solution.py:460
  70.5 17.3 %collective-permute-start.4 = (bf16[160,256]{1,0:T(8,128)(2,1)S(1)}, bf16[160,256]{1,0:T(8,128)(2,1)S(1)}, u32[]{:S(2)}, u32[]{:S(2)}) collective-permute-start(bf16[160,256]{1,0:T(8,128)(2,1)S(1)} %get-tuple-element.40), channel_id=1, source_target_pairs={{0,32},{1,33},{2,34},{3,35},{4,36},{5,37},{6,38},{7,39},{8,40},{9,... | collective-permute-start | bytes 245768 | tf_op jit(solution)/shard_map/ppermute | solution.py:460
  85.1 16.1 %collective-permute-start.5 = (bf16[160,256]{1,0:T(8,128)(2,1)S(1)}, bf16[160,256]{1,0:T(8,128)(2,1)S(1)}, u32[]{:S(2)}, u32[]{:S(2)}) collective-permute-start(bf16[160,256]{1,0:T(8,128)(2,1)S(1)} %get-tuple-element.41), channel_id=1, source_target_pairs={{0,33},{1,34},{2,35},{3,36},{4,37},{5,38},{6,39},{7,40},{8,41},{9,... | collective-permute-start | bytes 245768 | tf_op jit(solution)/shard_map/ppermute | solution.py:460

commit v3 on v2

--- a/solution.py
+++ b/solution.py
@@ -25,10 +25,6 @@
 
 def mm_t(a, b):
     return lax.dot_general(a, b, (((1,), (1,)), ((), ())), preferred_element_type=F32)
-
-
-def mm_left(a, b):
-    return lax.dot_general(a, b, (((0,), (0,)), ((), ())), preferred_element_type=F32)
 
 
 def iota(shape, axis):
@@ -175,7 +171,7 @@
     return jnp.concatenate(tables, axis=0)
 
 
-def block_backward(cot, hidden, gains, coords, saved, w_qkv, w_out, w_up, w_down):
+def block_backward(cot, hidden, gains, coords, saved, w_qkv, w_out, w_up, w_down, with_table=True):
     projected, probs, middle, up = saved
     cot_middle, cot_mixed = feed_forward_back(cot, gains, middle, up, w_out, w_up, w_down)
     cells_t = cells(coords, False).astype(BF)
@@ -199,7 +195,8 @@
         for j in range(4):
             rows = slice(j * SLOTS, (j + 1) * SLOTS)
             lanes = slice(j * HD, (j + 1) * HD)
-            both = mm(jnp.concatenate([q_t[lanes], cells_t], axis=0), cot_scores[rows])
+            left = jnp.concatenate([q_t[lanes], cells_t], axis=0) if with_table else q_t[lanes]
+            both = mm(left, cot_scores[rows])
             k_rows.append(both[:HD])
             pair_sums.append(both[HD:])
             v_rows.append(mm(dm_t[lanes], soft[rows]))
@@ -209,6 +206,8 @@
     cot_normed = mm_t(cot_projected, w_qkv[...]) * gains[0:1]
     unit, inv = normalise(hidden)
     cot_hidden = cot_middle + normalise_back(cot_normed, unit, inv)
+    if not with_table:
+        return cot_hidden.astype(BF), None
     pairs = mm(jnp.concatenate(pair_sums, axis=0).astype(BF), cells_key)
     per_head = [
         [pairs[(3 * h + e) * PITCH : (3 * h + e) * PITCH + SPAN] for e in range(3)]
@@ -227,7 +226,7 @@
 
 
 def halo_forward(points, places, occupieds, place, gains, table, w_qkv, w_out, w_up, w_down):
-    unit, inv = normalise(points)
+    unit, _ = normalise(points)
     normed = (unit * gains[0:1]).astype(BF)
     key_value = mm(normed, w_qkv[:, WIDTH:]).astype(BF)
     quarters = [slice(p * SLOTS + (3 - p) * QUAD, p * SLOTS + (4 - p) * QUAD) for p in range(4)]
@@ -260,50 +259,31 @@
     up = mm((unit_two * gains[1:2]).astype(BF), w_up[...])
     expanded, _ = gelu_parts(up)
     out = middle + mm(expanded.astype(BF), w_down[...])
-    return out.astype(BF), (unit, inv, query, key_value, probs, key_sides, middle, up)
-
-
-def halo_backward(cot, place, gains, saved, w_qkv, w_out, w_up, w_down):
-    unit, inv, query, key_value, probs, key_sides, middle, up = saved
-    cot_middle, cot_mixed = feed_forward_back(cot, gains, middle, up, w_out, w_up, w_down)
-    cot_query, cot_windows, pair_rows = [], [], []
+    return out.astype(BF), (key_value, probs, key_sides, middle, up)
+
+
+def halo_table(cot, place, gains, saved, w_out, w_up, w_down):
+    key_value, probs, key_sides, middle, up = saved
+    _, cot_mixed = feed_forward_back(cot, gains, middle, up, w_out, w_up, w_down)
+    pair_rows = []
     for p in range(4):
         rows, window = slice(p * QUAD, (p + 1) * QUAD), slice(p * SLOTS, (p + 1) * SLOTS)
-        cot_q, cot_k, cot_v, pairs = [], [], [], []
+        pairs = []
         for g in range(2):
-            lanes = slice(128 * g, 128 * g + 128)
-            k = key_value[window, 128 * g : 128 * g + 128]
             v = key_value[window, WIDTH + 128 * g : WIDTH + 128 * g + 128]
-            spread_dm = spread(cot_mixed[rows, lanes])
-            soft = probs[p, g]
-            weighted = soft.astype(F32) * mm_t(spread_dm, v)
+            soft = probs[p, g].astype(F32)
+            weighted = soft * mm_t(spread(cot_mixed[rows, 128 * g : 128 * g + 128]), v)
             total = jnp.sum(weighted, axis=-1, keepdims=True)
-            cot_scores = (weighted - soft.astype(F32) * total).astype(BF)
-            both = mm(cot_scores, jnp.concatenate([k, key_sides[p]], axis=1))
-            cot_q.append(head_lanes(both[:, :128]))
-            pairs += [both[j * QUAD : (j + 1) * QUAD, 128:] for j in range(4)]
-            cot_k.append(mm_left(cot_scores, spread(query[rows, lanes])))
-            cot_v.append(mm_left(soft, spread_dm))
-        cot_query.append(jnp.concatenate(cot_q, axis=1))
-        cot_windows.append(
-            jnp.concatenate([x * SCALE for x in cot_k] + cot_v, axis=1)
-        )
+            both = mm((weighted - soft * total).astype(BF), key_sides[p])
+            pairs += [both[j * QUAD : (j + 1) * QUAD] for j in range(4)]
         pair_rows.append(jnp.concatenate(pairs, axis=1))
-    from_query = mm_t((jnp.concatenate(cot_query, axis=0) * SCALE).astype(BF), w_qkv[:, :WIDTH])
-    cot_normed = mm_t(jnp.concatenate(cot_windows, axis=0).astype(BF), w_qkv[:, WIDTH:])
-    spread_query, spread_middle = [], []
-    for p in range(4):
-        for source, target in ((from_query, spread_query), (cot_middle, spread_middle)):
-            part = source[p * QUAD : (p + 1) * QUAD]
-            target += [part if q == 3 - p else jnp.zeros_like(part) for q in range(4)]
-    cot_normed = (cot_normed + jnp.concatenate(spread_query, axis=0)) * gains[0:1]
-    cot_points = normalise_back(cot_normed, unit, inv) + jnp.concatenate(spread_middle, axis=0)
     pairs = mm(cells(place, False).astype(BF), jnp.concatenate(pair_rows, axis=0).astype(BF))
-    per_head = [
-        [pairs[e * PITCH : e * PITCH + SPAN, 128 * h : 128 * h + 128] for e in range(3)]
-        for h in range(HEADS)
-    ]
-    return cot_points, table_sums(per_head)
+    return table_sums(
+        [
+            [pairs[e * PITCH : e * PITCH + SPAN, 128 * h : 128 * h + 128] for e in range(3)]
+            for h in range(HEADS)
+        ]
+    )
 
 
 def pack_kernel(
@@ -349,7 +329,7 @@
 def main_kernel(
     features, occupancy, coords, grad_out, from_y, from_x, from_xy,
     gains, tables, w_qkv, w_out, w_up, w_down,
-    own_cot, own_second, back_y, back_x, back_xy, tables_out,
+    own, back_y, back_x, back_xy, tables_out,
 ):
     received = (from_y, from_x, from_xy)
     points = jnp.concatenate(
@@ -391,31 +371,38 @@
     cot, second_table = block_backward(
         grad, hidden, gains[1], shifted, second_saved, *second_weights
     )
-    cot_points, first_table = halo_backward(cot, place, gains[0], first_saved, *first_weights)
-    own_cot[...] = cot_points[:SLOTS]
-    own_second[...] = second[:QUAD]
-    for position, target in enumerate((back_y, back_x, back_xy), 1):
-        target[0:SLOTS] = cot_points[position * SLOTS : (position + 1) * SLOTS].astype(BF)
-        target[SLOTS:] = second[position * QUAD : (position + 1) * QUAD]
+    first_table = halo_table(cot, place, gains[0], first_saved, *first_weights[1:])
+    for position, target in enumerate((own, back_y, back_x, back_xy)):
+        rows = slice(position * QUAD, (position + 1) * QUAD)
+        target[0:QUAD] = second[rows]
+        target[QUAD:] = cot[rows]
     both = first_table + pltpu.roll(second_table, 3 * PITCH, 1)
     for i in range(tables_out.shape[0]):
-        tables_out[i] = both
-
-
-def gather_kernel(own_cot, own_second, home_y, home_x, home_xy, occupancy, out_points, grad_points):
-    total = own_cot[...]
-    for part in (home_y, home_x, home_xy):
-        total = total + part[0:SLOTS].astype(F32)
-    grad_points[...] = total.astype(BF)
-    second = jnp.concatenate([part[SLOTS:] for part in (home_xy, home_x, home_y)] + [own_second[...]], axis=0)
+        tables_out[i] = both.astype(BF)
+
+
+def window_kernel(
+    home_xy, home_x, home_y, own, features, occupancy, coords,
+    gains, tables, w_qkv, w_out, w_up, w_down, out_points, grad_points,
+):
+    parts = (home_xy, home_x, home_y, own)
+    second = jnp.concatenate([part[0:QUAD] for part in parts], axis=0)
+    cot = jnp.concatenate([part[QUAD:] for part in parts], axis=0)
     column = jnp.transpose(jnp.broadcast_to(occupancy[...].astype(F32), (SLOTS, SLOTS)))
     out_points[...] = second * jnp.concatenate([column, column], axis=1).astype(BF)
+    place = jnp.concatenate([coords[e] for e in range(3)], axis=0)
+    weights = (w_qkv.at[0], w_out.at[0], w_up.at[0], w_down.at[0])
+    points = features[...].astype(F32)
+    _, saved = block_forward(points, gains[0], place, occupancy[...], tables[0], *weights)
+    grad_points[...], _ = block_backward(
+        cot, points, gains[0], place, saved, *weights, with_table=False
+    )
 
 
 def unpack_kernel(parts, out):
-    total = parts[0]
+    total = parts[0].astype(F32)
     for i in range(1, parts.shape[0]):
-        total = total + parts[i]
+        total = total + parts[i].astype(F32)
     for k in range(2):
         for e in range(3):
             start = (3 * k + e) * PITCH
@@ -461,7 +448,7 @@
 
     points, occupied, grad = features[0, 0], occupancy[0], grad_out[0, 0]
     place = jnp.swapaxes(coords[0], 0, 1)
-    packet, reply = ((SLOTS + QUAD + 16, WIDTH), BF), ((SLOTS + QUAD, WIDTH), BF)
+    packet, reply = ((SLOTS + QUAD + 16, WIDTH), BF), ((2 * QUAD, WIDTH), BF)
     to_y, to_x, to_xy = call(
         pack_kernel, [packet] * 3, points, occupied, place, grad, far=0,
         scratch=[pltpu.VMEM(occupied.shape, jnp.int32), pltpu.VMEM(place.shape, jnp.int32), pltpu.SemaphoreType.DMA((8,))],
@@ -472,21 +459,21 @@
         scratch=[pltpu.SemaphoreType.DMA((len(sources),))],
     )
     first = lax.axis_size(phases[0])
-    own_cot, own_second, back_y, back_x, back_xy, tables = call(
+    own, back_y, back_x, back_xy, tables = call(
         main_kernel,
-        [((SLOTS, WIDTH), F32), ((QUAD, WIDTH), BF)] + [reply] * 3 + [((first, HEADS, 128), F32)],
+        [reply] * 4 + [((first, HEADS, 128), BF)],
         *staged[:4], move(to_y, 0, -1), move(to_x, -1, 0), move(to_xy, -1, -1), *staged[4:],
     )
-    home = move(back_y, 0, 1), move(back_x, 1, 0), move(back_xy, 1, 1)
-    for phase, after in zip(phases, phases[1:] + (None,)):
-        tables = lax.all_to_all(tables, phase, 0, 0)
-        if after is not None:
-            tables = jnp.broadcast_to(
-                jnp.sum(tables, axis=0)[None], (lax.axis_size(after), HEADS, 128)
-            )
+    home_y = move(back_y, 0, 1)
+    home_x = move(back_x, 1, 0)
+    home_xy = move(back_xy, 1, 1)
+    tables = lax.all_to_all(tables, phases[0], 0, 0)
+    total = jnp.sum(tables.astype(F32), axis=0).astype(BF)
+    tables = jnp.broadcast_to(total[None], (lax.axis_size(phases[1]), HEADS, 128))
+    tables = lax.all_to_all(tables, phases[1], 0, 0)
     (grad_tables,) = call(unpack_kernel, [(bias_tables.shape, F32)], tables)
     out_points, grad_points = call(
-        gather_kernel, [((SLOTS, WIDTH), BF)] * 2, own_cot, own_second, *home, staged[1]
+        window_kernel, [((SLOTS, WIDTH), BF)] * 2, home_xy, home_x, home_y, own, *staged[:3], *staged[4:]
     )
     return out_points[None, None], grad_points[None, None], grad_tables
 

time: 103 us -> 103 us (level)
  the two profiles are of different devices: /device:TPU:25 before, /device:TPU:24 now
where the time goes in v3:
time: 103 us
  starting transfers between devices  55.2 us (54%)
  Pallas kernels  17.7 us (17%)
  blocking collectives  15 us (15%)
  waiting for transfers between devices  13.5 us (13%)
    ppermute x6, starting transfers between devices, move(): return lax.ppermute(value, gx + gy, pairs)  39 us
    pallas_call x5, Pallas kernels, call(): pl.pallas_call(kernel, out_shape=[jax.ShapeDtypeStruct(s, d) for s, d in...  17.7 us
    all_to_all x1, starting transfers between devices, on_device(): tables = lax.all_to_all(tables, phases[1], 0, 0)  16.3 us
    all_to_all x1, blocking collectives, on_device(): tables = lax.all_to_all(tables, phases[0], 0, 0)  15 us
    ppermute x6, waiting for transfers between devices, move(): return lax.ppermute(value, gx + gy, pairs)  13.4 us
  transfers between devices with their start and end apart: 7, of which 2 were waited for; matrix products, arithmetic and copies ran while one was open for 0% of the time, Pallas kernels for 6%

profile of v3, /device:TPU:24, one launch (start us, length us, event | category | flops | bytes accessed | tf_op | source)
XLA Modules:
  0.0 102.8 jit_solution(5944699908842095394)
XLA Ops:
  0.6 1.1 %shard_map.121 = (bf16[176,256]{1,0:T(8,128)(2,1)S(1)}, bf16[176,256]{1,0:T(8,128)(2,1)S(1)}, bf16[176,256]{1,0:T(8,128)(2,1)S(1)}) custom-call(bf16[128,256]{1,0:T(8,128)(2,1)} %bitcast.6, s32[1,128]{1,0:T(1,128)} %bitcast.12, s32[3,1,128]{2,1,0:T(1,128)} %bitcast.10, bf16[128,256]{1,0:T(8,128)(2,1)} %bitcast.8), custom_call_target="tpu_custom_call" | custom-call | tf_op jit(solution)/shard_map/pallas_call | solution.py:420
  1.7 2.1 %collective-permute-start.1 = (bf16[176,256]{1,0:T(8,128)(2,1)S(1)}, bf16[176,256]{1,0:T(8,128)(2,1)S(1)}, u32[]{:S(2)}, u32[]{:S(2)}) collective-permute-start(bf16[176,256]{1,0:T(8,128)(2,1)S(1)} %get-tuple-element.28), channel_id=1, source_target_pairs={{0,480},{1,481},{2,482},{3,483},{4,484},{5,485},{6,486},{7,487},{8... | collective-permute-start | bytes 270344 | tf_op jit(solution)/shard_map/ppermute | solution.py:447
  3.8 15.5 %collective-permute-start.2 = (bf16[176,256]{1,0:T(8,128)(2,1)S(1)}, bf16[176,256]{1,0:T(8,128)(2,1)S(1)}, u32[]{:S(2)}, u32[]{:S(2)}) collective-permute-start(bf16[176,256]{1,0:T(8,128)(2,1)S(1)} %get-tuple-element.29), channel_id=1, source_target_pairs={{0,511},{1,480},{2,481},{3,482},{4,483},{5,484},{6,485},{7,486},{8... | collective-permute-start | bytes 270344 | tf_op jit(solution)/shard_map/ppermute | solution.py:447
  19.3 2.7 %collective-permute-start = (bf16[176,256]{1,0:T(8,128)(2,1)S(1)}, bf16[176,256]{1,0:T(8,128)(2,1)S(1)}, u32[]{:S(2)}, u32[]{:S(2)}) collective-permute-start(bf16[176,256]{1,0:T(8,128)(2,1)S(1)} %get-tuple-element.23.refs_0_), channel_id=1, source_target_pairs={{0,31},{1,0},{2,1},{3,2},{4,3},{5,4},{6,5},{7,6},{8,7},{9,8},{10,9... | collective-permute-start | bytes 270344 | tf_op jit(solution)/shard_map/ppermute | solution.py:447
  22.0 2.1 %shard_map.122 = (bf16[128,256]{1,0:T(8,128)(2,1)S(1)}, s32[1,128]{1,0:T(1,128)S(1)}, s32[3,1,128]{2,1,0:T(1,128)S(1)}, bf16[128,256]{1,0:T(8,128)(2,1)S(1)}, f3...) custom-call(bf16[176,256]{1,0:T(8,128)(2,1)S(1)} %get-tuple-element., ...), custom_call_target="tpu_custom_call" | custom-call | tf_op jit(solution)/shard_map/pallas_call | solution.py:420
  24.1 0.0 collective-permute-done.1.from_x
  24.1 0.0 collective-permute-done.2.from_xy
  24.2 1.5 %collective-permute-done.from_y = bf16[176,256]{1,0:T(8,128)(2,1)S(1)} collective-permute-done((bf16[176,256]{1,0:T(8,128)(2,1)S(1)}, bf16[176,256]{1,0:T(8,128)(2,1)S(1)}, u32[]{:S(2)}, u32[]{:S(2)}) %collective-permute-start) | collective-permute-done | bytes 90144 | tf_op jit(solution)/shard_map/ppermute | solution.py:447
  25.7 9.5 %shard_map.123 = (bf16[64,256]{1,0:T(8,128)(2,1)S(1)}, bf16[64,256]{1,0:T(8,128)(2,1)S(1)}, bf16[64,256]{1,0:T(8,128)(2,1)S(1)}, bf16[64,256]{1,0:T(8,128)(2,1)S(1)}, bf16[32,8,128]{2,1,0:T(8,128)(2,1)S(1)}) custom-call(bf16[128,256]{1,0:T(8,128)(2,1)S(1)} %get-tuple-element.24.features, s32[1,128]{1,0:T(1,128)S(1)} %get-tuple-element.25.occupancy, ...), custom_call_target="tpu_custom_call" | custom-call | tf_op jit(solution)/shard_map/pallas_call | solution.py:420
  35.2 15.0 %all_to_all.10 = bf16[32,8,128]{2,1,0:T(8,128)(2,1)S(1)} all-to-all(bf16[32,8,128]{2,1,0:T(8,128)(2,1)S(1)} %get-tuple-element.42), channel_id=1, replica_groups=mesh['zh'=2,'y'=4,'c'=2,'zl'=8,'x'=4] {'y','c','x'}, dimensions={0} | all-to-all | bytes 131072 | tf_op jit(solution)/shard_map/all_to_all | solution.py:470
  50.2 0.6 broadcast_in_dim.14
  50.8 16.3 %all-to-all-start.1 = ((bf16[16,8,128]{2,1,0:T(8,128)(2,1)}), bf16[16,8,128]{2,1,0:T(8,128)(2,1)S(1)}, u32[]{:S(2)}, u32[]{:S(2)}) async-start(bf16[16,8,128]{2,1,0:T(8,128)(2,1)} %broadcast_in_dim.14), calls=%async_computation.1 | async-start | bytes 65536 | tf_op jit(solution)/shard_map/all_to_all | solution.py:473
  67.1 1.9 %collective-permute-start.3 = (bf16[64,256]{1,0:T(8,128)(2,1)S(1)}, bf16[64,256]{1,0:T(8,128)(2,1)S(1)}, u32[]{:S(2)}, u32[]{:S(2)}) collective-permute-start(bf16[64,256]{1,0:T(8,128)(2,1)S(1)} %get-tuple-element.36), channel_id=1, source_target_pairs={{0,33},{1,34},{2,35},{3,36},{4,37},{5,38},{6,39},{7,40},{8,41},{9,... | collective-permute-start | bytes 98312 | tf_op jit(solution)/shard_map/ppermute | solution.py:447
  69.0 14.2 %collective-permute-start.4 = (bf16[64,256]{1,0:T(8,128)(2,1)S(1)}, bf16[64,256]{1,0:T(8,128)(2,1)S(1)}, u32[]{:S(2)}, u32[]{:S(2)}) collective-permute-start(bf16[64,256]{1,0:T(8,128)(2,1)S(1)} %get-tuple-element.37), channel_id=1, source_target_pairs={{0,32},{1,33},{2,34},{3,35},{4,36},{5,37},{6,38},{7,39},{8,40},{9,... | collective-permute-start | bytes 98312 | tf_op jit(solution)/shard_map/ppermute | solution.py:447
  83.2 2.6 %collective-permute-start.5 = (bf16[64,256]{1,0:T(8,128)(2,1)S(1)}, bf16[64,256]{1,0:T(8,128)(2,1)S(1)}, u32[]{:S(2)}, u32[]{:S(2)}) collective-permute-start(bf16[64,256]{1,0:T(8,128)(2,1)S(1)} %get-tuple-element.38), channel_id=1, source_target_pairs={{0,1},{1,2},{2,3},{3,4},{4,5},{5,6},{6,7},{7,8},{8,9},{9,10},{10,1... | collective-permute-start | bytes 98312 | tf_op jit(solution)/shard_map/ppermute | solution.py:447
  85.8 0.0 collective-permute-done.3.home_xy
  85.8 0.0 collective-permute-done.4.home_x
  85.8 11.9 %collective-permute-done.5.home_y = bf16[64,256]{1,0:T(8,128)(2,1)S(1)} collective-permute-done((bf16[64,256]{1,0:T(8,128)(2,1)S(1)}, bf16[64,256]{1,0:T(8,128)(2,1)S(1)}, u32[]{:S(2)}, u32[]{:S(2)}) %collective-permute-start.5) | collective-permute-done | bytes 32800 | tf_op jit(solution)/shard_map/ppermute | solution.py:447
  97.7 4.4 %shard_map.124 = (bf16[128,256]{1,0:T(8,128)(2,1)}, bf16[128,256]{1,0:T(8,128)(2,1)}) custom-call(bf16[64,256]{1,0:T(8,128)(2,1)S(1)} %collective-permute-done.3.home_xy, bf16[64,256]{1,0:T(8,128)(2,1)S(1)} %collective-permute-done.4.home_x, bf16[64,256]{1,0:T(8,128)(2,1)S(1)} %collective-permute-done.5.home_y, bf16[64,256]{1,0:T(8,128)(2,1)S(1)} %get-tuple-element.39.own, ...), custom_call_target="tpu_custom_call" | custom-call | tf_op jit(solution)/shard_map/pallas_call | solution.py:420
  102.1 0.0 all-to-all-done.1.parts
  102.1 0.7 shard_map.125
  (1 shorter events, 0.0 us)
Async XLA Ops:
  1.7 22.4 %collective-permute-start.1 = (bf16[176,256]{1,0:T(8,128)(2,1)S(1)}, bf16[176,256]{1,0:T(8,128)(2,1)S(1)}, u32[]{:S(2)}, u32[]{:S(2)}) collective-permute-start(bf16[176,256]{1,0:T(8,128)(2,1)S(1)} %get-tuple-element.28), channel_id=1, source_target_pairs={{0,480},{1,481},{2,482},{3,483},{4,484},{5,485},{6,486},{7,487},{8... | collective-permute-start | bytes 270344 | tf_op jit(solution)/shard_map/ppermute | solution.py:447
  3.8 20.3 %collective-permute-start.2 = (bf16[176,256]{1,0:T(8,128)(2,1)S(1)}, bf16[176,256]{1,0:T(8,128)(2,1)S(1)}, u32[]{:S(2)}, u32[]{:S(2)}) collective-permute-start(bf16[176,256]{1,0:T(8,128)(2,1)S(1)} %get-tuple-element.29), channel_id=1, source_target_pairs={{0,511},{1,480},{2,481},{3,482},{4,483},{5,484},{6,485},{7,486},{8... | collective-permute-start | bytes 270344 | tf_op jit(solution)/shard_map/ppermute | solution.py:447
  19.3 6.4 %collective-permute-start = (bf16[176,256]{1,0:T(8,128)(2,1)S(1)}, bf16[176,256]{1,0:T(8,128)(2,1)S(1)}, u32[]{:S(2)}, u32[]{:S(2)}) collective-permute-start(bf16[176,256]{1,0:T(8,128)(2,1)S(1)} %get-tuple-element.23.refs_0_), channel_id=1, source_target_pairs={{0,31},{1,0},{2,1},{3,2},{4,3},{5,4},{6,5},{7,6},{8,7},{9,8},{10,9... | collective-permute-start | bytes 270344 | tf_op jit(solution)/shard_map/ppermute | solution.py:447
  50.8 51.3 %all-to-all-start.1 = ((bf16[16,8,128]{2,1,0:T(8,128)(2,1)}), bf16[16,8,128]{2,1,0:T(8,128)(2,1)S(1)}, u32[]{:S(2)}, u32[]{:S(2)}) async-start(bf16[16,8,128]{2,1,0:T(8,128)(2,1)} %broadcast_in_dim.14), calls=%async_computation.1 | async-start | bytes 65536 | tf_op jit(solution)/shard_map/all_to_all | solution.py:473
  67.1 18.7 %collective-permute-start.3 = (bf16[64,256]{1,0:T(8,128)(2,1)S(1)}, bf16[64,256]{1,0:T(8,128)(2,1)S(1)}, u32[]{:S(2)}, u32[]{:S(2)}) collective-permute-start(bf16[64,256]{1,0:T(8,128)(2,1)S(1)} %get-tuple-element.36), channel_id=1, source_target_pairs={{0,33},{1,34},{2,35},{3,36},{4,37},{5,38},{6,39},{7,40},{8,41},{9,... | collective-permute-start | bytes 98312 | tf_op jit(solution)/shard_map/ppermute | solution.py:447
  69.0 16.8 %collective-permute-start.4 = (bf16[64,256]{1,0:T(8,128)(2,1)S(1)}, bf16[64,256]{1,0:T(8,128)(2,1)S(1)}, u32[]{:S(2)}, u32[]{:S(2)}) collective-permute-start(bf16[64,256]{1,0:T(8,128)(2,1)S(1)} %get-tuple-element.37), channel_id=1, source_target_pairs={{0,32},{1,33},{2,34},{3,35},{4,36},{5,37},{6,38},{7,39},{8,40},{9,... | collective-permute-start | bytes 98312 | tf_op jit(solution)/shard_map/ppermute | solution.py:447
  83.2 14.5 %collective-permute-start.5 = (bf16[64,256]{1,0:T(8,128)(2,1)S(1)}, bf16[64,256]{1,0:T(8,128)(2,1)S(1)}, u32[]{:S(2)}, u32[]{:S(2)}) collective-permute-start(bf16[64,256]{1,0:T(8,128)(2,1)S(1)} %get-tuple-element.38), channel_id=1, source_target_pairs={{0,1},{1,2},{2,3},{3,4},{4,5},{5,6},{6,7},{7,8},{8,9},{9,10},{10,1... | collective-permute-start | bytes 98312 | tf_op jit(solution)/shard_map/ppermute | solution.py:447

commit v4 on v3

--- a/solution.py
+++ b/solution.py
@@ -16,6 +16,7 @@
 SPAN, PITCH = 8, 16
 SCALE = HD ** (-0.5)
 MASKED = -1e30
+COST = 10_000_000_000
 VMEM_LIMIT = 24 * 1024 * 1024
 
 
@@ -107,54 +108,65 @@
     return jnp.concatenate([stack[j * SLOTS : (j + 1) * SLOTS] for j in range(4)], axis=1)
 
 
-def softmax(scores):
-    weights = jnp.exp((scores - jnp.max(scores, axis=-1, keepdims=True)) * SCALE)
-    return (weights * (1.0 / jnp.sum(weights, axis=-1, keepdims=True))).astype(BF)
-
-
-def gelu_parts(v):
+def attend(scores, values):
+    tops = [jnp.max(x, axis=-1, keepdims=True) for x in scores]
+    factor = SCALE * 1.4426950408889634
+    weights = [jnp.exp2((x - top) * factor) for x, top in zip(scores, tops)]
+    ones = jnp.ones_like(values[0])
+    both = [mm(w.astype(BF), jnp.concatenate([v, ones], axis=1)) for w, v in zip(weights, values)]
+    shares = [1.0 / x[:, 128:] for x in both]
+    return (
+        [w * share for w, share in zip(weights, shares)],
+        [head_lanes(x[:, :128] * share) for x, share in zip(both, shares)],
+    )
+
+
+def attend_back(soft, mixed, cot_mixed, v):
+    product = mixed * cot_mixed.astype(F32)
+    high = product.astype(BF)
+    low = (product - high.astype(F32)).astype(BF)
+    ones = jnp.ones_like(v)
+    left = jnp.concatenate([spread(cot_mixed), spread(-high), spread(-low)], axis=1)
+    return (soft * mm_t(left, jnp.concatenate([v, ones, ones], axis=1))).astype(BF)
+
+
+def gelu_and_slope(v):
     c = 0.7978845608028654
-    t = jnp.tanh(c * (v + 0.044715 * (v * v * v)))
-    return 0.5 * v * (1.0 + t), t
-
-
-def gelu_slope(v):
-    c = 0.7978845608028654
-    t = jnp.tanh(c * (v + 0.044715 * (v * v * v)))
-    return 0.5 * (1.0 + t) + 0.5 * v * (1.0 - t * t) * c * (1.0 + 3 * 0.044715 * (v * v))
+    square = v * v
+    t = jnp.tanh(v * (c + (c * 0.044715) * square))
+    half = 0.5 + 0.5 * t
+    return v * half, half + (0.5 * v) * (1.0 - t * t) * (c + (3 * c * 0.044715) * square)
 
 
 def block_forward(hidden, gains, coords, occupied, table, w_qkv, w_out, w_up, w_down):
-    unit, _ = normalise(hidden)
+    unit, inv = normalise(hidden)
     projected = mm((unit * gains[0:1]).astype(BF), w_qkv[...]).astype(BF)
     query_side = jnp.transpose(query_cells(coords)).astype(BF)
     key_side = jnp.transpose(key_cells(coords, occupied)).astype(BF)
     bias_left = mm(query_side, table_matrix(table)).astype(BF)
-    probs, mixed = [], []
+    scores, values = [], []
     for g in range(2):
         q = projected[:, 128 * g : 128 * g + 128]
         k = projected[:, 256 + 128 * g : 256 + 128 * g + 128]
-        v = projected[:, 512 + 128 * g : 512 + 128 * g + 128]
+        values.append(projected[:, 512 + 128 * g : 512 + 128 * g + 128])
         lefts = jnp.concatenate(
             [bias_left[:, 128 * h : 128 * h + 128] for h in range(4 * g, 4 * g + 4)], axis=0
         )
-        scores = mm_t(
-            jnp.concatenate([spread(q), lefts], axis=1), jnp.concatenate([k, key_side], axis=1)
+        scores.append(
+            mm_t(jnp.concatenate([spread(q), lefts], axis=1), jnp.concatenate([k, key_side], axis=1))
         )
-        soft = softmax(scores)
-        probs.append(soft)
-        mixed.append(mm(side_by_side(soft), spread(v)))
-    middle = hidden + mm(jnp.concatenate(mixed, axis=1).astype(BF), w_out[...])
-    unit_two, _ = normalise(middle)
+    probs, mixed = attend(scores, values)
+    mixed = jnp.concatenate(mixed, axis=1)
+    middle = hidden + mm(mixed.astype(BF), w_out[...])
+    unit_two, inv_two = normalise(middle)
     up = mm((unit_two * gains[1:2]).astype(BF), w_up[...])
-    expanded, _ = gelu_parts(up)
+    expanded, slope = gelu_and_slope(up)
     out = middle + mm(expanded.astype(BF), w_down[...])
-    return out.astype(BF), (projected, probs, middle, up)
-
-
-def feed_forward_back(cot, gains, middle, up, w_out, w_up, w_down):
-    unit, inv = normalise(middle)
-    cot_up = mm_t(cot, w_down[...]) * gelu_slope(up)
+    return out.astype(BF), (projected, probs, mixed, unit, inv, unit_two, inv_two, slope)
+
+
+def feed_forward_back(cot, gains, unit, inv, slope, w_out, w_up, w_down):
+    cot_up = mm_t(cot, w_down[...]) * slope
     cot_two = mm_t(cot_up.astype(BF), w_up[...]) * gains[1:2]
     cot_middle = cot.astype(F32) + normalise_back(cot_two, unit, inv)
     return cot_middle, mm_t(cot_middle.astype(BF), w_out[...]).astype(BF)
@@ -171,9 +183,11 @@
     return jnp.concatenate(tables, axis=0)
 
 
-def block_backward(cot, hidden, gains, coords, saved, w_qkv, w_out, w_up, w_down, with_table=True):
-    projected, probs, middle, up = saved
-    cot_middle, cot_mixed = feed_forward_back(cot, gains, middle, up, w_out, w_up, w_down)
+def block_backward(cot, gains, coords, saved, w_qkv, w_out, w_up, w_down, with_table=True):
+    projected, probs, mixed, unit, inv, unit_two, inv_two, slope = saved
+    cot_middle, cot_mixed = feed_forward_back(
+        cot, gains, unit_two, inv_two, slope, w_out, w_up, w_down
+    )
     cells_t = cells(coords, False).astype(BF)
     blank = jnp.zeros((SLOTS - 3 * PITCH, SLOTS), F32)
     cells_key = jnp.transpose(jnp.concatenate([cells(coords, True), blank], axis=0)).astype(BF)
@@ -185,11 +199,8 @@
         dm = cot_mixed[:, 128 * g : 128 * g + 128]
         q_t = jnp.transpose(q.astype(F32)).astype(BF)
         dm_t = jnp.transpose(dm.astype(F32)).astype(BF)
-        soft = probs[g]
-        cot_soft = mm_t(spread(dm), v)
-        weighted = soft.astype(F32) * cot_soft
-        total = jnp.sum(weighted, axis=-1, keepdims=True)
-        cot_scores = (weighted - soft.astype(F32) * total).astype(BF)
+        cot_scores = attend_back(probs[g], mixed[:, 128 * g : 128 * g + 128], dm, v)
+        soft = probs[g].astype(BF)
         cot_q.append(mm(side_by_side(cot_scores), spread(k)) * SCALE)
         k_rows, v_rows = [], []
         for j in range(4):
@@ -204,7 +215,6 @@
         cot_v.append(jnp.transpose(jnp.concatenate(v_rows, axis=0)))
     cot_projected = jnp.concatenate(cot_q + cot_k + cot_v, axis=1).astype(BF)
     cot_normed = mm_t(cot_projected, w_qkv[...]) * gains[0:1]
-    unit, inv = normalise(hidden)
     cot_hidden = cot_middle + normalise_back(cot_normed, unit, inv)
     if not with_table:
         return cot_hidden.astype(BF), None
@@ -234,49 +244,56 @@
     hidden = jnp.concatenate([points[r] for r in quarters], axis=0)
     query_side = jnp.transpose(query_cells(place)).astype(BF)
     bias_left = mm(query_side, table_matrix(table)).astype(BF)
-    probs, mixed, key_sides = {}, [], []
+    key_sides = [
+        jnp.transpose(key_cells(places[p], occupieds[p])).astype(BF) for p in range(4)
+    ]
+    scores, values = [], []
     for p in range(4):
-        key_side = jnp.transpose(key_cells(places[p], occupieds[p])).astype(BF)
-        key_sides.append(key_side)
         rows, window = slice(p * QUAD, (p + 1) * QUAD), slice(p * SLOTS, (p + 1) * SLOTS)
-        groups = []
         for g in range(2):
             lanes = slice(128 * g, 128 * g + 128)
             k = key_value[window, 128 * g : 128 * g + 128]
-            v = key_value[window, WIDTH + 128 * g : WIDTH + 128 * g + 128]
+            values.append(key_value[window, WIDTH + 128 * g : WIDTH + 128 * g + 128])
             lefts = jnp.concatenate(
                 [bias_left[rows, 128 * h : 128 * h + 128] for h in range(4 * g, 4 * g + 4)], axis=0
             )
-            scores = mm_t(
-                jnp.concatenate([spread(query[rows, lanes]), lefts], axis=1),
-                jnp.concatenate([k, key_side], axis=1),
+            scores.append(
+                mm_t(
+                    jnp.concatenate([spread(query[rows, lanes]), lefts], axis=1),
+                    jnp.concatenate([k, key_sides[p]], axis=1),
+                )
             )
-            probs[p, g] = softmax(scores)
-            groups.append(head_lanes(mm(probs[p, g], v)))
-        mixed.append(jnp.concatenate(groups, axis=1))
-    middle = hidden + mm(jnp.concatenate(mixed, axis=0).astype(BF), w_out[...])
-    unit_two, _ = normalise(middle)
+    probs, mixed = attend(scores, values)
+    mixed = [jnp.concatenate(mixed[2 * p : 2 * p + 2], axis=1) for p in range(4)]
+    mixed = jnp.concatenate(mixed, axis=0)
+    middle = hidden + mm(mixed.astype(BF), w_out[...])
+    unit_two, inv_two = normalise(middle)
     up = mm((unit_two * gains[1:2]).astype(BF), w_up[...])
-    expanded, _ = gelu_parts(up)
+    expanded, slope = gelu_and_slope(up)
     out = middle + mm(expanded.astype(BF), w_down[...])
-    return out.astype(BF), (key_value, probs, key_sides, middle, up)
+    return out.astype(BF), (key_value, probs, mixed, key_sides, unit_two, inv_two, slope)
 
 
 def halo_table(cot, place, gains, saved, w_out, w_up, w_down):
-    key_value, probs, key_sides, middle, up = saved
-    _, cot_mixed = feed_forward_back(cot, gains, middle, up, w_out, w_up, w_down)
+    key_value, probs, mixed, key_sides, unit_two, inv_two, slope = saved
+    _, cot_mixed = feed_forward_back(
+        cot, gains, unit_two, inv_two, slope, w_out, w_up, w_down
+    )
+    cot_scores = []
+    for p in range(4):
+        rows, window = slice(p * QUAD, (p + 1) * QUAD), slice(p * SLOTS, (p + 1) * SLOTS)
+        for g in range(2):
+            lanes = slice(128 * g, 128 * g + 128)
+            v = key_value[window, WIDTH + 128 * g : WIDTH + 128 * g + 128]
+            cot_scores.append(
+                attend_back(probs[2 * p + g], mixed[rows, lanes], cot_mixed[rows, lanes], v)
+            )
     pair_rows = []
     for p in range(4):
-        rows, window = slice(p * QUAD, (p + 1) * QUAD), slice(p * SLOTS, (p + 1) * SLOTS)
-        pairs = []
-        for g in range(2):
-            v = key_value[window, WIDTH + 128 * g : WIDTH + 128 * g + 128]
-            soft = probs[p, g].astype(F32)
-            weighted = soft * mm_t(spread(cot_mixed[rows, 128 * g : 128 * g + 128]), v)
-            total = jnp.sum(weighted, axis=-1, keepdims=True)
-            both = mm((weighted - soft * total).astype(BF), key_sides[p])
-            pairs += [both[j * QUAD : (j + 1) * QUAD] for j in range(4)]
-        pair_rows.append(jnp.concatenate(pairs, axis=1))
+        both = [mm(x, key_sides[p]) for x in cot_scores[2 * p : 2 * p + 2]]
+        pair_rows.append(
+            jnp.concatenate([x[j * QUAD : (j + 1) * QUAD] for x in both for j in range(4)], axis=1)
+        )
     pairs = mm(cells(place, False).astype(BF), jnp.concatenate(pair_rows, axis=0).astype(BF))
     return table_sums(
         [
@@ -313,19 +330,6 @@
         copy.wait()
 
 
-def stage_kernel(*refs):
-    count = (len(refs) - 2) // 2
-    sources, targets, arrived = refs[1 : 1 + count], refs[1 + count : -1], refs[-1]
-    copies = [
-        pltpu.make_async_copy(source, target, arrived.at[i])
-        for i, (source, target) in enumerate(zip(sources, targets))
-    ]
-    for copy in copies:
-        copy.start()
-    for copy in copies:
-        copy.wait()
-
-
 def main_kernel(
     features, occupancy, coords, grad_out, from_y, from_x, from_xy,
     gains, tables, w_qkv, w_out, w_up, w_down,
@@ -369,7 +373,7 @@
         hidden, gains[1], shifted, occupied, tables[1], *second_weights
     )
     cot, second_table = block_backward(
-        grad, hidden, gains[1], shifted, second_saved, *second_weights
+        grad, gains[1], shifted, second_saved, *second_weights
     )
     first_table = halo_table(cot, place, gains[0], first_saved, *first_weights[1:])
     for position, target in enumerate((own, back_y, back_x, back_xy)):
@@ -395,14 +399,25 @@
     points = features[...].astype(F32)
     _, saved = block_forward(points, gains[0], place, occupancy[...], tables[0], *weights)
     grad_points[...], _ = block_backward(
-        cot, points, gains[0], place, saved, *weights, with_table=False
-    )
-
-
-def unpack_kernel(parts, out):
+        cot, gains[0], place, saved, *weights, with_table=False
+    )
+
+
+def sum_of(parts):
     total = parts[0].astype(F32)
     for i in range(1, parts.shape[0]):
         total = total + parts[i].astype(F32)
+    return total
+
+
+def relay_kernel(parts, out):
+    total = sum_of(parts).astype(BF)
+    for i in range(out.shape[0]):
+        out[i] = total
+
+
+def unpack_kernel(parts, out):
+    total = sum_of(parts)
     for k in range(2):
         for e in range(3):
             start = (3 * k + e) * PITCH
@@ -410,7 +425,7 @@
             out[k, e] = moved[:, : out.shape[-1]]
 
 
-def call(kernel, shapes, *args, far=None, scratch=()):
+def call(kernel, shapes, *args, far=None, scratch=(), cost=None):
     options = {}
     if far is not None:
         args = args[:far] + tuple(in_hbm(a) for a in args[far:])
@@ -422,6 +437,7 @@
         out_shape=[jax.ShapeDtypeStruct(s, d) for s, d in shapes],
         scratch_shapes=scratch,
         compiler_params=pltpu.CompilerParams(vmem_limit_bytes=VMEM_LIMIT),
+        cost_estimate=cost,
         interpret=INTERPRET,
         **options,
     )(*args)
@@ -451,25 +467,24 @@
     packet, reply = ((SLOTS + QUAD + 16, WIDTH), BF), ((2 * QUAD, WIDTH), BF)
     to_y, to_x, to_xy = call(
         pack_kernel, [packet] * 3, points, occupied, place, grad, far=0,
+        cost=pl.CostEstimate(flops=COST, transcendentals=0, bytes_accessed=8 * 1024 * 1024),
         scratch=[pltpu.VMEM(occupied.shape, jnp.int32), pltpu.VMEM(place.shape, jnp.int32), pltpu.SemaphoreType.DMA((8,))],
     )
-    sources = (points, occupied, place, grad, norm_gains, bias_tables, w_qkv, w_out, w_up, w_down)
-    staged = call(
-        stage_kernel, [(a.shape, a.dtype) for a in sources], to_y, *sources, far=1,
-        scratch=[pltpu.SemaphoreType.DMA((len(sources),))],
-    )
+    from_x = move(to_x, -1, 0)
+    from_xy = move(to_xy, -1, -1)
+    from_y = move(to_y, 0, -1)
     first = lax.axis_size(phases[0])
+    staged = (points, occupied, place, grad, norm_gains, bias_tables, w_qkv, w_out, w_up, w_down)
     own, back_y, back_x, back_xy, tables = call(
         main_kernel,
         [reply] * 4 + [((first, HEADS, 128), BF)],
-        *staged[:4], move(to_y, 0, -1), move(to_x, -1, 0), move(to_xy, -1, -1), *staged[4:],
+        *staged[:4], from_y, from_x, from_xy, *staged[4:],
     )
     home_y = move(back_y, 0, 1)
     home_x = move(back_x, 1, 0)
     home_xy = move(back_xy, 1, 1)
     tables = lax.all_to_all(tables, phases[0], 0, 0)
-    total = jnp.sum(tables.astype(F32), axis=0).astype(BF)
-    tables = jnp.broadcast_to(total[None], (lax.axis_size(phases[1]), HEADS, 128))
+    (tables,) = call(relay_kernel, [((lax.axis_size(phases[1]), HEADS, 128), BF)], tables)
     tables = lax.all_to_all(tables, phases[1], 0, 0)
     (grad_tables,) = call(unpack_kernel, [(bias_tables.shape, F32)], tables)
     out_points, grad_points = call(
@@ -483,7 +498,7 @@
     if shape == (16, 32):
         fine = Mesh(mesh.devices.reshape(2, 4, 2, 8, 4), ("zh", "y", "c", "zl", "x"))
         gx, gy = ("zh", "y", "c"), ("zl", "x")
-        phases = (("y", "c", "x"), ("zh", "zl"))
+        phases = (("zh", "zl"), ("y", "c", "x"))
     else:
         fine = Mesh(mesh.devices, ("gx", "gy"))
         gx, gy, phases = ("gx",), ("gy",), (("gx",), ("gy",))

time: 103 us -> 99.8 us (0.969)
  the two profiles are of different devices: /device:TPU:24 before, /device:TPU:1 now
where the time goes in v4:
time: 99.8 us; the launch traced here: 99.4 us
  starting transfers between devices  50 us (50%)
  blocking collectives  18.7 us (19%)
  waiting for transfers between devices  16.4 us (16%)
  Pallas kernels  13.3 us (13%)
    ppermute x6, starting transfers between devices, move(): return lax.ppermute(value, gx + gy, pairs)  38.7 us
    all_to_all x1, blocking collectives, on_device(): tables = lax.all_to_all(tables, phases[0], 0, 0)  18.7 us
    ppermute x6, waiting for transfers between devices, move(): return lax.ppermute(value, gx + gy, pairs)  16.4 us
    pallas_call x5, Pallas kernels, call(): pl.pallas_call(kernel, out_shape=[jax.ShapeDtypeStruct(s, d) for s, d in...  13.3 us
    all_to_all x1, starting transfers between devices, on_device(): tables = lax.all_to_all(tables, phases[1], 0, 0)  11.3 us
  transfers between devices with their start and end apart: 7, of which 3 were waited for; matrix products, arithmetic and copies ran while one was open for 0% of the time, Pallas kernels for 4%

profile of v4, /device:TPU:1, one launch (start us, length us, event | category | flops | bytes accessed | tf_op | source)
XLA Modules:
  0.0 99.4 jit_solution(15251752528634256013)
XLA Ops:
  0.6 0.0 copy-start
  0.6 0.0 copy-start.1
  0.7 0.0 copy-start.2
  0.7 0.0 copy-start.3
  0.7 0.0 copy-start.4
  0.7 0.0 copy-start.5
  0.7 0.0 copy-start.6
  0.7 0.0 copy-start.9
  0.7 1.1 %shard_map.121 = (bf16[176,256]{1,0:T(8,128)(2,1)S(1)}, bf16[176,256]{1,0:T(8,128)(2,1)S(1)}, bf16[176,256]{1,0:T(8,128)(2,1)S(1)}) custom-call(bf16[128,256]{1,0:T(8,128)(2,1)} %bitcast.6, s32[1,128]{1,0:T(1,128)} %bitcast.14, s32[3,1,128]{2,1,0:T(1,128)} %bitcast.11, bf16[128,256]{1,0:T(8,128)(2,1)} %bitcast.9), custom_call_target="tpu_custom_call" | custom-call | flops 10000000000 | bytes 8388608 | tf_op jit(solution)/shard_map/pallas_call | solution.py:435
  1.9 0.0 copy-start.7
  1.9 0.0 copy-start.8
  1.9 15.9 %collective-permute-start = (bf16[176,256]{1,0:T(8,128)(2,1)S(1)}, bf16[176,256]{1,0:T(8,128)(2,1)S(1)}, u32[]{:S(2)}, u32[]{:S(2)}) collective-permute-start(bf16[176,256]{1,0:T(8,128)(2,1)S(1)} %get-tuple-element.13), channel_id=1, source_target_pairs={{0,31},{1,0},{2,1},{3,2},{4,3},{5,4},{6,5},{7,6},{8,7},{9,8},{10,9... | collective-permute-start | bytes 270344 | tf_op jit(solution)/shard_map/ppermute | solution.py:463
  17.8 2.9 %collective-permute-start.1 = (bf16[176,256]{1,0:T(8,128)(2,1)S(1)}, bf16[176,256]{1,0:T(8,128)(2,1)S(1)}, u32[]{:S(2)}, u32[]{:S(2)}) collective-permute-start(bf16[176,256]{1,0:T(8,128)(2,1)S(1)} %get-tuple-element.14), channel_id=1, source_target_pairs={{0,480},{1,481},{2,482},{3,483},{4,484},{5,485},{6,486},{7,487},{8... | collective-permute-start | bytes 270344 | tf_op jit(solution)/shard_map/ppermute | solution.py:463
  20.7 10.3 %collective-permute-start.2 = (bf16[176,256]{1,0:T(8,128)(2,1)S(1)}, bf16[176,256]{1,0:T(8,128)(2,1)S(1)}, u32[]{:S(2)}, u32[]{:S(2)}) collective-permute-start(bf16[176,256]{1,0:T(8,128)(2,1)S(1)} %get-tuple-element.15), channel_id=1, source_target_pairs={{0,511},{1,480},{2,481},{3,482},{4,483},{5,484},{6,485},{7,486},{8... | collective-permute-start | bytes 270344 | tf_op jit(solution)/shard_map/ppermute | solution.py:463
  30.9 0.0 collective-permute-done.from_y
  30.9 0.0 collective-permute-done.1.from_x
  30.9 6.2 %collective-permute-done.2.from_xy = bf16[176,256]{1,0:T(8,128)(2,1)S(1)} collective-permute-done((bf16[176,256]{1,0:T(8,128)(2,1)S(1)}, bf16[176,256]{1,0:T(8,128)(2,1)S(1)}, u32[]{:S(2)}, u32[]{:S(2)}) %collective-permute-start.2) | collective-permute-done | bytes 90144 | tf_op jit(solution)/shard_map/ppermute | solution.py:463
  37.1 0.0 copy-done
  37.1 0.0 copy-done.1
  37.1 0.0 copy-done.2
  37.1 0.0 copy-done.3
  37.1 0.0 copy-done.4
  37.1 0.0 copy-done.5
  37.1 0.0 copy-done.6
  37.2 0.0 copy-done.9
  37.2 0.0 copy-done.7
  37.2 0.0 copy-done.8
  37.2 6.9 %shard_map.122 = (bf16[64,256]{1,0:T(8,128)(2,1)S(1)}, bf16[64,256]{1,0:T(8,128)(2,1)S(1)}, bf16[64,256]{1,0:T(8,128)(2,1)S(1)}, bf16[64,256]{1,0:T(8,128)(2,1)S(1)}, bf16[16,8,128]{2,1,0:T(8,128)(2,1)S(1)}) custom-call(bf16[128,256]{1,0:T(8,128)(2,1)S(1)} %bitcast.7, s32[1,128]{1,0:T(1,128)S(1)} %bitcast.15, s32[3,1,128]{2,1,0:T(1,128)S(1)} %bitcast.12, ...), custom_call_target="tpu_custom_call" | custom-call | tf_op jit(solution)/shard_map/pallas_call | solution.py:435
  44.1 18.7 %all_to_all.10.parts = bf16[16,8,128]{2,1,0:T(8,128)(2,1)S(1)} all-to-all(bf16[16,8,128]{2,1,0:T(8,128)(2,1)S(1)} %get-tuple-element.22), channel_id=1, replica_groups=mesh['zh'=2,'y'=4,'c'=2,'zl'=8,'x'=4] {'zh','zl'}, dimensions={0} | all-to-all | bytes 65536 | tf_op jit(solution)/shard_map/all_to_all | solution.py:486
  62.7 0.6 shard_map.124
  63.4 11.3 %all-to-all-start.1 = ((bf16[32,8,128]{2,1,0:T(8,128)(2,1)}), bf16[32,8,128]{2,1,0:T(8,128)(2,1)S(1)}, u32[]{:S(2)}, u32[]{:S(2)}) async-start(bf16[32,8,128]{2,1,0:T(8,128)(2,1)} %shard_map.124), calls=%async_computation.1 | async-start | bytes 131072 | tf_op jit(solution)/shard_map/all_to_all | solution.py:488
  74.7 4.4 %collective-permute-start.3 = (bf16[64,256]{1,0:T(8,128)(2,1)S(1)}, bf16[64,256]{1,0:T(8,128)(2,1)S(1)}, u32[]{:S(2)}, u32[]{:S(2)}) collective-permute-start(bf16[64,256]{1,0:T(8,128)(2,1)S(1)} %get-tuple-element.16), channel_id=1, source_target_pairs={{0,33},{1,34},{2,35},{3,36},{4,37},{5,38},{6,39},{7,40},{8,41},{9,... | collective-permute-start | bytes 98312 | tf_op jit(solution)/shard_map/ppermute | solution.py:463
  79.1 2.2 %collective-permute-start.4 = (bf16[64,256]{1,0:T(8,128)(2,1)S(1)}, bf16[64,256]{1,0:T(8,128)(2,1)S(1)}, u32[]{:S(2)}, u32[]{:S(2)}) collective-permute-start(bf16[64,256]{1,0:T(8,128)(2,1)S(1)} %get-tuple-element.17), channel_id=1, source_target_pairs={{0,32},{1,33},{2,34},{3,35},{4,36},{5,37},{6,38},{7,39},{8,40},{9,... | collective-permute-start | bytes 98312 | tf_op jit(solution)/shard_map/ppermute | solution.py:463
  81.3 3.1 %collective-permute-start.5 = (bf16[64,256]{1,0:T(8,128)(2,1)S(1)}, bf16[64,256]{1,0:T(8,128)(2,1)S(1)}, u32[]{:S(2)}, u32[]{:S(2)}) collective-permute-start(bf16[64,256]{1,0:T(8,128)(2,1)S(1)} %get-tuple-element.18), channel_id=1, source_target_pairs={{0,1},{1,2},{2,3},{3,4},{4,5},{5,6},{6,7},{7,8},{8,9},{9,10},{10,1... | collective-permute-start | bytes 98312 | tf_op jit(solution)/shard_map/ppermute | solution.py:463
  84.4 4.2 %collective-permute-done.3.home_xy = bf16[64,256]{1,0:T(8,128)(2,1)S(1)} collective-permute-done((bf16[64,256]{1,0:T(8,128)(2,1)S(1)}, bf16[64,256]{1,0:T(8,128)(2,1)S(1)}, u32[]{:S(2)}, u32[]{:S(2)}) %collective-permute-start.3) | collective-permute-done | bytes 32800 | tf_op jit(solution)/shard_map/ppermute | solution.py:463
  88.6 0.0 collective-permute-done.4.home_x
  88.6 6.1 %collective-permute-done.5.home_y = bf16[64,256]{1,0:T(8,128)(2,1)S(1)} collective-permute-done((bf16[64,256]{1,0:T(8,128)(2,1)S(1)}, bf16[64,256]{1,0:T(8,128)(2,1)S(1)}, u32[]{:S(2)}, u32[]{:S(2)}) %collective-permute-start.5) | collective-permute-done | bytes 32800 | tf_op jit(solution)/shard_map/ppermute | solution.py:463
  94.7 4.0 %shard_map.123 = (bf16[128,256]{1,0:T(8,128)(2,1)}, bf16[128,256]{1,0:T(8,128)(2,1)}) custom-call(bf16[64,256]{1,0:T(8,128)(2,1)S(1)} %collective-permute-done.3.home_xy, bf16[64,256]{1,0:T(8,128)(2,1)S(1)} %collective-permute-done.4.home_x, bf16[64,256]{1,0:T(8,128)(2,1)S(1)} %collective-permute-done.5.home_y, bf16[64,256]{1,0:T(8,128)(2,1)S(1)} %get-tuple-element.19.own, ...), custom_call_target="tpu_custom_call" | custom-call | tf_op jit(solution)/shard_map/pallas_call | solution.py:435
  98.6 0.0 all-to-all-done.1.parts
  98.6 0.7 shard_map.125
Async XLA Ops:
  0.6 36.5 %copy-start = (bf16[2,256,1024]{2,1,0:T(8,128)(2,1)S(1)}, bf16[2,256,1024]{2,1,0:T(8,128)(2,1)}, u32[]{:S(2)}) copy-start(bf16[2,256,1024]{2,1,0:T(8,128)(2,1)} %w_up.3) | copy-start | bytes 3145732
  0.6 36.5 %copy-start.1 = (bf16[2,1024,256]{2,1,0:T(8,128)(2,1)S(1)}, bf16[2,1024,256]{2,1,0:T(8,128)(2,1)}, u32[]{:S(2)}) copy-start(bf16[2,1024,256]{2,1,0:T(8,128)(2,1)} %w_down.3) | copy-start | bytes 3145732
  0.7 36.5 %copy-start.2 = (bf16[2,256,768]{2,1,0:T(8,128)(2,1)S(1)}, bf16[2,256,768]{2,1,0:T(8,128)(2,1)}, u32[]{:S(2)}) copy-start(bf16[2,256,768]{2,1,0:T(8,128)(2,1)} %w_qkv.3) | copy-start | bytes 2359300
  0.7 36.5 %copy-start.3 = (bf16[2,256,256]{2,1,0:T(8,128)(2,1)S(1)}, bf16[2,256,256]{2,1,0:T(8,128)(2,1)}, u32[]{:S(2)}) copy-start(bf16[2,256,256]{2,1,0:T(8,128)(2,1)} %w_out.3) | copy-start | bytes 786436
  0.7 36.5 %copy-start.4 = (bf16[1,1,128,256]{3,2,1,0:T(8,128)(2,1)S(1)}, bf16[1,1,128,256]{3,2,1,0:T(8,128)(2,1)}, u32[]{:S(2)}) copy-start(bf16[1,1,128,256]{3,2,1,0:T(8,128)(2,1)} %param.10) | copy-start | bytes 196612
  0.7 36.5 %copy-start.5 = (f32[2,3,8,15]{3,2,1,0:T(8,128)S(1)}, f32[2,3,8,15]{3,2,1,0:T(8,128)}, u32[]{:S(2)}) copy-start(f32[2,3,8,15]{3,2,1,0:T(8,128)} %tables.3) | copy-start | bytes 8644
  0.7 36.5 %copy-start.6 = (bf16[1,1,128,256]{3,2,1,0:T(8,128)(2,1)S(1)}, bf16[1,1,128,256]{3,2,1,0:T(8,128)(2,1)}, u32[]{:S(2)}) copy-start(bf16[1,1,128,256]{3,2,1,0:T(8,128)(2,1)} %param.19) | copy-start | bytes 196612
  0.7 36.5 %copy-start.9 = (s32[1,1,128]{2,1,0:T(1,128)S(1)}, s32[1,1,128]{2,1,0:T(1,128)}, u32[]{:S(2)}) copy-start(s32[1,1,128]{2,1,0:T(1,128)} %param.11) | copy-start | bytes 1540
  1.9 35.3 %copy-start.7 = (f32[2,2,256]{2,1,0:T(2,128)S(1)}, f32[2,2,256]{2,1,0:T(2,128)}, u32[]{:S(2)}) copy-start(f32[2,2,256]{2,1,0:T(2,128)} %gains.3) | copy-start | bytes 12292
  1.9 35.3 %copy-start.8 = (s32[1,1,3,128]{3,1,2,0:T(1,128)S(1)}, s32[1,1,3,128]{3,1,2,0:T(1,128)}, u32[]{:S(2)}) copy-start(s32[1,1,3,128]{3,1,2,0:T(1,128)} %param.12) | copy-start | bytes 4612
  1.9 29.0 %collective-permute-start = (bf16[176,256]{1,0:T(8,128)(2,1)S(1)}, bf16[176,256]{1,0:T(8,128)(2,1)S(1)}, u32[]{:S(2)}, u32[]{:S(2)}) collective-permute-start(bf16[176,256]{1,0:T(8,128)(2,1)S(1)} %get-tuple-element.13), channel_id=1, source_target_pairs={{0,31},{1,0},{2,1},{3,2},{4,3},{5,4},{6,5},{7,6},{8,7},{9,8},{10,9... | collective-permute-start | bytes 270344 | tf_op jit(solution)/shard_map/ppermute | solution.py:463
  17.8 13.2 %collective-permute-start.1 = (bf16[176,256]{1,0:T(8,128)(2,1)S(1)}, bf16[176,256]{1,0:T(8,128)(2,1)S(1)}, u32[]{:S(2)}, u32[]{:S(2)}) collective-permute-start(bf16[176,256]{1,0:T(8,128)(2,1)S(1)} %get-tuple-element.14), channel_id=1, source_target_pairs={{0,480},{1,481},{2,482},{3,483},{4,484},{5,485},{6,486},{7,487},{8... | collective-permute-start | bytes 270344 | tf_op jit(solution)/shard_map/ppermute | solution.py:463
  20.7 16.5 %collective-permute-start.2 = (bf16[176,256]{1,0:T(8,128)(2,1)S(1)}, bf16[176,256]{1,0:T(8,128)(2,1)S(1)}, u32[]{:S(2)}, u32[]{:S(2)}) collective-permute-start(bf16[176,256]{1,0:T(8,128)(2,1)S(1)} %get-tuple-element.15), channel_id=1, source_target_pairs={{0,511},{1,480},{2,481},{3,482},{4,483},{5,484},{6,485},{7,486},{8... | collective-permute-start | bytes 270344 | tf_op jit(solution)/shard_map/ppermute | solution.py:463
  63.4 35.3 %all-to-all-start.1 = ((bf16[32,8,128]{2,1,0:T(8,128)(2,1)}), bf16[32,8,128]{2,1,0:T(8,128)(2,1)S(1)}, u32[]{:S(2)}, u32[]{:S(2)}) async-start(bf16[32,8,128]{2,1,0:T(8,128)(2,1)} %shard_map.124), calls=%async_computation.1 | async-start | bytes 131072 | tf_op jit(solution)/shard_map/all_to_all | solution.py:488
  74.7 13.9 %collective-permute-start.3 = (bf16[64,256]{1,0:T(8,128)(2,1)S(1)}, bf16[64,256]{1,0:T(8,128)(2,1)S(1)}, u32[]{:S(2)}, u32[]{:S(2)}) collective-permute-start(bf16[64,256]{1,0:T(8,128)(2,1)S(1)} %get-tuple-element.16), channel_id=1, source_target_pairs={{0,33},{1,34},{2,35},{3,36},{4,37},{5,38},{6,39},{7,40},{8,41},{9,... | collective-permute-start | bytes 98312 | tf_op jit(solution)/shard_map/ppermute | solution.py:463
  79.1 9.5 %collective-permute-start.4 = (bf16[64,256]{1,0:T(8,128)(2,1)S(1)}, bf16[64,256]{1,0:T(8,128)(2,1)S(1)}, u32[]{:S(2)}, u32[]{:S(2)}) collective-permute-start(bf16[64,256]{1,0:T(8,128)(2,1)S(1)} %get-tuple-element.17), channel_id=1, source_target_pairs={{0,32},{1,33},{2,34},{3,35},{4,36},{5,37},{6,38},{7,39},{8,40},{9,... | collective-permute-start | bytes 98312 | tf_op jit(solution)/shard_map/ppermute | solution.py:463
  81.3 13.4 %collective-permute-start.5 = (bf16[64,256]{1,0:T(8,128)(2,1)S(1)}, bf16[64,256]{1,0:T(8,128)(2,1)S(1)}, u32[]{:S(2)}, u32[]{:S(2)}) collective-permute-start(bf16[64,256]{1,0:T(8,128)(2,1)S(1)} %get-tuple-element.18), channel_id=1, source_target_pairs={{0,1},{1,2},{2,3},{3,4},{4,5},{5,6},{6,7},{7,8},{8,9},{9,10},{10,1... | collective-permute-start | bytes 98312 | tf_op jit(solution)/shard_map/ppermute | solution.py:463

commit v5 on v4

--- a/solution.py
+++ b/solution.py
@@ -122,12 +122,9 @@
 
 
 def attend_back(soft, mixed, cot_mixed, v):
-    product = mixed * cot_mixed.astype(F32)
-    high = product.astype(BF)
-    low = (product - high.astype(F32)).astype(BF)
-    ones = jnp.ones_like(v)
-    left = jnp.concatenate([spread(cot_mixed), spread(-high), spread(-low)], axis=1)
-    return (soft * mm_t(left, jnp.concatenate([v, ones, ones], axis=1))).astype(BF)
+    product = (-mixed * cot_mixed.astype(F32)).astype(BF)
+    left = jnp.concatenate([spread(cot_mixed), spread(product)], axis=1)
+    return (soft * mm_t(left, jnp.concatenate([v, jnp.ones_like(v)], axis=1))).astype(BF)
 
 
 def gelu_and_slope(v):
@@ -322,8 +319,7 @@
     meta = jnp.concatenate(
         [occupied[...]] + [place[e] for e in range(3)] + [jnp.zeros((4, SLOTS), jnp.int32)], axis=0
     ).astype(F32)
-    meta = jnp.concatenate([meta, jnp.zeros((8, SLOTS), F32)], axis=0)
-    meta = jnp.concatenate([meta, jnp.zeros((16, SLOTS), F32)], axis=1).astype(BF)
+    meta = jnp.concatenate([meta, jnp.zeros((8, SLOTS), F32)], axis=1).astype(BF)
     for target in (to_y, to_x, to_xy):
         target[SLOTS + QUAD :] = meta
     for copy in copies[2:]:
@@ -348,7 +344,7 @@
             axis=0,
         )
     ] + [
-        part[SLOTS + QUAD :].astype(F32)[0:8, 0:SLOTS].astype(jnp.int32) for part in received
+        part[SLOTS + QUAD :].astype(F32)[:, 0:SLOTS].astype(jnp.int32) for part in received
     ]
     quarter = iota((8, SLOTS), 1) // QUAD
     meta = jnp.zeros((8, SLOTS), jnp.int32)
@@ -464,7 +460,7 @@
 
     points, occupied, grad = features[0, 0], occupancy[0], grad_out[0, 0]
     place = jnp.swapaxes(coords[0], 0, 1)
-    packet, reply = ((SLOTS + QUAD + 16, WIDTH), BF), ((2 * QUAD, WIDTH), BF)
+    packet, reply = ((SLOTS + QUAD + 8, WIDTH), BF), ((2 * QUAD, WIDTH), BF)
     to_y, to_x, to_xy = call(
         pack_kernel, [packet] * 3, points, occupied, place, grad, far=0,
         cost=pl.CostEstimate(flops=COST, transcendentals=0, bytes_accessed=8 * 1024 * 1024),

time: 99.8 us -> 99.1 us (level)
  no operation moved by 1% of the time
where the time goes in v5:
time: 99.1 us; the launch traced here: 98.7 us
  starting transfers between devices  50.1 us (51%)
  blocking collectives  18.8 us (19%)
  waiting for transfers between devices  15.8 us (16%)
  Pallas kernels  13 us (13%)
    ppermute x6, starting transfers between devices, move(): return lax.ppermute(value, gx + gy, pairs)  38.7 us
    all_to_all x1, blocking collectives, on_device(): tables = lax.all_to_all(tables, phases[0], 0, 0)  18.8 us
    ppermute x6, waiting for transfers between devices, move(): return lax.ppermute(value, gx + gy, pairs)  15.8 us
    pallas_call x5, Pallas kernels, call(): pl.pallas_call(kernel, out_shape=[jax.ShapeDtypeStruct(s, d) for s, d in...  13 us
    all_to_all x1, starting transfers between devices, on_device(): tables = lax.all_to_all(tables, phases[1], 0, 0)  11.3 us
  transfers between devices with their start and end apart: 7, of which 3 were waited for; matrix products, arithmetic and copies ran while one was open for 0% of the time, Pallas kernels for 4%

profile of v5, /device:TPU:1, one launch (start us, length us, event | category | flops | bytes accessed | tf_op | source)
XLA Modules:
  0.0 98.7 jit_solution(5273705646069128609)
XLA Ops:
  0.6 0.0 copy-start
  0.6 0.0 copy-start.1
  0.7 0.0 copy-start.2
  0.7 0.0 copy-start.3
  0.7 0.0 copy-start.4
  0.7 0.0 copy-start.5
  0.7 0.0 copy-start.6
  0.7 0.0 copy-start.9
  0.7 1.1 %shard_map.121 = (bf16[168,256]{1,0:T(8,128)(2,1)S(1)}, bf16[168,256]{1,0:T(8,128)(2,1)S(1)}, bf16[168,256]{1,0:T(8,128)(2,1)S(1)}) custom-call(bf16[128,256]{1,0:T(8,128)(2,1)} %bitcast.6, s32[1,128]{1,0:T(1,128)} %bitcast.14, s32[3,1,128]{2,1,0:T(1,128)} %bitcast.11, bf16[128,256]{1,0:T(8,128)(2,1)} %bitcast.9), custom_call_target="tpu_custom_call" | custom-call | flops 10000000000 | bytes 8388608 | tf_op jit(solution)/shard_map/pallas_call | solution.py:431
  1.9 0.0 copy-start.7
  1.9 0.0 copy-start.8
  1.9 15.9 %collective-permute-start = (bf16[168,256]{1,0:T(8,128)(2,1)S(1)}, bf16[168,256]{1,0:T(8,128)(2,1)S(1)}, u32[]{:S(2)}, u32[]{:S(2)}) collective-permute-start(bf16[168,256]{1,0:T(8,128)(2,1)S(1)} %get-tuple-element.13), channel_id=1, source_target_pairs={{0,31},{1,0},{2,1},{3,2},{4,3},{5,4},{6,5},{7,6},{8,7},{9,8},{10,9... | collective-permute-start | bytes 258056 | tf_op jit(solution)/shard_map/ppermute | solution.py:459
  17.8 2.9 %collective-permute-start.1 = (bf16[168,256]{1,0:T(8,128)(2,1)S(1)}, bf16[168,256]{1,0:T(8,128)(2,1)S(1)}, u32[]{:S(2)}, u32[]{:S(2)}) collective-permute-start(bf16[168,256]{1,0:T(8,128)(2,1)S(1)} %get-tuple-element.14), channel_id=1, source_target_pairs={{0,480},{1,481},{2,482},{3,483},{4,484},{5,485},{6,486},{7,487},{8... | collective-permute-start | bytes 258056 | tf_op jit(solution)/shard_map/ppermute | solution.py:459
  20.7 10.3 %collective-permute-start.2 = (bf16[168,256]{1,0:T(8,128)(2,1)S(1)}, bf16[168,256]{1,0:T(8,128)(2,1)S(1)}, u32[]{:S(2)}, u32[]{:S(2)}) collective-permute-start(bf16[168,256]{1,0:T(8,128)(2,1)S(1)} %get-tuple-element.15), channel_id=1, source_target_pairs={{0,511},{1,480},{2,481},{3,482},{4,483},{5,484},{6,485},{7,486},{8... | collective-permute-start | bytes 258056 | tf_op jit(solution)/shard_map/ppermute | solution.py:459
  30.9 0.0 collective-permute-done.from_y
  30.9 0.0 collective-permute-done.1.from_x
  30.9 5.5 %collective-permute-done.2.from_xy = bf16[168,256]{1,0:T(8,128)(2,1)S(1)} collective-permute-done((bf16[168,256]{1,0:T(8,128)(2,1)S(1)}, bf16[168,256]{1,0:T(8,128)(2,1)S(1)}, u32[]{:S(2)}, u32[]{:S(2)}) %collective-permute-start.2) | collective-permute-done | bytes 86048 | tf_op jit(solution)/shard_map/ppermute | solution.py:459
  36.5 0.0 copy-done
  36.5 0.0 copy-done.1
  36.5 0.0 copy-done.2
  36.5 0.0 copy-done.3
  36.5 0.0 copy-done.4
  36.5 0.0 copy-done.5
  36.5 0.0 copy-done.6
  36.5 0.0 copy-done.9
  36.5 0.0 copy-done.7
  36.6 0.0 copy-done.8
  36.6 6.7 %shard_map.122 = (bf16[64,256]{1,0:T(8,128)(2,1)S(1)}, bf16[64,256]{1,0:T(8,128)(2,1)S(1)}, bf16[64,256]{1,0:T(8,128)(2,1)S(1)}, bf16[64,256]{1,0:T(8,128)(2,1)S(1)}, bf16[16,8,128]{2,1,0:T(8,128)(2,1)S(1)}) custom-call(bf16[128,256]{1,0:T(8,128)(2,1)S(1)} %bitcast.7, s32[1,128]{1,0:T(1,128)S(1)} %bitcast.15, s32[3,1,128]{2,1,0:T(1,128)S(1)} %bitcast.12, ...), custom_call_target="tpu_custom_call" | custom-call | tf_op jit(solution)/shard_map/pallas_call | solution.py:431
  43.2 18.8 %all_to_all.10.parts = bf16[16,8,128]{2,1,0:T(8,128)(2,1)S(1)} all-to-all(bf16[16,8,128]{2,1,0:T(8,128)(2,1)S(1)} %get-tuple-element.22), channel_id=1, replica_groups=mesh['zh'=2,'y'=4,'c'=2,'zl'=8,'x'=4] {'zh','zl'}, dimensions={0} | all-to-all | bytes 65536 | tf_op jit(solution)/shard_map/all_to_all | solution.py:482
  62.1 0.6 shard_map.124
  62.7 11.3 %all-to-all-start.1 = ((bf16[32,8,128]{2,1,0:T(8,128)(2,1)}), bf16[32,8,128]{2,1,0:T(8,128)(2,1)S(1)}, u32[]{:S(2)}, u32[]{:S(2)}) async-start(bf16[32,8,128]{2,1,0:T(8,128)(2,1)} %shard_map.124), calls=%async_computation.1 | async-start | bytes 131072 | tf_op jit(solution)/shard_map/all_to_all | solution.py:484
  74.0 4.4 %collective-permute-start.3 = (bf16[64,256]{1,0:T(8,128)(2,1)S(1)}, bf16[64,256]{1,0:T(8,128)(2,1)S(1)}, u32[]{:S(2)}, u32[]{:S(2)}) collective-permute-start(bf16[64,256]{1,0:T(8,128)(2,1)S(1)} %get-tuple-element.16), channel_id=1, source_target_pairs={{0,33},{1,34},{2,35},{3,36},{4,37},{5,38},{6,39},{7,40},{8,41},{9,... | collective-permute-start | bytes 98312 | tf_op jit(solution)/shard_map/ppermute | solution.py:459
  78.5 2.2 %collective-permute-start.4 = (bf16[64,256]{1,0:T(8,128)(2,1)S(1)}, bf16[64,256]{1,0:T(8,128)(2,1)S(1)}, u32[]{:S(2)}, u32[]{:S(2)}) collective-permute-start(bf16[64,256]{1,0:T(8,128)(2,1)S(1)} %get-tuple-element.17), channel_id=1, source_target_pairs={{0,32},{1,33},{2,34},{3,35},{4,36},{5,37},{6,38},{7,39},{8,40},{9,... | collective-permute-start | bytes 98312 | tf_op jit(solution)/shard_map/ppermute | solution.py:459
  80.7 3.1 %collective-permute-start.5 = (bf16[64,256]{1,0:T(8,128)(2,1)S(1)}, bf16[64,256]{1,0:T(8,128)(2,1)S(1)}, u32[]{:S(2)}, u32[]{:S(2)}) collective-permute-start(bf16[64,256]{1,0:T(8,128)(2,1)S(1)} %get-tuple-element.18), channel_id=1, source_target_pairs={{0,1},{1,2},{2,3},{3,4},{4,5},{5,6},{6,7},{7,8},{8,9},{9,10},{10,1... | collective-permute-start | bytes 98312 | tf_op jit(solution)/shard_map/ppermute | solution.py:459
  83.8 4.2 %collective-permute-done.3.home_xy = bf16[64,256]{1,0:T(8,128)(2,1)S(1)} collective-permute-done((bf16[64,256]{1,0:T(8,128)(2,1)S(1)}, bf16[64,256]{1,0:T(8,128)(2,1)S(1)}, u32[]{:S(2)}, u32[]{:S(2)}) %collective-permute-start.3) | collective-permute-done | bytes 32800 | tf_op jit(solution)/shard_map/ppermute | solution.py:459
  88.0 0.0 collective-permute-done.4.home_x
  88.0 6.1 %collective-permute-done.5.home_y = bf16[64,256]{1,0:T(8,128)(2,1)S(1)} collective-permute-done((bf16[64,256]{1,0:T(8,128)(2,1)S(1)}, bf16[64,256]{1,0:T(8,128)(2,1)S(1)}, u32[]{:S(2)}, u32[]{:S(2)}) %collective-permute-start.5) | collective-permute-done | bytes 32800 | tf_op jit(solution)/shard_map/ppermute | solution.py:459
  94.1 3.9 %shard_map.123 = (bf16[128,256]{1,0:T(8,128)(2,1)}, bf16[128,256]{1,0:T(8,128)(2,1)}) custom-call(bf16[64,256]{1,0:T(8,128)(2,1)S(1)} %collective-permute-done.3.home_xy, bf16[64,256]{1,0:T(8,128)(2,1)S(1)} %collective-permute-done.4.home_x, bf16[64,256]{1,0:T(8,128)(2,1)S(1)} %collective-permute-done.5.home_y, bf16[64,256]{1,0:T(8,128)(2,1)S(1)} %get-tuple-element.19.own, ...), custom_call_target="tpu_custom_call" | custom-call | tf_op jit(solution)/shard_map/pallas_call | solution.py:431
  98.0 0.0 all-to-all-done.1.parts
  98.0 0.7 shard_map.125
Async XLA Ops:
  0.6 35.9 %copy-start = (bf16[2,256,1024]{2,1,0:T(8,128)(2,1)S(1)}, bf16[2,256,1024]{2,1,0:T(8,128)(2,1)}, u32[]{:S(2)}) copy-start(bf16[2,256,1024]{2,1,0:T(8,128)(2,1)} %w_up.3) | copy-start | bytes 3145732
  0.6 35.9 %copy-start.1 = (bf16[2,1024,256]{2,1,0:T(8,128)(2,1)S(1)}, bf16[2,1024,256]{2,1,0:T(8,128)(2,1)}, u32[]{:S(2)}) copy-start(bf16[2,1024,256]{2,1,0:T(8,128)(2,1)} %w_down.3) | copy-start | bytes 3145732
  0.7 35.9 %copy-start.2 = (bf16[2,256,768]{2,1,0:T(8,128)(2,1)S(1)}, bf16[2,256,768]{2,1,0:T(8,128)(2,1)}, u32[]{:S(2)}) copy-start(bf16[2,256,768]{2,1,0:T(8,128)(2,1)} %w_qkv.3) | copy-start | bytes 2359300
  0.7 35.8 %copy-start.3 = (bf16[2,256,256]{2,1,0:T(8,128)(2,1)S(1)}, bf16[2,256,256]{2,1,0:T(8,128)(2,1)}, u32[]{:S(2)}) copy-start(bf16[2,256,256]{2,1,0:T(8,128)(2,1)} %w_out.3) | copy-start | bytes 786436
  0.7 35.8 %copy-start.4 = (bf16[1,1,128,256]{3,2,1,0:T(8,128)(2,1)S(1)}, bf16[1,1,128,256]{3,2,1,0:T(8,128)(2,1)}, u32[]{:S(2)}) copy-start(bf16[1,1,128,256]{3,2,1,0:T(8,128)(2,1)} %param.10) | copy-start | bytes 196612
  0.7 35.8 %copy-start.5 = (f32[2,3,8,15]{3,2,1,0:T(8,128)S(1)}, f32[2,3,8,15]{3,2,1,0:T(8,128)}, u32[]{:S(2)}) copy-start(f32[2,3,8,15]{3,2,1,0:T(8,128)} %tables.3) | copy-start | bytes 8644
  0.7 35.8 %copy-start.6 = (bf16[1,1,128,256]{3,2,1,0:T(8,128)(2,1)S(1)}, bf16[1,1,128,256]{3,2,1,0:T(8,128)(2,1)}, u32[]{:S(2)}) copy-start(bf16[1,1,128,256]{3,2,1,0:T(8,128)(2,1)} %param.19) | copy-start | bytes 196612
  0.7 35.8 %copy-start.9 = (s32[1,1,128]{2,1,0:T(1,128)S(1)}, s32[1,1,128]{2,1,0:T(1,128)}, u32[]{:S(2)}) copy-start(s32[1,1,128]{2,1,0:T(1,128)} %param.11) | copy-start | bytes 1540
  1.9 34.7 %copy-start.7 = (f32[2,2,256]{2,1,0:T(2,128)S(1)}, f32[2,2,256]{2,1,0:T(2,128)}, u32[]{:S(2)}) copy-start(f32[2,2,256]{2,1,0:T(2,128)} %gains.3) | copy-start | bytes 12292
  1.9 34.7 %copy-start.8 = (s32[1,1,3,128]{3,1,2,0:T(1,128)S(1)}, s32[1,1,3,128]{3,1,2,0:T(1,128)}, u32[]{:S(2)}) copy-start(s32[1,1,3,128]{3,1,2,0:T(1,128)} %param.12) | copy-start | bytes 4612
  1.9 29.0 %collective-permute-start = (bf16[168,256]{1,0:T(8,128)(2,1)S(1)}, bf16[168,256]{1,0:T(8,128)(2,1)S(1)}, u32[]{:S(2)}, u32[]{:S(2)}) collective-permute-start(bf16[168,256]{1,0:T(8,128)(2,1)S(1)} %get-tuple-element.13), channel_id=1, source_target_pairs={{0,31},{1,0},{2,1},{3,2},{4,3},{5,4},{6,5},{7,6},{8,7},{9,8},{10,9... | collective-permute-start | bytes 258056 | tf_op jit(solution)/shard_map/ppermute | solution.py:459
  17.8 13.2 %collective-permute-start.1 = (bf16[168,256]{1,0:T(8,128)(2,1)S(1)}, bf16[168,256]{1,0:T(8,128)(2,1)S(1)}, u32[]{:S(2)}, u32[]{:S(2)}) collective-permute-start(bf16[168,256]{1,0:T(8,128)(2,1)S(1)} %get-tuple-element.14), channel_id=1, source_target_pairs={{0,480},{1,481},{2,482},{3,483},{4,484},{5,485},{6,486},{7,487},{8... | collective-permute-start | bytes 258056 | tf_op jit(solution)/shard_map/ppermute | solution.py:459
  20.7 15.8 %collective-permute-start.2 = (bf16[168,256]{1,0:T(8,128)(2,1)S(1)}, bf16[168,256]{1,0:T(8,128)(2,1)S(1)}, u32[]{:S(2)}, u32[]{:S(2)}) collective-permute-start(bf16[168,256]{1,0:T(8,128)(2,1)S(1)} %get-tuple-element.15), channel_id=1, source_target_pairs={{0,511},{1,480},{2,481},{3,482},{4,483},{5,484},{6,485},{7,486},{8... | collective-permute-start | bytes 258056 | tf_op jit(solution)/shard_map/ppermute | solution.py:459
  62.7 35.3 %all-to-all-start.1 = ((bf16[32,8,128]{2,1,0:T(8,128)(2,1)}), bf16[32,8,128]{2,1,0:T(8,128)(2,1)S(1)}, u32[]{:S(2)}, u32[]{:S(2)}) async-start(bf16[32,8,128]{2,1,0:T(8,128)(2,1)} %shard_map.124), calls=%async_computation.1 | async-start | bytes 131072 | tf_op jit(solution)/shard_map/all_to_all | solution.py:484
  74.0 13.9 %collective-permute-start.3 = (bf16[64,256]{1,0:T(8,128)(2,1)S(1)}, bf16[64,256]{1,0:T(8,128)(2,1)S(1)}, u32[]{:S(2)}, u32[]{:S(2)}) collective-permute-start(bf16[64,256]{1,0:T(8,128)(2,1)S(1)} %get-tuple-element.16), channel_id=1, source_target_pairs={{0,33},{1,34},{2,35},{3,36},{4,37},{5,38},{6,39},{7,40},{8,41},{9,... | collective-permute-start | bytes 98312 | tf_op jit(solution)/shard_map/ppermute | solution.py:459
  78.5 9.5 %collective-permute-start.4 = (bf16[64,256]{1,0:T(8,128)(2,1)S(1)}, bf16[64,256]{1,0:T(8,128)(2,1)S(1)}, u32[]{:S(2)}, u32[]{:S(2)}) collective-permute-start(bf16[64,256]{1,0:T(8,128)(2,1)S(1)} %get-tuple-element.17), channel_id=1, source_target_pairs={{0,32},{1,33},{2,34},{3,35},{4,36},{5,37},{6,38},{7,39},{8,40},{9,... | collective-permute-start | bytes 98312 | tf_op jit(solution)/shard_map/ppermute | solution.py:459
  80.7 13.4 %collective-permute-start.5 = (bf16[64,256]{1,0:T(8,128)(2,1)S(1)}, bf16[64,256]{1,0:T(8,128)(2,1)S(1)}, u32[]{:S(2)}, u32[]{:S(2)}) collective-permute-start(bf16[64,256]{1,0:T(8,128)(2,1)S(1)} %get-tuple-element.18), channel_id=1, source_target_pairs={{0,1},{1,2},{2,3},{3,4},{4,5},{5,6},{6,7},{7,8},{8,9},{9,10},{10,1... | collective-permute-start | bytes 98312 | tf_op jit(solution)/shard_map/ppermute | solution.py:459

commit v6 on v5

--- a/solution.py
+++ b/solution.py
@@ -122,9 +122,12 @@
 
 
 def attend_back(soft, mixed, cot_mixed, v):
-    product = (-mixed * cot_mixed.astype(F32)).astype(BF)
-    left = jnp.concatenate([spread(cot_mixed), spread(product)], axis=1)
-    return (soft * mm_t(left, jnp.concatenate([v, jnp.ones_like(v)], axis=1))).astype(BF)
+    product = -mixed * cot_mixed.astype(F32)
+    high = product.astype(BF)
+    low = (product - high.astype(F32)).astype(BF)
+    ones = jnp.ones_like(v)
+    left = jnp.concatenate([spread(cot_mixed), spread(high), spread(low)], axis=1)
+    return (soft * mm_t(left, jnp.concatenate([v, ones, ones], axis=1))).astype(BF)
 
 
 def gelu_and_slope(v):

time: 99.1 us -> 99.3 us (level)
  no operation moved by 1% of the time
where the time goes in v6:
time: 99.3 us; the launch traced here: 98.9 us
  starting transfers between devices  50.1 us (50%)
  blocking collectives  18.8 us (19%)
  waiting for transfers between devices  15.8 us (16%)
  Pallas kernels  13.3 us (13%)
    ppermute x6, starting transfers between devices, move(): return lax.ppermute(value, gx + gy, pairs)  38.7 us
    all_to_all x1, blocking collectives, on_device(): tables = lax.all_to_all(tables, phases[0], 0, 0)  18.8 us
    ppermute x6, waiting for transfers between devices, move(): return lax.ppermute(value, gx + gy, pairs)  15.8 us
    pallas_call x5, Pallas kernels, call(): pl.pallas_call(kernel, out_shape=[jax.ShapeDtypeStruct(s, d) for s, d in...  13.3 us
    all_to_all x1, starting transfers between devices, on_device(): tables = lax.all_to_all(tables, phases[1], 0, 0)  11.3 us
  transfers between devices with their start and end apart: 7, of which 3 were waited for; matrix products, arithmetic and copies ran while one was open for 0% of the time, Pallas kernels for 4%

profile of v6, /device:TPU:1, one launch (start us, length us, event | category | flops | bytes accessed | tf_op | source)
XLA Modules:
  0.0 98.9 jit_solution(13116246695766100333)
XLA Ops:
  0.6 0.0 copy-start
  0.6 0.0 copy-start.1
  0.7 0.0 copy-start.2
  0.7 0.0 copy-start.3
  0.7 0.0 copy-start.4
  0.7 0.0 copy-start.5
  0.7 0.0 copy-start.6
  0.7 0.0 copy-start.9
  0.7 1.1 %shard_map.121 = (bf16[168,256]{1,0:T(8,128)(2,1)S(1)}, bf16[168,256]{1,0:T(8,128)(2,1)S(1)}, bf16[168,256]{1,0:T(8,128)(2,1)S(1)}) custom-call(bf16[128,256]{1,0:T(8,128)(2,1)} %bitcast.6, s32[1,128]{1,0:T(1,128)} %bitcast.14, s32[3,1,128]{2,1,0:T(1,128)} %bitcast.11, bf16[128,256]{1,0:T(8,128)(2,1)} %bitcast.9), custom_call_target="tpu_custom_call" | custom-call | flops 10000000000 | bytes 8388608 | tf_op jit(solution)/shard_map/pallas_call | solution.py:434
  1.9 0.0 copy-start.7
  1.9 0.0 copy-start.8
  1.9 15.9 %collective-permute-start = (bf16[168,256]{1,0:T(8,128)(2,1)S(1)}, bf16[168,256]{1,0:T(8,128)(2,1)S(1)}, u32[]{:S(2)}, u32[]{:S(2)}) collective-permute-start(bf16[168,256]{1,0:T(8,128)(2,1)S(1)} %get-tuple-element.13), channel_id=1, source_target_pairs={{0,31},{1,0},{2,1},{3,2},{4,3},{5,4},{6,5},{7,6},{8,7},{9,8},{10,9... | collective-permute-start | bytes 258056 | tf_op jit(solution)/shard_map/ppermute | solution.py:462
  17.8 2.9 %collective-permute-start.1 = (bf16[168,256]{1,0:T(8,128)(2,1)S(1)}, bf16[168,256]{1,0:T(8,128)(2,1)S(1)}, u32[]{:S(2)}, u32[]{:S(2)}) collective-permute-start(bf16[168,256]{1,0:T(8,128)(2,1)S(1)} %get-tuple-element.14), channel_id=1, source_target_pairs={{0,480},{1,481},{2,482},{3,483},{4,484},{5,485},{6,486},{7,487},{8... | collective-permute-start | bytes 258056 | tf_op jit(solution)/shard_map/ppermute | solution.py:462
  20.7 10.3 %collective-permute-start.2 = (bf16[168,256]{1,0:T(8,128)(2,1)S(1)}, bf16[168,256]{1,0:T(8,128)(2,1)S(1)}, u32[]{:S(2)}, u32[]{:S(2)}) collective-permute-start(bf16[168,256]{1,0:T(8,128)(2,1)S(1)} %get-tuple-element.15), channel_id=1, source_target_pairs={{0,511},{1,480},{2,481},{3,482},{4,483},{5,484},{6,485},{7,486},{8... | collective-permute-start | bytes 258056 | tf_op jit(solution)/shard_map/ppermute | solution.py:462
  30.9 0.0 collective-permute-done.from_y
  30.9 0.0 collective-permute-done.1.from_x
  30.9 5.5 %collective-permute-done.2.from_xy = bf16[168,256]{1,0:T(8,128)(2,1)S(1)} collective-permute-done((bf16[168,256]{1,0:T(8,128)(2,1)S(1)}, bf16[168,256]{1,0:T(8,128)(2,1)S(1)}, u32[]{:S(2)}, u32[]{:S(2)}) %collective-permute-start.2) | collective-permute-done | bytes 86048 | tf_op jit(solution)/shard_map/ppermute | solution.py:462
  36.5 0.0 copy-done
  36.5 0.0 copy-done.1
  36.5 0.0 copy-done.2
  36.5 0.0 copy-done.3
  36.5 0.0 copy-done.4
  36.5 0.0 copy-done.5
  36.5 0.0 copy-done.6
  36.5 0.0 copy-done.9
  36.5 0.0 copy-done.7
  36.6 0.0 copy-done.8
  36.6 6.9 %shard_map.122 = (bf16[64,256]{1,0:T(8,128)(2,1)S(1)}, bf16[64,256]{1,0:T(8,128)(2,1)S(1)}, bf16[64,256]{1,0:T(8,128)(2,1)S(1)}, bf16[64,256]{1,0:T(8,128)(2,1)S(1)}, bf16[16,8,128]{2,1,0:T(8,128)(2,1)S(1)}) custom-call(bf16[128,256]{1,0:T(8,128)(2,1)S(1)} %bitcast.7, s32[1,128]{1,0:T(1,128)S(1)} %bitcast.15, s32[3,1,128]{2,1,0:T(1,128)S(1)} %bitcast.12, ...), custom_call_target="tpu_custom_call" | custom-call | tf_op jit(solution)/shard_map/pallas_call | solution.py:434
  43.4 18.8 %all_to_all.10.parts = bf16[16,8,128]{2,1,0:T(8,128)(2,1)S(1)} all-to-all(bf16[16,8,128]{2,1,0:T(8,128)(2,1)S(1)} %get-tuple-element.22), channel_id=1, replica_groups=mesh['zh'=2,'y'=4,'c'=2,'zl'=8,'x'=4] {'zh','zl'}, dimensions={0} | all-to-all | bytes 65536 | tf_op jit(solution)/shard_map/all_to_all | solution.py:485
  62.2 0.6 shard_map.124
  62.9 11.3 %all-to-all-start.1 = ((bf16[32,8,128]{2,1,0:T(8,128)(2,1)}), bf16[32,8,128]{2,1,0:T(8,128)(2,1)S(1)}, u32[]{:S(2)}, u32[]{:S(2)}) async-start(bf16[32,8,128]{2,1,0:T(8,128)(2,1)} %shard_map.124), calls=%async_computation.1 | async-start | bytes 131072 | tf_op jit(solution)/shard_map/all_to_all | solution.py:487
  74.2 4.4 %collective-permute-start.3 = (bf16[64,256]{1,0:T(8,128)(2,1)S(1)}, bf16[64,256]{1,0:T(8,128)(2,1)S(1)}, u32[]{:S(2)}, u32[]{:S(2)}) collective-permute-start(bf16[64,256]{1,0:T(8,128)(2,1)S(1)} %get-tuple-element.16), channel_id=1, source_target_pairs={{0,33},{1,34},{2,35},{3,36},{4,37},{5,38},{6,39},{7,40},{8,41},{9,... | collective-permute-start | bytes 98312 | tf_op jit(solution)/shard_map/ppermute | solution.py:462
  78.7 2.2 %collective-permute-start.4 = (bf16[64,256]{1,0:T(8,128)(2,1)S(1)}, bf16[64,256]{1,0:T(8,128)(2,1)S(1)}, u32[]{:S(2)}, u32[]{:S(2)}) collective-permute-start(bf16[64,256]{1,0:T(8,128)(2,1)S(1)} %get-tuple-element.17), channel_id=1, source_target_pairs={{0,32},{1,33},{2,34},{3,35},{4,36},{5,37},{6,38},{7,39},{8,40},{9,... | collective-permute-start | bytes 98312 | tf_op jit(solution)/shard_map/ppermute | solution.py:462
  80.9 3.1 %collective-permute-start.5 = (bf16[64,256]{1,0:T(8,128)(2,1)S(1)}, bf16[64,256]{1,0:T(8,128)(2,1)S(1)}, u32[]{:S(2)}, u32[]{:S(2)}) collective-permute-start(bf16[64,256]{1,0:T(8,128)(2,1)S(1)} %get-tuple-element.18), channel_id=1, source_target_pairs={{0,1},{1,2},{2,3},{3,4},{4,5},{5,6},{6,7},{7,8},{8,9},{9,10},{10,1... | collective-permute-start | bytes 98312 | tf_op jit(solution)/shard_map/ppermute | solution.py:462
  84.0 4.2 %collective-permute-done.3.home_xy = bf16[64,256]{1,0:T(8,128)(2,1)S(1)} collective-permute-done((bf16[64,256]{1,0:T(8,128)(2,1)S(1)}, bf16[64,256]{1,0:T(8,128)(2,1)S(1)}, u32[]{:S(2)}, u32[]{:S(2)}) %collective-permute-start.3) | collective-permute-done | bytes 32800 | tf_op jit(solution)/shard_map/ppermute | solution.py:462
  88.2 0.0 collective-permute-done.4.home_x
  88.2 6.1 %collective-permute-done.5.home_y = bf16[64,256]{1,0:T(8,128)(2,1)S(1)} collective-permute-done((bf16[64,256]{1,0:T(8,128)(2,1)S(1)}, bf16[64,256]{1,0:T(8,128)(2,1)S(1)}, u32[]{:S(2)}, u32[]{:S(2)}) %collective-permute-start.5) | collective-permute-done | bytes 32800 | tf_op jit(solution)/shard_map/ppermute | solution.py:462
  94.2 4.0 %shard_map.123 = (bf16[128,256]{1,0:T(8,128)(2,1)}, bf16[128,256]{1,0:T(8,128)(2,1)}) custom-call(bf16[64,256]{1,0:T(8,128)(2,1)S(1)} %collective-permute-done.3.home_xy, bf16[64,256]{1,0:T(8,128)(2,1)S(1)} %collective-permute-done.4.home_x, bf16[64,256]{1,0:T(8,128)(2,1)S(1)} %collective-permute-done.5.home_y, bf16[64,256]{1,0:T(8,128)(2,1)S(1)} %get-tuple-element.19.own, ...), custom_call_target="tpu_custom_call" | custom-call | tf_op jit(solution)/shard_map/pallas_call | solution.py:434
  98.2 0.0 all-to-all-done.1.parts
  98.2 0.7 shard_map.125
Async XLA Ops:
  0.6 35.9 %copy-start = (bf16[2,256,1024]{2,1,0:T(8,128)(2,1)S(1)}, bf16[2,256,1024]{2,1,0:T(8,128)(2,1)}, u32[]{:S(2)}) copy-start(bf16[2,256,1024]{2,1,0:T(8,128)(2,1)} %w_up.3) | copy-start | bytes 3145732
  0.6 35.9 %copy-start.1 = (bf16[2,1024,256]{2,1,0:T(8,128)(2,1)S(1)}, bf16[2,1024,256]{2,1,0:T(8,128)(2,1)}, u32[]{:S(2)}) copy-start(bf16[2,1024,256]{2,1,0:T(8,128)(2,1)} %w_down.3) | copy-start | bytes 3145732
  0.7 35.9 %copy-start.2 = (bf16[2,256,768]{2,1,0:T(8,128)(2,1)S(1)}, bf16[2,256,768]{2,1,0:T(8,128)(2,1)}, u32[]{:S(2)}) copy-start(bf16[2,256,768]{2,1,0:T(8,128)(2,1)} %w_qkv.3) | copy-start | bytes 2359300
  0.7 35.8 %copy-start.3 = (bf16[2,256,256]{2,1,0:T(8,128)(2,1)S(1)}, bf16[2,256,256]{2,1,0:T(8,128)(2,1)}, u32[]{:S(2)}) copy-start(bf16[2,256,256]{2,1,0:T(8,128)(2,1)} %w_out.3) | copy-start | bytes 786436
  0.7 35.8 %copy-start.4 = (bf16[1,1,128,256]{3,2,1,0:T(8,128)(2,1)S(1)}, bf16[1,1,128,256]{3,2,1,0:T(8,128)(2,1)}, u32[]{:S(2)}) copy-start(bf16[1,1,128,256]{3,2,1,0:T(8,128)(2,1)} %param.10) | copy-start | bytes 196612
  0.7 35.8 %copy-start.5 = (f32[2,3,8,15]{3,2,1,0:T(8,128)S(1)}, f32[2,3,8,15]{3,2,1,0:T(8,128)}, u32[]{:S(2)}) copy-start(f32[2,3,8,15]{3,2,1,0:T(8,128)} %tables.3) | copy-start | bytes 8644
  0.7 35.8 %copy-start.6 = (bf16[1,1,128,256]{3,2,1,0:T(8,128)(2,1)S(1)}, bf16[1,1,128,256]{3,2,1,0:T(8,128)(2,1)}, u32[]{:S(2)}) copy-start(bf16[1,1,128,256]{3,2,1,0:T(8,128)(2,1)} %param.19) | copy-start | bytes 196612
  0.7 35.8 %copy-start.9 = (s32[1,1,128]{2,1,0:T(1,128)S(1)}, s32[1,1,128]{2,1,0:T(1,128)}, u32[]{:S(2)}) copy-start(s32[1,1,128]{2,1,0:T(1,128)} %param.11) | copy-start | bytes 1540
  1.9 34.7 %copy-start.7 = (f32[2,2,256]{2,1,0:T(2,128)S(1)}, f32[2,2,256]{2,1,0:T(2,128)}, u32[]{:S(2)}) copy-start(f32[2,2,256]{2,1,0:T(2,128)} %gains.3) | copy-start | bytes 12292
  1.9 34.7 %copy-start.8 = (s32[1,1,3,128]{3,1,2,0:T(1,128)S(1)}, s32[1,1,3,128]{3,1,2,0:T(1,128)}, u32[]{:S(2)}) copy-start(s32[1,1,3,128]{3,1,2,0:T(1,128)} %param.12) | copy-start | bytes 4612
  1.9 29.0 %collective-permute-start = (bf16[168,256]{1,0:T(8,128)(2,1)S(1)}, bf16[168,256]{1,0:T(8,128)(2,1)S(1)}, u32[]{:S(2)}, u32[]{:S(2)}) collective-permute-start(bf16[168,256]{1,0:T(8,128)(2,1)S(1)} %get-tuple-element.13), channel_id=1, source_target_pairs={{0,31},{1,0},{2,1},{3,2},{4,3},{5,4},{6,5},{7,6},{8,7},{9,8},{10,9... | collective-permute-start | bytes 258056 | tf_op jit(solution)/shard_map/ppermute | solution.py:462
  17.8 13.2 %collective-permute-start.1 = (bf16[168,256]{1,0:T(8,128)(2,1)S(1)}, bf16[168,256]{1,0:T(8,128)(2,1)S(1)}, u32[]{:S(2)}, u32[]{:S(2)}) collective-permute-start(bf16[168,256]{1,0:T(8,128)(2,1)S(1)} %get-tuple-element.14), channel_id=1, source_target_pairs={{0,480},{1,481},{2,482},{3,483},{4,484},{5,485},{6,486},{7,487},{8... | collective-permute-start | bytes 258056 | tf_op jit(solution)/shard_map/ppermute | solution.py:462
  20.7 15.8 %collective-permute-start.2 = (bf16[168,256]{1,0:T(8,128)(2,1)S(1)}, bf16[168,256]{1,0:T(8,128)(2,1)S(1)}, u32[]{:S(2)}, u32[]{:S(2)}) collective-permute-start(bf16[168,256]{1,0:T(8,128)(2,1)S(1)} %get-tuple-element.15), channel_id=1, source_target_pairs={{0,511},{1,480},{2,481},{3,482},{4,483},{5,484},{6,485},{7,486},{8... | collective-permute-start | bytes 258056 | tf_op jit(solution)/shard_map/ppermute | solution.py:462
  62.9 35.3 %all-to-all-start.1 = ((bf16[32,8,128]{2,1,0:T(8,128)(2,1)}), bf16[32,8,128]{2,1,0:T(8,128)(2,1)S(1)}, u32[]{:S(2)}, u32[]{:S(2)}) async-start(bf16[32,8,128]{2,1,0:T(8,128)(2,1)} %shard_map.124), calls=%async_computation.1 | async-start | bytes 131072 | tf_op jit(solution)/shard_map/all_to_all | solution.py:487
  74.2 13.9 %collective-permute-start.3 = (bf16[64,256]{1,0:T(8,128)(2,1)S(1)}, bf16[64,256]{1,0:T(8,128)(2,1)S(1)}, u32[]{:S(2)}, u32[]{:S(2)}) collective-permute-start(bf16[64,256]{1,0:T(8,128)(2,1)S(1)} %get-tuple-element.16), channel_id=1, source_target_pairs={{0,33},{1,34},{2,35},{3,36},{4,37},{5,38},{6,39},{7,40},{8,41},{9,... | collective-permute-start | bytes 98312 | tf_op jit(solution)/shard_map/ppermute | solution.py:462
  78.7 9.5 %collective-permute-start.4 = (bf16[64,256]{1,0:T(8,128)(2,1)S(1)}, bf16[64,256]{1,0:T(8,128)(2,1)S(1)}, u32[]{:S(2)}, u32[]{:S(2)}) collective-permute-start(bf16[64,256]{1,0:T(8,128)(2,1)S(1)} %get-tuple-element.17), channel_id=1, source_target_pairs={{0,32},{1,33},{2,34},{3,35},{4,36},{5,37},{6,38},{7,39},{8,40},{9,... | collective-permute-start | bytes 98312 | tf_op jit(solution)/shard_map/ppermute | solution.py:462
  80.9 13.4 %collective-permute-start.5 = (bf16[64,256]{1,0:T(8,128)(2,1)S(1)}, bf16[64,256]{1,0:T(8,128)(2,1)S(1)}, u32[]{:S(2)}, u32[]{:S(2)}) collective-permute-start(bf16[64,256]{1,0:T(8,128)(2,1)S(1)} %get-tuple-element.18), channel_id=1, source_target_pairs={{0,1},{1,2},{2,3},{3,4},{4,5},{5,6},{6,7},{7,8},{8,9},{9,10},{10,1... | collective-permute-start | bytes 98312 | tf_op jit(solution)/shard_map/ppermute | solution.py:462
